TPU v7x, 8 devices: a whole 2x2x1 slice. The times are simulated.
8 devices in a mesh: etp: 2 (over z, y), ep: 4 (over x, core).
Axes of the slice: x: 2, y: 2, z: 1, core: 2. Of those that a mesh axis runs over, the one named last changes fastest.
Arguments:
- hidden: bfloat16 [16384, 512], P(('ep', 'etp'))
- w_router: float32 [512, 32], replicated
- expert_ids: int32 [16384, 2], P(('ep', 'etp'))
- d_out: bfloat16 [16384, 512], P(('ep', 'etp'))
- w_gate: bfloat16 [32, 512, 768], P('ep', None, 'etp')
- w_up: bfloat16 [32, 512, 768], P('ep', None, 'etp')
- w_down: bfloat16 [32, 768, 512], P('ep', 'etp')
Outputs:
- output 1: bfloat16 [16384, 512], P(('ep', 'etp'))
- output 2: bfloat16 [16384, 512], P(('ep', 'etp'))
- output 3: float32 [512, 32], replicated
- output 4: float32 [], replicated
- output 5: float32 [32, 512, 768], P('ep', None, 'etp')
- output 6: float32 [32, 512, 768], P('ep', None, 'etp')
- output 7: float32 [32, 768, 512], P('ep', 'etp')
All inputs are finite; a program needn't handle non-finite values.
Results may differ from a plain program's by a relative error of at most 0.00900198.
Values are sent between devices in bfloat16 or wider.
A program may use at most 1 GiB of HBM per device.

v0:
```python
import functools
import jax
import jax.numpy as jnp
from jax import lax
from jax.experimental import pallas as pl
from jax.experimental.pallas import tpu as pltpu
from jax.sharding import PartitionSpec as P

AUX_COEF = 0.01
OUT_SCALE = 2.0
CHUNKS = ((0, 2), (2, 4), (4, 6), (6, 7), (7, 8))

f32, bf16 = jnp.float32, jnp.bfloat16
TILE = 256
WIN = 48


def nn(a, b):
    return jnp.dot(a, b, preferred_element_type=f32)


def nt(a, b):
    return lax.dot_general(a, b, (((1,), (1,)), ((), ())), preferred_element_type=f32)


def tn(a, b):
    return lax.dot_general(a, b, (((0,), (0,)), ((), ())), preferred_element_type=f32)


def split3(v):
    hi = v.astype(bf16)
    rest = v - hi.astype(f32)
    mid = rest.astype(bf16)
    return hi, mid, (rest - mid.astype(f32)).astype(bf16)


def iota(shape, dim):
    return lax.broadcasted_iota(jnp.int32, shape, dim)


def params(**kw):
    return pltpu.CompilerParams(vmem_limit_bytes=60 * 2**20, **kw)


def cost(flops):
    return pl.CostEstimate(flops=int(flops), bytes_accessed=1 << 20, transcendentals=0)


def route_kernel(n_experts, h_ref, wr_ref, ids_ref, p_ref, code_ref, win_ref, stat_ref):
    step = pl.program_id(0)

    @pl.when(step == 0)
    def _():
        stat_ref[...] = jnp.zeros_like(stat_ref)
        win_ref[...] = jnp.zeros_like(win_ref)

    w_hi, w_mid, w_lo = split3(wr_ref[...])
    h = h_ref[...]
    z = (nn(h, w_lo) + nn(h, w_mid)) + nn(h, w_hi)
    z = jnp.exp(z - jnp.max(z, axis=1, keepdims=True))
    p = z / jnp.sum(z, axis=1, keepdims=True)
    p_ref[...] = p
    ids = ids_ref[...]
    lane = iota((TILE, n_experts), 1)
    e0, e1 = ids[:, 0:1], ids[:, 1:2]
    m0, m1 = lane == e0, lane == e1
    hist = jnp.where(m0 | m1, 1.0, 0.0).astype(f32)
    before = (iota((TILE, TILE), 1) < iota((TILE, TILE), 0)).astype(f32).astype(bf16)
    seen = stat_ref[0:1, 0:n_experts]
    after = seen + jnp.sum(hist, axis=0, keepdims=True)
    start = jnp.floor(seen * (1.0 / 16)) * 16
    n_win = jnp.max(jnp.floor((after - start + (WIN - 1)) * (1.0 / WIN) + 1e-3), axis=1, keepdims=True)
    rank = nn(before, hist.astype(bf16)) + seen
    pick = lambda m, v: jnp.sum(jnp.where(m, v, 0.0), axis=1, keepdims=True)
    p0, p1 = pick(m0, p), pick(m1, p)
    s = p0 + p1
    wide = iota((TILE, 128), 1)
    code = jnp.zeros((TILE, 128), f32)
    rel = rank - start
    for k, v in enumerate((e0.astype(f32), e1.astype(f32), pick(m0, rel), pick(m1, rel), p0 / s, p1 / s, s)):
        code = jnp.where(wide == k, v, code)
    code_ref[...] = code
    win_ref[pl.ds(step, 1), 0:n_experts] = start.astype(jnp.int32)
    win_ref[pl.ds(step, 1), n_experts:n_experts + 1] = n_win.astype(jnp.int32)
    stat_ref[0:1, 0:n_experts] = after
    stat_ref[1:2, 0:n_experts] = stat_ref[1:2, 0:n_experts] + jnp.sum(p, axis=0, keepdims=True)


def slot_kernel(capacity, slots, n_local, info_ref, ids_ref, wr_ref, slot_ref, other_ref, start_ref, wr3_ref, total_ref):
    @pl.when(pl.program_id(0) == 0)
    def _():
        total_ref[...] = jnp.zeros_like(total_ref)
        wr3_ref[...] = jnp.zeros_like(wr3_ref)
        width = wr_ref.shape[1]
        for k, piece in enumerate(split3(wr_ref[...])):
            wr3_ref[:, k * width:(k + 1) * width] = piece

    steps = ids_ref.shape[1] // 2
    expert = iota((n_local, TILE), 0) + info_ref[0]
    before = (iota((TILE, TILE), 0) < iota((TILE, TILE), 1)).astype(f32).astype(bf16)
    row = iota((TILE, TILE), 0).astype(f32)
    lane = iota((n_local, 128), 1)
    carry = jnp.zeros((n_local, 1), f32)
    starts = jnp.zeros((n_local, 128), f32)
    other = jnp.zeros((n_local, TILE), f32)
    for i in range(steps):
        e0, e1 = ids_ref[0, 2 * i:2 * i + 1, :], ids_ref[0, 2 * i + 1:2 * i + 2, :]
        m0, m1 = expert == e0, expert == e1
        hit = jnp.where(m0 | m1, 1.0, 0.0).astype(f32)
        rank = nn(hit.astype(bf16), before) + carry
        slot_ref[0, i * n_local:(i + 1) * n_local, :] = jnp.where(m0 | m1, rank, -1.0)
        starts = jnp.where(lane == i, carry, starts)
        for m, e in ((m0, e1), (m1, e0)):
            pos = jnp.sum(jnp.where(m, rank + 1.0, 0.0), axis=0, keepdims=True) - 1.0
            one = jnp.where(row == pos, 1.0, 0.0).astype(bf16)
            other = other + nt(jnp.where(m, e.astype(f32), 0.0).astype(bf16), one)
        carry = carry + jnp.sum(hit, axis=1, keepdims=True)
    other_ref[0] = other
    prefix = total_ref[:, 0:1]
    room = jnp.clip(capacity - prefix, 0.0, float(slots))
    starts = jnp.where(lane == steps, carry, jnp.where(lane == steps + 1, jnp.minimum(room, carry), starts))
    start_ref[0] = starts.astype(jnp.int32)
    total_ref[...] = total_ref[...] + carry


def gather_kernel(slots, n_local, n_experts, info_ref, start_ref, slot_ref, other_ref, wr3_ref, ha_ref, hb_ref, da_ref, db_ref,
                  x_ref, c_ref, m_ref, xs_ref, ds_ref):
    step = pl.program_id(0)
    steps = pl.num_programs(0) - n_local

    @pl.when(step < steps)
    def _():
        row = iota((WIN, TILE), 0)
        for b, (h_ref, d_ref) in enumerate(((ha_ref, da_ref), (hb_ref, db_ref))):
            j = info_ref[b]
            first = [(start_ref[j, e, step] // 16) * 16 for e in range(n_local)]
            span = functools.reduce(jnp.maximum, [start_ref[j, e, step + 1] - first[e] for e in range(n_local)])

            def window(w, carry):
                for e in range(n_local):
                    slot = slot_ref[j, pl.ds(step * n_local + e, 1), :]
                    hit = (row + (first[e] + w * WIN)).astype(f32) == slot
                    m_ref[e * WIN:(e + 1) * WIN, :] = jnp.where(hit, 1.0, 0.0).astype(bf16)
                m = m_ref[...]
                for src, dst in ((h_ref, xs_ref), (d_ref, ds_ref)):
                    r = nn(m, src[...]).astype(bf16)
                    for e in range(n_local):
                        at = pl.multiple_of(jnp.minimum(first[e] + w * WIN, slots + 16), 16)
                        old = dst[b, e, pl.ds(at, 16), :]
                        keep = iota((16, 1), 0) + at < start_ref[j, e, step]
                        head = r[e * WIN:e * WIN + 16].astype(f32)
                        dst[b, e, pl.ds(at, 16), :] = jnp.where(keep, old.astype(f32), head).astype(bf16)
                        dst[b, e, pl.ds(pl.multiple_of(at + 16, 16), WIN - 16), :] = r[e * WIN + 16:(e + 1) * WIN]
                return carry

            lax.fori_loop(0, (span + WIN - 1) // WIN, window, 0)

    @pl.when(step >= steps)
    def _():
        e = step - steps
        lane = iota((slots, 128), 1)
        for b in range(2):
            j = info_ref[b]
            kept = iota((slots, 1), 0) < start_ref[j, e, steps + 1]
            x = jnp.where(kept, xs_ref[b, e, 0:slots, :].astype(f32), 0.0)
            d = jnp.where(kept, ds_ref[b, e, 0:slots, :].astype(f32), 0.0)
            x = x.astype(bf16)
            x_ref[0, b * slots:(b + 1) * slots, :] = x
            z = nn(x, wr3_ref[...])
            other = other_ref[j].T[0:slots, :]
            other = jnp.sum(jnp.where(iota((slots, n_local), 1) == e, other, 0.0), axis=1, keepdims=True)
            name = lane % n_experts
            here = jnp.sum(jnp.where(name == info_ref[2] + e, z, 0.0), axis=1, keepdims=True)
            there = jnp.sum(jnp.where(name == other.astype(jnp.int32), z, 0.0), axis=1, keepdims=True)
            g = 1.0 / (1.0 + jnp.exp(there - here))
            c_ref[0, b * slots:(b + 1) * slots, :] = (g * (OUT_SCALE * d)).astype(bf16)


def act(ab, du):
    ff = du.shape[1]
    a, b = ab[:, :ff], ab[:, ff:]
    sig = jax.nn.sigmoid(a)
    silu = a * sig
    u = (silu * b).astype(bf16)
    da = (du * b * sig * (1.0 + a * (1.0 - sig))).astype(bf16)
    db = (du * silu).astype(bf16)
    return u, jnp.concatenate([da, db], axis=1)


def grad_kernel(accumulate, xa_ref, xb_ref, ca_ref, cb_ref, w13_ref, w2_ref, *refs):
    g1_ref, g3_ref, g2_ref = refs[-3:]
    ff = w2_ref.shape[1]
    d13, d2 = None, None
    for x_ref, c_ref in ((xa_ref, ca_ref), (xb_ref, cb_ref)):
        x, c = x_ref[0], c_ref[0]
        u, dab = act(nn(x, w13_ref[0]), nt(c, w2_ref[0]))
        p13, p2 = tn(x, dab), tn(u, c)
        d13, d2 = (p13, p2) if d13 is None else (d13 + p13, d2 + p2)
    if accumulate:
        g1_ref[0] = refs[0][0] + d13[:, :ff]
        g3_ref[0] = refs[1][0] + d13[:, ff:]
        g2_ref[0] = refs[2][0] + d2
    else:
        g1_ref[0] = d13[:, :ff]
        g3_ref[0] = d13[:, ff:]
        g2_ref[0] = d2


def row_kernel(slots, xa_ref, xb_ref, ca_ref, cb_ref, wo_ref, w2o_ref, wp_ref, w2p_ref, *r_refs):
    for q, (x_ref, c_ref) in enumerate(((xa_ref, ca_ref), (xb_ref, cb_ref))):
        x, c = x_ref[0], c_ref[0]
        y, dx = None, None
        for w_ref, v_ref in ((wo_ref, w2o_ref), (wp_ref, w2p_ref)):
            u, dab = act(nn(x, w_ref[0]), nt(c, v_ref[0]))
            py, pdx = nn(u, v_ref[0]), nt(dab, w_ref[0])
            y, dx = (py, pdx) if y is None else (y + py, dx + pdx)
        y, dx = y.astype(bf16), dx.astype(bf16)
        for b in range(2):
            r_refs[2 * q + b][0, 0] = y[b * slots:(b + 1) * slots]
            r_refs[2 * q + b][0, 1] = dx[b * slots:(b + 1) * slots]


def combine_kernel(groups, accumulate, slots, n_local, info_ref, win_ref, code_ref, *refs):
    n_r = 4 * len(groups)
    r_refs, rest = refs[:n_r], refs[n_r:-2]
    y0_ref, y1_ref, dx_ref = rest[-3:]
    yc_ref, xc_ref = refs[-2:]
    step = pl.program_id(0)
    code = code_ref[...]
    rows = code.shape[0]
    n_experts = 4 * n_local
    names = [(q, lo + el, r_refs[4 * gi + q], el) for gi, (lo, hi) in enumerate(groups) for q in range(4) for el in range(hi - lo)]
    width = len(names) * WIN
    lane = iota((rows, width), 1)
    place = []
    for k in range(2):
        e = code[:, k:k + 1].astype(jnp.int32)
        q, el = (e // n_local) ^ info_ref[0], e % n_local
        index = jnp.full(e.shape, -(1 << 20), jnp.int32)
        done = 0
        for lo, hi in groups:
            index = jnp.where((el >= lo) & (el < hi), done + q * (hi - lo) + (el - lo), index)
            done += 4 * (hi - lo)
        place.append(index * WIN)
    rel = [code[:, k:k + 1].astype(jnp.int32) for k in (2, 3)]

    def window(w, acc):
        y, dx = acc
        for i, (q, el_abs, r_ref, el) in enumerate(names):
            first = win_ref[step, info_ref[q] * n_local + el_abs]
            for piece in range(0, WIN, 16):
                at = pl.multiple_of(jnp.minimum(first + w * WIN + piece, slots - 16), 16)
                yc_ref[i * WIN + piece:i * WIN + piece + 16, :] = r_ref[el, 0, pl.ds(at, 16), :]
                xc_ref[i * WIN + piece:i * WIN + piece + 16, :] = r_ref[el, 1, pl.ds(at, 16), :]
        ms = []
        for k in range(2):
            inside = (rel[k] >= w * WIN) & (rel[k] < w * WIN + WIN)
            at = jnp.where(inside, place[k] + rel[k] - w * WIN, -1)
            ms.append(jnp.where(lane == at, 1.0, 0.0))
        m0, m1 = ms
        y = y + nn(jnp.concatenate([m0, m1], axis=0).astype(bf16), yc_ref[...])
        dx = dx + nn((m0 + m1).astype(bf16), xc_ref[...])
        return y, dx

    d_model = y0_ref.shape[1]
    y, dx = window(0, (jnp.zeros((2 * rows, d_model), f32), jnp.zeros((rows, d_model), f32)))
    if accumulate:
        y0_ref[...] = (rest[0][...].astype(f32) + y[:rows]).astype(bf16)
        y1_ref[...] = (rest[1][...].astype(f32) + y[rows:]).astype(bf16)
        dx_ref[...] = rest[2][...] + dx
    else:
        y0_ref[...] = y[:rows].astype(bf16)
        y1_ref[...] = y[rows:].astype(bf16)
        dx_ref[...] = dx
    n_win = win_ref[step, n_experts]

    @pl.when(n_win > 1)
    def _():
        def more(w, carry):
            y, dx = window(w, (jnp.zeros((2 * rows, d_model), f32), jnp.zeros((rows, d_model), f32)))
            y0_ref[...] = (y0_ref[...].astype(f32) + y[:rows]).astype(bf16)
            y1_ref[...] = (y1_ref[...].astype(f32) + y[rows:]).astype(bf16)
            dx_ref[...] = dx_ref[...] + dx
            return carry

        lax.fori_loop(1, n_win, more, 0)


def final_kernel(h_ref, d_ref, y0_ref, y1_ref, dx_ref, code_ref, p_ref, coef_ref, wr_ref, stat_ref,
                 out_ref, dh_ref, dr_ref):
    n_experts = p_ref.shape[1]
    code, p = code_ref[...], p_ref[...]
    e0, e1 = code[:, 0:1].astype(jnp.int32), code[:, 1:2].astype(jnp.int32)
    g0, g1, s = code[:, 4:5], code[:, 5:6], code[:, 6:7]
    h = h_ref[...]
    d = d_ref[...].astype(f32)
    y0, y1 = y0_ref[...].astype(f32), y1_ref[...].astype(f32)
    out_ref[...] = (h.astype(f32) + OUT_SCALE * (g0 * y0 + g1 * y1)).astype(bf16)
    m = OUT_SCALE * d
    dg0 = jnp.sum(m * y0, axis=1, keepdims=True)
    dg1 = jnp.sum(m * y1, axis=1, keepdims=True)
    mean = g0 * dg0 + g1 * dg1
    lane = iota(p.shape, 1)
    dp = (jnp.where(lane == e0, (dg0 - mean) / s, 0.0) + jnp.where(lane == e1, (dg1 - mean) / s, 0.0)
          + coef_ref[...])
    dz = p * (dp - jnp.sum(p * dp, axis=1, keepdims=True))
    z3 = split3(dz)
    w_hi, w_lo, _ = split3(wr_ref[...])
    back = nt(z3[0], w_hi) + (nt(z3[1], w_hi) + nt(z3[0], w_lo))
    dh_ref[...] = (d + dx_ref[...] + back).astype(bf16)
    part = tn(z3[0], h) + (tn(z3[1], h) + tn(z3[2], h))

    @pl.when(pl.program_id(0) == 0)
    def _():
        dr_ref[...] = jnp.zeros_like(dr_ref)
        dr_ref[n_experts:n_experts + 1, 0:128] = stat_ref[1:2, :]

    dr_ref[0:n_experts, :] = dr_ref[0:n_experts, :] + part


def solution(mesh):
    ep_size = mesh.shape["ep"]
    etp_size = mesh.shape["etp"]
    n_dev = ep_size * etp_size
    all_axes = ("ep", "etp")
    tok_spec = P(all_axes, None)
    gate_spec = P("ep", None, "etp")
    down_spec = P("ep", "etp", None)

    def permute(v, dep, detp):
        pairs = [(t * ep_size + o, (t ^ detp) * ep_size + (o ^ dep)) for t in range(etp_size) for o in range(ep_size)]
        return lax.ppermute(v, ("etp", "ep"), pairs)

    def kernel(body, **kw):
        return pl.pallas_call(body, **kw)

    def layer(hidden, w_router, expert_ids, d_out, w_gate, w_up, w_down):
        tok_rows, d_model = hidden.shape
        n_experts = w_router.shape[1]
        n_local, _, ff = w_gate.shape
        n_tokens = tok_rows * n_dev
        capacity = (5 * n_tokens + 2 * n_experts - 1) // (2 * n_experts)
        slots = 7 * tok_rows // (2 * n_experts)
        ep, etp = lax.axis_index("ep"), lax.axis_index("etp")
        steps = tok_rows // TILE
        sds = jax.ShapeDtypeStruct
        smem = pl.BlockSpec(memory_space=pltpu.SMEM)

        def whole(shape):
            return pl.BlockSpec(shape, lambda i: (0,) * len(shape))

        def tokens(width, tile=TILE):
            return pl.BlockSpec((tile, width), lambda i: (i, 0))

        def expert_block(shape, lo=0):
            return pl.BlockSpec((1,) + shape, lambda i: (i + lo,) + (0,) * len(shape))

        tile_ids = expert_ids.reshape(steps, TILE, 2).transpose(0, 2, 1).reshape(2 * steps, TILE)
        all_ids = lax.all_gather(tile_ids, all_axes)
        w13 = jnp.concatenate([w_gate, w_up], axis=2)
        h_send, d_send, w13_send, w2_send, all_ids = lax.optimization_barrier((hidden, d_out, w13, w_down, all_ids))

        hx, hy = permute(h_send, 2, 0), permute(h_send, 0, 1)
        dx_, dy_ = permute(d_send, 2, 0), permute(d_send, 0, 1)
        hd, dd = permute(hy, 2, 0), permute(dy_, 2, 0)
        core = lambda v: permute(v, 1, 0)
        h_pairs = {(0, 0): (hidden, core(h_send)), (1, 0): (hx, core(hx)), (0, 1): (hy, core(hy)), (1, 1): (hd, core(hd))}
        d_pairs = {(0, 0): (d_out, core(d_send)), (1, 0): (dx_, core(dx_)), (0, 1): (dy_, core(dy_)), (1, 1): (dd, core(dd))}
        partner = [(permute(w13_send[lo:hi], 0, 1), permute(w2_send[lo:hi], 0, 1)) for lo, hi in CHUNKS]

        per_block = lambda *shape: pl.BlockSpec((1,) + shape, lambda i: (i,) + (0,) * len(shape))
        slot_rows, others, starts, wr3 = kernel(
            functools.partial(slot_kernel, capacity, slots, n_local),
            grid=(n_dev,),
            in_specs=[smem, per_block(2 * steps, TILE), whole((d_model, n_experts))],
            out_specs=[per_block(steps * n_local, TILE), per_block(n_local, TILE), per_block(n_local, 128), whole((d_model, 128))],
            out_shape=[sds((n_dev, steps * n_local, TILE), f32), sds((n_dev, n_local, TILE), f32),
                       sds((n_dev, n_local, 128), jnp.int32), sds((d_model, 128), bf16)],
            scratch_shapes=[pltpu.VMEM((n_local, 128), f32)],
            compiler_params=params(), cost_estimate=cost(5e9),
        )((ep * n_local).astype(jnp.int32)[None], all_ids, w_router)

        probs, code, wins, stats = kernel(
            functools.partial(route_kernel, n_experts),
            grid=(steps,),
            in_specs=[tokens(d_model), whole((d_model, n_experts)), tokens(2)],
            out_specs=[tokens(n_experts), tokens(128), whole((8, 128)), whole((8, 128))],
            out_shape=[sds((tok_rows, n_experts), f32), sds((tok_rows, 128), f32), sds((8, 128), jnp.int32), sds((8, 128), f32)],
            compiler_params=params(), cost_estimate=cost(3e9),
        )(hidden, w_router, expert_ids)

        def gather(pair):
            x, t = pair
            info = jnp.stack([(ep ^ (2 * x)) * etp_size + (etp ^ t), (ep ^ (2 * x + 1)) * etp_size + (etp ^ t), ep * n_local]).astype(jnp.int32)
            block = sds((n_local, 2 * slots, d_model), bf16)
            tile = pl.BlockSpec((TILE, d_model), lambda i: (jnp.minimum(i, steps - 1), 0))
            out = pl.BlockSpec((1, 2 * slots, d_model), lambda i: (jnp.maximum(i - steps, 0), 0, 0))
            return kernel(
                functools.partial(gather_kernel, slots, n_local, n_experts),
                grid=(steps + n_local,),
                in_specs=[smem, smem, whole(slot_rows.shape), whole(others.shape), whole(wr3.shape)] + [tile] * 4,
                out_specs=[out] * 2,
                out_shape=[block, block],
                scratch_shapes=[pltpu.VMEM((n_local * WIN, TILE), bf16)] + [pltpu.VMEM((2, n_local, slots + 64, d_model), bf16)] * 2,
                compiler_params=params(), cost_estimate=cost(8e9),
            )(info, starts, slot_rows, others, wr3, *h_pairs[pair], *d_pairs[pair])

        rows = {pair: gather(pair) for pair in h_pairs}
        row_block = expert_block((2 * slots, d_model))
        g13, g2 = expert_block((d_model, ff)), expert_block((ff, d_model))

        def grads(first, second, acc):
            (xa, ca), (xb, cb) = rows[first], rows[second]
            return kernel(
                functools.partial(grad_kernel, bool(acc)),
                grid=(n_local,),
                in_specs=[row_block] * 4 + [expert_block((d_model, 2 * ff)), expert_block((ff, d_model))] + [g13, g13, g2][:len(acc)],
                out_specs=[g13, g13, g2],
                out_shape=[sds((n_local, d_model, ff), f32)] * 2 + [sds((n_local, ff, d_model), f32)],
                input_output_aliases={6 + k: k for k in range(len(acc))},
                compiler_params=params(), cost_estimate=cost(25e9),
            )(xa, xb, ca, cb, w13, w_down, *acc)

        grad = grads((0, 0), (1, 0), ())
        g_gate, g_up, g_down = grads((0, 1), (1, 1), tuple(grad))

        def back(index):
            lo, hi = CHUNKS[index]
            (xa, ca), (xb, cb) = rows[(0, 0)], rows[(1, 0)]
            at = lambda shape: expert_block(shape, lo)
            outs = kernel(
                functools.partial(row_kernel, slots),
                grid=(hi - lo,),
                in_specs=[at((2 * slots, d_model))] * 4 + [at((d_model, 2 * ff)), at((ff, d_model)),
                          expert_block((d_model, 2 * ff)), expert_block((ff, d_model))],
                out_specs=[expert_block((2, slots, d_model))] * 4,
                out_shape=[sds((hi - lo, 2, slots, d_model), bf16)] * 4,
                compiler_params=params(), cost_estimate=cost(6e9 * (hi - lo)),
            )(xa, xb, ca, cb, w13, w_down, *partner[index])
            return [outs[0]] + [permute(outs[q], q, 0) for q in (1, 2, 3)]

        returned = [back(i) for i in range(len(CHUNKS))]
        total = jnp.sum((all_ids.reshape(-1)[:, None] == jnp.arange(n_experts)[None, :]).astype(f32), axis=0)[None, :]
        coef = (AUX_COEF * n_experts / n_tokens / (2 * n_tokens)) * total
        ep_info = jnp.stack([ep ^ q for q in range(4)]).astype(jnp.int32)

        def combine(chunk_ids, acc):
            groups = tuple(CHUNKS[i] for i in chunk_ids)
            arrays = [r for i in chunk_ids for r in returned[i]]
            acc_specs = [tokens(d_model)] * 3
            width = 4 * sum(hi - lo for lo, hi in groups) * WIN
            return kernel(
                functools.partial(combine_kernel, groups, bool(acc), slots, n_local),
                grid=(steps,),
                in_specs=[smem, smem, tokens(128)] + [whole(r.shape) for r in arrays] + acc_specs[:len(acc)],
                out_specs=acc_specs,
                out_shape=[sds((tok_rows, d_model), bf16)] * 2 + [sds((tok_rows, d_model), f32)],
                scratch_shapes=[pltpu.VMEM((width, d_model), bf16)] * 2,
                compiler_params=params(), cost_estimate=cost(3e9 * len(chunk_ids)),
            )(ep_info, wins, code, *arrays, *acc)

        acc = combine((0, 1), ())
        acc = combine((2, 3), tuple(acc))
        y0, y1, dxs = combine((4,), tuple(acc))

        output, d_hidden, d_rt = kernel(
            final_kernel,
            grid=(steps,),
            in_specs=[tokens(d_model)] * 5 + [tokens(128), tokens(n_experts), whole((1, n_experts)), whole((d_model, n_experts)),
                      whole((8, 128))],
            out_specs=[tokens(d_model)] * 2 + [whole((n_experts + 8, d_model))],
            out_shape=[sds((tok_rows, d_model), bf16)] * 2 + [sds((n_experts + 8, d_model), f32)],
            compiler_params=params(), cost_estimate=cost(4e9),
        )(hidden, d_out, y0, y1, dxs, code, probs, coef, w_router, stats)
        for dep, detp in ((1, 0), (2, 0), (0, 1)):
            d_rt = d_rt + permute(d_rt, dep, detp)
        d_router = d_rt[:n_experts].T
        route_frac = total[0] / (2 * n_tokens)
        aux_loss = AUX_COEF * n_experts * jnp.sum(route_frac * (d_rt[n_experts, :n_experts] / n_tokens))
        return output, d_hidden, d_router, aux_loss, g_gate, g_up, g_down


    return jax.shard_map(layer, mesh=mesh, in_specs=(tok_spec, P(), tok_spec, tok_spec, gate_spec, gate_spec, down_spec), out_specs=(tok_spec, tok_spec, P(), P(), gate_spec, gate_spec, down_spec), check_vma=False)
```

profile of v0, /device:TPU:0, one launch (start us, length us, event | category | flops | bytes accessed | tf_op | source)
XLA Modules:
  0.0 767.0 jit_solution(8257511812707970721)
XLA Ops:
  1.4 13.9 %all_gather.3.ids_ref = s32[8,16,256]{2,1,0:T(8,128)S(1)} all-gather(s32[1,16,256]{2,1,0:T(8,128)S(1)} %all_gather_reshape.3), channel_id=1, replica_groups=mesh['etp'=2,'ep'=4] {'ep','etp'}, dimensions={0}, use_global_device_ids=true | all-gather | bytes 147456 | tf_op jit(solution)/shard_map/all_gather | solution.py:359
  15.3 4.2 constant_dynamic-update-slice_fusion.1
  19.5 2.0 constant_dynamic-update-slice_fusion.wo_ref.w13_ref
  22.0 1.5 collective-permute-start.4
  28.3 8.6 %shard_map.126 = (f32[2048,32]{1,0:T(8,128)}, f32[2048,128]{1,0:T(8,128)}, s32[8,128]{1,0:T(8,128)}, f32[8,128]{1,0:T(8,128)}) custom-call(bf16[2048,512]{1,0:T(8,128)(2,1)} %h_ref.3, f32[512,32]{1,0:T(8,128)} %copy.27.wr_ref, s32[2048,2]{1,0:T(8,128)} %copy.28.ids_ref), custom_call_target="tpu_custom_call" | custom-call | flops 3000000000 | bytes 1048576 | tf_op jit(solution)/shard_map/pallas_call | solution.py:383
  36.9 33.5 %collective-permute-done.2.ha_ref = bf16[2048,512]{1,0:T(8,128)(2,1)} collective-permute-done((bf16[2048,512]{1,0:T(8,128)(2,1)}, bf16[2048,512]{1,0:T(8,128)(2,1)}, u32[]{:S(2)}, u32[]{:S(2)}) %collective-permute-start.2) | collective-permute-done | bytes 2097184 | tf_op jit(solution)/shard_map/ppermute | solution.py:332
  71.5 2.6 fusion.4
  75.3 37.0 %collective-permute-done.4.da_ref = bf16[2048,512]{1,0:T(8,128)(2,1)} collective-permute-done((bf16[2048,512]{1,0:T(8,128)(2,1)}, bf16[2048,512]{1,0:T(8,128)(2,1)}, u32[]{:S(2)}, u32[]{:S(2)}) %collective-permute-start.4) | collective-permute-done | bytes 2097184 | tf_op jit(solution)/shard_map/ppermute | solution.py:332
  112.3 4.6 fusion.3
  117.0 1.5 collective-permute-start.16
  120.6 16.5 %shard_map.127 = (f32[8,64,256]{2,1,0:T(8,128)}, f32[8,8,256]{2,1,0:T(8,128)}, s32[8,8,128]{2,1,0:T(8,128)}, bf16[512,128]{1,0:T(8,128)(2,1)}) custom-call(s32[1]{0:T(128)} %bitcast.6.info_ref, s32[8,16,256]{2,1,0:T(8,128)} %copy-done.5, f32[512,32]{1,0:T(8,128)} %copy.27.wr_ref), custom_call_target="tpu_custom_call" | custom-call | flops 5000000000 | bytes 1048576 | tf_op jit(solution)/shard_map/pallas_call | solution.py:372
  137.2 1.5 collective-permute-start.26
  139.9 1.5 collective-permute-start.27
  141.9 16.7 %shard_map.128 = (bf16[8,448,512]{2,1,0:T(8,128)(2,1)}, bf16[8,448,512]{2,1,0:T(8,128)(2,1)}) custom-call(s32[3]{0:T(128)} %add_add_fusion.info_ref, s32[8,8,128]{2,1,0:T(8,128)} %get-tuple-element.69.start_ref, f32[8,64,256]{2,1,0:T(8,128)} %get-tuple-element.70.slot_ref, f32[8,8,256]{2,1,0:T(8,128)} %get-tuple-element.71.other_ref, ...), custom_call_target="tpu_custom_call" | custom-call | flops 8000000000 | bytes 1048576 | tf_op jit(solution)/shard_map/pallas_call | solution.py:398
  158.7 1.5 collective-permute-start.34
  160.2 16.7 %shard_map.129 = (bf16[8,448,512]{2,1,0:T(8,128)(2,1)}, bf16[8,448,512]{2,1,0:T(8,128)(2,1)}) custom-call(s32[3]{0:T(128)} %add_add_fusion.1.info_ref, s32[8,8,128]{2,1,0:T(8,128)} %get-tuple-element.69.start_ref, f32[8,64,256]{2,1,0:T(8,128)} %get-tuple-element.70.slot_ref, f32[8,8,256]{2,1,0:T(8,128)} %get-tuple-element.71.other_ref, ...), custom_call_target="tpu_custom_call" | custom-call | flops 8000000000 | bytes 1048576 | tf_op jit(solution)/shard_map/pallas_call | solution.py:398
  176.9 14.7 %collective-permute-done.6.wp_ref = bf16[1,512,768]{2,1,0:T(8,128)(2,1)S(1)} collective-permute-done((bf16[1,512,768]{2,1,0:T(8,128)(2,1)}, bf16[1,512,768]{2,1,0:T(8,128)(2,1)S(1)}, u32[]{:S(2)}, u32[]{:S(2)}) %collective-permute-start.6) | collective-permute-done | bytes 786464 | tf_op jit(solution)/shard_map/ppermute | solution.py:332
  191.6 1.5 collective-permute-start.36
  193.0 15.5 %collective-permute-done.27.w2p_ref = bf16[2,384,512]{2,1,0:T(8,128)(2,1)} collective-permute-done((bf16[2,384,512]{2,1,0:T(8,128)(2,1)}, bf16[2,384,512]{2,1,0:T(8,128)(2,1)}, u32[]{:S(2)}, u32[]{:S(2)}) %collective-permute-start.27) | collective-permute-done | bytes 786464 | tf_op jit(solution)/shard_map/ppermute | solution.py:332
  208.5 1.5 collective-permute-start.12
  210.0 15.4 %collective-permute-done.22.w2p_ref = bf16[2,384,512]{2,1,0:T(8,128)(2,1)} collective-permute-done((bf16[2,384,512]{2,1,0:T(8,128)(2,1)}, bf16[2,384,512]{2,1,0:T(8,128)(2,1)}, u32[]{:S(2)}, u32[]{:S(2)}) %collective-permute-start.22) | collective-permute-done | bytes 786464 | tf_op jit(solution)/shard_map/ppermute | solution.py:332
  225.4 1.5 collective-permute-start.21
  227.4 14.3 %shard_map.134 = (bf16[2,2,224,512]{3,2,1,0:T(8,128)(2,1)}, bf16[2,2,224,512]{3,2,1,0:T(8,128)(2,1)}, bf16[2,2,224,512]{3,2,1,0:T(8,128)(2,1)}, bf16[2,2,224,512]{3,2,1,0:T(8,128)(2,1)}) custom-call(bf16[8,448,512]{2,1,0:T(8,128)(2,1)} %get-tuple-element.75.xa_ref, bf16[8,448,512]{2,1,0:T(8,128)(2,1)} %get-tuple-element.76.xb_ref, ...), custom_call_target="tpu_custom_call" | custom-call | flops 12000000000 | bytes 1048576 | tf_op jit(solution)/shard_map/pallas_call | solution.py:431
  241.7 8.4 %shard_map.132 = (bf16[1,2,224,512]{3,2,1,0:T(8,128)(2,1)}, bf16[1,2,224,512]{3,2,1,0:T(8,128)(2,1)}, bf16[1,2,224,512]{3,2,1,0:T(8,128)(2,1)}, bf16[1,2,224,512]{3,2,1,0:T(8,128)(2,1)}) custom-call(bf16[8,448,512]{2,1,0:T(8,128)(2,1)} %get-tuple-element.75.xa_ref, bf16[8,448,512]{2,1,0:T(8,128)(2,1)} %get-tuple-element.76.xb_ref, ...), custom_call_target="tpu_custom_call" | custom-call | flops 6000000000 | bytes 1048576 | tf_op jit(solution)/shard_map/pallas_call | solution.py:431
  250.1 82.0 %collective-permute-done.12.w2p_ref = bf16[2,384,512]{2,1,0:T(8,128)(2,1)} collective-permute-done((bf16[2,384,512]{2,1,0:T(8,128)(2,1)}, bf16[2,384,512]{2,1,0:T(8,128)(2,1)}, u32[]{:S(2)}, u32[]{:S(2)}) %collective-permute-start.12) | collective-permute-done | bytes 786464 | tf_op jit(solution)/shard_map/ppermute | solution.py:332
  332.1 33.7 %collective-permute-done.21.wp_ref = bf16[2,512,768]{2,1,0:T(8,128)(2,1)} collective-permute-done((bf16[2,512,768]{2,1,0:T(8,128)(2,1)S(1)}, bf16[2,512,768]{2,1,0:T(8,128)(2,1)}, u32[]{:S(2)}, u32[]{:S(2)}) %collective-permute-start.21) | collective-permute-done | bytes 1572896 | tf_op jit(solution)/shard_map/ppermute | solution.py:332
  365.8 1.5 collective-permute-start.19
  367.3 31.4 %collective-permute-done.11.wp_ref = bf16[2,512,768]{2,1,0:T(8,128)(2,1)} collective-permute-done((bf16[2,512,768]{2,1,0:T(8,128)(2,1)S(1)}, bf16[2,512,768]{2,1,0:T(8,128)(2,1)}, u32[]{:S(2)}, u32[]{:S(2)}) %collective-permute-start.11) | collective-permute-done | bytes 1572896 | tf_op jit(solution)/shard_map/ppermute | solution.py:332
  399.8 13.9 %shard_map.133 = (bf16[2,2,224,512]{3,2,1,0:T(8,128)(2,1)}, bf16[2,2,224,512]{3,2,1,0:T(8,128)(2,1)}, bf16[2,2,224,512]{3,2,1,0:T(8,128)(2,1)}, bf16[2,2,224,512]{3,2,1,0:T(8,128)(2,1)}) custom-call(bf16[8,448,512]{2,1,0:T(8,128)(2,1)} %get-tuple-element.75.xa_ref, bf16[8,448,512]{2,1,0:T(8,128)(2,1)} %get-tuple-element.76.xb_ref, ...), custom_call_target="tpu_custom_call" | custom-call | flops 12000000000 | bytes 1048576 | tf_op jit(solution)/shard_map/pallas_call | solution.py:431
  417.3 14.0 %shard_map.131 = (bf16[2,2,224,512]{3,2,1,0:T(8,128)(2,1)}, bf16[2,2,224,512]{3,2,1,0:T(8,128)(2,1)}, bf16[2,2,224,512]{3,2,1,0:T(8,128)(2,1)}, bf16[2,2,224,512]{3,2,1,0:T(8,128)(2,1)}) custom-call(bf16[8,448,512]{2,1,0:T(8,128)(2,1)} %get-tuple-element.75.xa_ref, bf16[8,448,512]{2,1,0:T(8,128)(2,1)} %get-tuple-element.76.xb_ref, ...), custom_call_target="tpu_custom_call" | custom-call | flops 12000000000 | bytes 1048576 | tf_op jit(solution)/shard_map/pallas_call | solution.py:431
  431.2 5.8 collective-permute-done.29.refs_6_
  438.0 17.2 %collective-permute-done.30.refs_7_ = bf16[2,2,224,512]{3,2,1,0:T(8,128)(2,1)} collective-permute-done((bf16[2,2,224,512]{3,2,1,0:T(8,128)(2,1)}, bf16[2,2,224,512]{3,2,1,0:T(8,128)(2,1)}, u32[]{:S(2)}, u32[]{:S(2)}) %collective-permute-start.30) | collective-permute-done | bytes 917536 | tf_op jit(solution)/shard_map/ppermute | solution.py:332
  457.2 19.1 %collective-permute-done.24.refs_2_ = bf16[2,2,224,512]{3,2,1,0:T(8,128)(2,1)} collective-permute-done((bf16[2,2,224,512]{3,2,1,0:T(8,128)(2,1)}, bf16[2,2,224,512]{3,2,1,0:T(8,128)(2,1)}, u32[]{:S(2)}, u32[]{:S(2)}) %collective-permute-start.24) | collective-permute-done | bytes 917536 | tf_op jit(solution)/shard_map/ppermute | solution.py:332
  477.4 17.2 %collective-permute-done.25.refs_3_ = bf16[2,2,224,512]{3,2,1,0:T(8,128)(2,1)} collective-permute-done((bf16[2,2,224,512]{3,2,1,0:T(8,128)(2,1)}, bf16[2,2,224,512]{3,2,1,0:T(8,128)(2,1)}, u32[]{:S(2)}, u32[]{:S(2)}) %collective-permute-start.25) | collective-permute-done | bytes 917536 | tf_op jit(solution)/shard_map/ppermute | solution.py:332
  494.5 1.9 collective-permute-start.15
  496.5 8.4 %shard_map.130 = (bf16[1,2,224,512]{3,2,1,0:T(8,128)(2,1)}, bf16[1,2,224,512]{3,2,1,0:T(8,128)(2,1)}, bf16[1,2,224,512]{3,2,1,0:T(8,128)(2,1)}, bf16[1,2,224,512]{3,2,1,0:T(8,128)(2,1)}) custom-call(bf16[8,448,512]{2,1,0:T(8,128)(2,1)} %get-tuple-element.75.xa_ref, bf16[8,448,512]{2,1,0:T(8,128)(2,1)} %get-tuple-element.76.xb_ref, ...), custom_call_target="tpu_custom_call" | custom-call | flops 6000000000 | bytes 1048576 | tf_op jit(solution)/shard_map/pallas_call | solution.py:431
  504.8 14.1 %shard_map.135 = (bf16[2048,512]{1,0:T(8,128)(2,1)}, bf16[2048,512]{1,0:T(8,128)(2,1)}, f32[2048,512]{1,0:T(8,128)}) custom-call(s32[4]{0:T(128)} %pad_add_fusion.info_ref, s32[8,128]{1,0:T(8,128)} %get-tuple-element.66.win_ref, f32[2048,128]{1,0:T(8,128)} %get-tuple-element.67.code_ref, bf16[2,2,224,512]{3,2,1,0:T(8,128)(2,1)} %get-tuple-element.93.refs_0_, ...), custom_call_target="tpu_custom_call" | custom-call | flops 6000000000 | bytes 1048576 | tf_op jit(solution)/shard_map/pallas_call | solution.py:452
  519.4 86.1 %collective-permute-done.14.refs_2_ = bf16[2,2,224,512]{3,2,1,0:T(8,128)(2,1)} collective-permute-done((bf16[2,2,224,512]{3,2,1,0:T(8,128)(2,1)}, bf16[2,2,224,512]{3,2,1,0:T(8,128)(2,1)}, u32[]{:S(2)}, u32[]{:S(2)}) %collective-permute-start.14) | collective-permute-done | bytes 917536 | tf_op jit(solution)/shard_map/ppermute | solution.py:332
  606.6 17.2 %collective-permute-done.15.refs_3_ = bf16[2,2,224,512]{3,2,1,0:T(8,128)(2,1)} collective-permute-done((bf16[2,2,224,512]{3,2,1,0:T(8,128)(2,1)}, bf16[2,2,224,512]{3,2,1,0:T(8,128)(2,1)}, u32[]{:S(2)}, u32[]{:S(2)}) %collective-permute-start.15) | collective-permute-done | bytes 917536 | tf_op jit(solution)/shard_map/ppermute | solution.py:332
  623.8 1.9 collective-permute-start.10
  625.7 14.9 %shard_map.136 = (bf16[2048,512]{1,0:T(8,128)(2,1)}, bf16[2048,512]{1,0:T(8,128)(2,1)}, f32[2048,512]{1,0:T(8,128)}) custom-call(s32[4]{0:T(128)} %pad_add_fusion.info_ref, s32[8,128]{1,0:T(8,128)} %get-tuple-element.66.win_ref, f32[2048,128]{1,0:T(8,128)} %get-tuple-element.67.code_ref, bf16[2,2,224,512]{3,2,1,0:T(8,128)(2,1)} %get-tuple-element.85.refs_0_, ...), custom_call_target="tpu_custom_call" | custom-call | flops 6000000000 | bytes 1048576 | tf_op jit(solution)/shard_map/pallas_call | solution.py:452
  640.6 2.3 collective-permute-done.10.refs_3_
  643.7 11.5 %shard_map.137 = (bf16[2048,512]{1,0:T(8,128)(2,1)}, bf16[2048,512]{1,0:T(8,128)(2,1)}, f32[2048,512]{1,0:T(8,128)}) custom-call(s32[4]{0:T(128)} %pad_add_fusion.info_ref, s32[8,128]{1,0:T(8,128)} %get-tuple-element.66.win_ref, f32[2048,128]{1,0:T(8,128)} %get-tuple-element.67.code_ref, bf16[1,2,224,512]{3,2,1,0:T(8,128)(2,1)} %get-tuple-element.81.refs_0_, ...), custom_call_target="tpu_custom_call" | custom-call | flops 3000000000 | bytes 1048576 | tf_op jit(solution)/shard_map/pallas_call | solution.py:452
  655.2 15.1 %shard_map.138 = (bf16[2048,512]{1,0:T(8,128)(2,1)}, bf16[2048,512]{1,0:T(8,128)(2,1)}, f32[40,512]{1,0:T(8,128)}) custom-call(bf16[2048,512]{1,0:T(8,128)(2,1)} %h_ref.3, bf16[2048,512]{1,0:T(8,128)(2,1)} %d_ref.1, bf16[2048,512]{1,0:T(8,128)(2,1)} %get-tuple-element.107.y0_ref, bf16[2048,512]{1,0:T(8,128)(2,1)} %get-tuple-element.108.y1_ref, ...), custom_call_target="tpu_custom_call" | custom-call | flops 4000000000 | bytes 1048576 | tf_op jit(solution)/shard_map/pallas_call | solution.py:466
  674.8 26.8 %shard_map.141 = (f32[8,512,384]{2,1,0:T(8,128)}, f32[8,512,384]{2,1,0:T(8,128)}, f32[8,384,512]{2,1,0:T(8,128)}) custom-call(bf16[8,448,512]{2,1,0:T(8,128)(2,1)} %get-tuple-element.75.xa_ref, bf16[8,448,512]{2,1,0:T(8,128)(2,1)} %get-tuple-element.76.xb_ref, bf16[8,448,512]{2,1,0:T(8,128)(2,1)} %get-tuple-element.77.ca_ref, ...), custom_call_target="tpu_custom_call" | custom-call | flops 24999999488 | bytes 1048576 | tf_op jit(solution)/shard_map/pallas_call | solution.py:414
  702.6 16.7 %shard_map.139 = (bf16[8,448,512]{2,1,0:T(8,128)(2,1)}, bf16[8,448,512]{2,1,0:T(8,128)(2,1)}) custom-call(s32[3]{0:T(128)} %add_add_fusion.2.info_ref, s32[8,8,128]{2,1,0:T(8,128)} %get-tuple-element.69.start_ref, f32[8,64,256]{2,1,0:T(8,128)} %get-tuple-element.70.slot_ref, f32[8,8,256]{2,1,0:T(8,128)} %get-tuple-element.71.other_ref, ...), custom_call_target="tpu_custom_call" | custom-call | flops 8000000000 | bytes 1048576 | tf_op jit(solution)/shard_map/pallas_call | solution.py:398
  721.3 16.7 %shard_map.140 = (bf16[8,448,512]{2,1,0:T(8,128)(2,1)}, bf16[8,448,512]{2,1,0:T(8,128)(2,1)}) custom-call(s32[3]{0:T(128)} %add_add_fusion.3.info_ref, s32[8,8,128]{2,1,0:T(8,128)} %get-tuple-element.69.start_ref, f32[8,64,256]{2,1,0:T(8,128)} %get-tuple-element.70.slot_ref, f32[8,8,256]{2,1,0:T(8,128)} %get-tuple-element.71.other_ref, ...), custom_call_target="tpu_custom_call" | custom-call | flops 8000000000 | bytes 1048576 | tf_op jit(solution)/shard_map/pallas_call | solution.py:398
  738.0 27.6 %shard_map.142 = (f32[8,512,384]{2,1,0:T(8,128)}, f32[8,512,384]{2,1,0:T(8,128)}, f32[8,384,512]{2,1,0:T(8,128)}) custom-call(bf16[8,448,512]{2,1,0:T(8,128)(2,1)} %get-tuple-element.115.xa_ref, bf16[8,448,512]{2,1,0:T(8,128)(2,1)} %get-tuple-element.116.xb_ref, ...), custom_call_target="tpu_custom_call", output_to_operand_aliasing={{0}: (6, {}), {1}: (7, {}), {2}: (8, {})} | custom-call | flops 24999999488 | bytes 1048576 | tf_op jit(solution)/shard_map/pallas_call | solution.py:414
  (114 shorter events, 30.8 us)
Async XLA Ops:
  21.5 48.8 %collective-permute-start.2 = (bf16[2048,512]{1,0:T(8,128)(2,1)}, bf16[2048,512]{1,0:T(8,128)(2,1)}, u32[]{:S(2)}, u32[]{:S(2)}) collective-permute-start(bf16[2048,512]{1,0:T(8,128)(2,1)} %h_ref.3), channel_id=1, source_target_pairs={{0,2},{1,3},{2,0},{3,1},{4,6},{5,7},{6,4},{7,5}} | collective-permute-start | bytes 6291464 | tf_op jit(solution)/shard_map/ppermute | solution.py:332
  22.0 90.3 %collective-permute-start.4 = (bf16[2048,512]{1,0:T(8,128)(2,1)}, bf16[2048,512]{1,0:T(8,128)(2,1)}, u32[]{:S(2)}, u32[]{:S(2)}) collective-permute-start(bf16[2048,512]{1,0:T(8,128)(2,1)} %d_ref.1), channel_id=1, source_target_pairs={{0,2},{1,3},{2,0},{3,1},{4,6},{5,7},{6,4},{7,5}} | collective-permute-start | bytes 6291464 | tf_op jit(solution)/shard_map/ppermute | solution.py:332
  23.5 115.8 %collective-permute-start = (bf16[2048,512]{1,0:T(8,128)(2,1)}, bf16[2048,512]{1,0:T(8,128)(2,1)}, u32[]{:S(2)}, u32[]{:S(2)}) collective-permute-start(bf16[2048,512]{1,0:T(8,128)(2,1)} %h_ref.3), channel_id=1, source_target_pairs={{0,1},{1,0},{2,3},{3,2},{4,5},{5,4},{6,7},{7,6}} | collective-permute-start | bytes 6291464 | tf_op jit(solution)/shard_map/ppermute | solution.py:332
  23.5 116.4 %collective-permute-start.1 = (bf16[2048,512]{1,0:T(8,128)(2,1)}, bf16[2048,512]{1,0:T(8,128)(2,1)}, u32[]{:S(2)}, u32[]{:S(2)}) collective-permute-start(bf16[2048,512]{1,0:T(8,128)(2,1)} %d_ref.1), channel_id=1, source_target_pairs={{0,1},{1,0},{2,3},{3,2},{4,5},{5,4},{6,7},{7,6}} | collective-permute-start | bytes 6291464 | tf_op jit(solution)/shard_map/ppermute | solution.py:332
  25.0 49.2 %collective-permute-start.17 = (bf16[1,384,512]{2,1,0:T(8,128)(2,1)}, bf16[1,384,512]{2,1,0:T(8,128)(2,1)}, u32[]{:S(2)}, u32[]{:S(2)}) collective-permute-start(bf16[1,384,512]{2,1,0:T(8,128)(2,1)} %get-tuple-element.133), channel_id=1, source_target_pairs={{0,4},{1,5},{2,6},{3,7},{4,0},{5,1},{6,2},{7,3}} | collective-permute-start | bytes 1179656 | tf_op jit(solution)/shard_map/ppermute | solution.py:332
  36.9 37.3 %copy-start.9 = (bf16[1,384,512]{2,1,0:T(8,128)(2,1)S(1)}, bf16[1,384,512]{2,1,0:T(8,128)(2,1)}, u32[]{:S(2)}) copy-start(bf16[1,384,512]{2,1,0:T(8,128)(2,1)} %get-tuple-element.134) | copy-start | bytes 1179652
  70.3 71.1 %collective-permute-start.3 = (bf16[2048,512]{1,0:T(8,128)(2,1)}, bf16[2048,512]{1,0:T(8,128)(2,1)}, u32[]{:S(2)}, u32[]{:S(2)}) collective-permute-start(bf16[2048,512]{1,0:T(8,128)(2,1)} %collective-permute-done.2.ha_ref), channel_id=1, source_target_pairs={{0,1},{1,0},{2,3},{3,2},{4,5},{5,4},{6,7},{7,6}} | collective-permute-start | bytes 6291464 | tf_op jit(solution)/shard_map/ppermute | solution.py:332
  74.1 42.8 %collective-permute-start.7 = (bf16[1,384,512]{2,1,0:T(8,128)(2,1)S(1)}, bf16[1,384,512]{2,1,0:T(8,128)(2,1)}, u32[]{:S(2)}, u32[]{:S(2)}) collective-permute-start(bf16[1,384,512]{2,1,0:T(8,128)(2,1)S(1)} %copy-done.9), channel_id=1, source_target_pairs={{0,4},{1,5},{2,6},{3,7},{4,0},{5,1},{6,2},{7,3}} | collective-permute-start | bytes 1179656 | tf_op jit(solution)/shard_map/ppermute | solution.py:332
  112.3 46.3 %collective-permute-start.5 = (bf16[2048,512]{1,0:T(8,128)(2,1)}, bf16[2048,512]{1,0:T(8,128)(2,1)}, u32[]{:S(2)}, u32[]{:S(2)}) collective-permute-start(bf16[2048,512]{1,0:T(8,128)(2,1)} %collective-permute-done.4.da_ref), channel_id=1, source_target_pairs={{0,1},{1,0},{2,3},{3,2},{4,5},{5,4},{6,7},{7,6}} | collective-permute-start | bytes 6291464 | tf_op jit(solution)/shard_map/ppermute | solution.py:332
  117.0 20.3 %collective-permute-start.16 = (bf16[1,512,768]{2,1,0:T(8,128)(2,1)}, bf16[1,512,768]{2,1,0:T(8,128)(2,1)}, u32[]{:S(2)}, u32[]{:S(2)}) collective-permute-start(bf16[1,512,768]{2,1,0:T(8,128)(2,1)} %get-tuple-element.128), channel_id=1, source_target_pairs={{0,4},{1,5},{2,6},{3,7},{4,0},{5,1},{6,2},{7,3}} | collective-permute-start | bytes 2359304 | tf_op jit(solution)/shard_map/ppermute | solution.py:332
  137.2 89.6 %collective-permute-start.26 = (bf16[2,512,768]{2,1,0:T(8,128)(2,1)}, bf16[2,512,768]{2,1,0:T(8,128)(2,1)}, u32[]{:S(2)}, u32[]{:S(2)}) collective-permute-start(bf16[2,512,768]{2,1,0:T(8,128)(2,1)} %get-tuple-element.125), channel_id=1, source_target_pairs={{0,4},{1,5},{2,6},{3,7},{4,0},{5,1},{6,2},{7,3}} | collective-permute-start | bytes 4718600 | tf_op jit(solution)/shard_map/ppermute | solution.py:332
  139.4 52.2 %collective-permute-start.6 = (bf16[1,512,768]{2,1,0:T(8,128)(2,1)}, bf16[1,512,768]{2,1,0:T(8,128)(2,1)S(1)}, u32[]{:S(2)}, u32[]{:S(2)}) collective-permute-start(bf16[1,512,768]{2,1,0:T(8,128)(2,1)} %get-tuple-element.129), channel_id=1, source_target_pairs={{0,4},{1,5},{2,6},{3,7},{4,0},{5,1},{6,2},{7,3}} | collective-permute-start | bytes 2359304 | tf_op jit(solution)/shard_map/ppermute | solution.py:332
  139.9 68.6 %collective-permute-start.27 = (bf16[2,384,512]{2,1,0:T(8,128)(2,1)}, bf16[2,384,512]{2,1,0:T(8,128)(2,1)}, u32[]{:S(2)}, u32[]{:S(2)}) collective-permute-start(bf16[2,384,512]{2,1,0:T(8,128)(2,1)} %get-tuple-element.130), channel_id=1, source_target_pairs={{0,4},{1,5},{2,6},{3,7},{4,0},{5,1},{6,2},{7,3}} | collective-permute-start | bytes 2359304 | tf_op jit(solution)/shard_map/ppermute | solution.py:332
  141.4 84.0 %collective-permute-start.22 = (bf16[2,384,512]{2,1,0:T(8,128)(2,1)}, bf16[2,384,512]{2,1,0:T(8,128)(2,1)}, u32[]{:S(2)}, u32[]{:S(2)}) collective-permute-start(bf16[2,384,512]{2,1,0:T(8,128)(2,1)} %get-tuple-element.131), channel_id=1, source_target_pairs={{0,4},{1,5},{2,6},{3,7},{4,0},{5,1},{6,2},{7,3}} | collective-permute-start | bytes 2359304 | tf_op jit(solution)/shard_map/ppermute | solution.py:332
  158.6 66.7 %copy-start.3 = (bf16[2,512,768]{2,1,0:T(8,128)(2,1)S(1)}, bf16[2,512,768]{2,1,0:T(8,128)(2,1)}, u32[]{:S(2)}) copy-start(bf16[2,512,768]{2,1,0:T(8,128)(2,1)} %get-tuple-element.126) | copy-start | bytes 4718596
  158.6 68.2 %copy-start.2 = (bf16[2,512,768]{2,1,0:T(8,128)(2,1)S(1)}, bf16[2,512,768]{2,1,0:T(8,128)(2,1)}, u32[]{:S(2)}) copy-start(bf16[2,512,768]{2,1,0:T(8,128)(2,1)} %get-tuple-element.127) | copy-start | bytes 4718596
  158.7 240.0 %collective-permute-start.34 = (bf16[2048,512]{1,0:T(8,128)(2,1)}, bf16[2048,512]{1,0:T(8,128)(2,1)}, u32[]{:S(2)}, u32[]{:S(2)}) collective-permute-start(bf16[2048,512]{1,0:T(8,128)(2,1)} %h_ref.3), channel_id=1, source_target_pairs={{0,4},{1,5},{2,6},{3,7},{4,0},{5,1},{6,2},{7,3}} | collective-permute-start | bytes 6291464 | tf_op jit(solution)/shard_map/ppermute | solution.py:332
  191.6 50.1 %copy-start.4 = (bf16[1,512,768]{2,1,0:T(8,128)(2,1)}, bf16[1,512,768]{2,1,0:T(8,128)(2,1)S(1)}, u32[]{:S(2)}) copy-start(bf16[1,512,768]{2,1,0:T(8,128)(2,1)S(1)} %collective-permute-done.6.wp_ref) | copy-start | bytes 2359300
  191.6 222.1 %collective-permute-start.36 = (bf16[2048,512]{1,0:T(8,128)(2,1)}, bf16[2048,512]{1,0:T(8,128)(2,1)}, u32[]{:S(2)}, u32[]{:S(2)}) collective-permute-start(bf16[2048,512]{1,0:T(8,128)(2,1)} %d_ref.1), channel_id=1, source_target_pairs={{0,4},{1,5},{2,6},{3,7},{4,0},{5,1},{6,2},{7,3}} | collective-permute-start | bytes 6291464 | tf_op jit(solution)/shard_map/ppermute | solution.py:332
  208.5 123.6 %collective-permute-start.12 = (bf16[2,384,512]{2,1,0:T(8,128)(2,1)}, bf16[2,384,512]{2,1,0:T(8,128)(2,1)}, u32[]{:S(2)}, u32[]{:S(2)}) collective-permute-start(bf16[2,384,512]{2,1,0:T(8,128)(2,1)} %get-tuple-element.132), channel_id=1, source_target_pairs={{0,4},{1,5},{2,6},{3,7},{4,0},{5,1},{6,2},{7,3}} | collective-permute-start | bytes 2359304 | tf_op jit(solution)/shard_map/ppermute | solution.py:332
  225.4 140.4 %collective-permute-start.21 = (bf16[2,512,768]{2,1,0:T(8,128)(2,1)S(1)}, bf16[2,512,768]{2,1,0:T(8,128)(2,1)}, u32[]{:S(2)}, u32[]{:S(2)}) collective-permute-start(bf16[2,512,768]{2,1,0:T(8,128)(2,1)S(1)} %copy-done.3), channel_id=1, source_target_pairs={{0,4},{1,5},{2,6},{3,7},{4,0},{5,1},{6,2},{7,3}} | collective-permute-start | bytes 4718600 | tf_op jit(solution)/shard_map/ppermute | solution.py:332
  226.9 171.8 %collective-permute-start.11 = (bf16[2,512,768]{2,1,0:T(8,128)(2,1)S(1)}, bf16[2,512,768]{2,1,0:T(8,128)(2,1)}, u32[]{:S(2)}, u32[]{:S(2)}) collective-permute-start(bf16[2,512,768]{2,1,0:T(8,128)(2,1)S(1)} %copy-done.2), channel_id=1, source_target_pairs={{0,4},{1,5},{2,6},{3,7},{4,0},{5,1},{6,2},{7,3}} | collective-permute-start | bytes 4718600 | tf_op jit(solution)/shard_map/ppermute | solution.py:332
  332.1 82.6 %collective-permute-start.18 = (bf16[1,2,224,512]{3,2,1,0:T(8,128)(2,1)}, bf16[1,2,224,512]{3,2,1,0:T(8,128)(2,1)}, u32[]{:S(2)}, u32[]{:S(2)}) collective-permute-start(bf16[1,2,224,512]{3,2,1,0:T(8,128)(2,1)} %get-tuple-element.90), channel_id=1, source_target_pairs={{0,1},{1,0},{2,3},{3,2},{4,5},{5,4},{6,7},{7,6}} | collective-permute-start | bytes 1376264 | tf_op jit(solution)/shard_map/ppermute | solution.py:332
  365.8 49.3 %collective-permute-start.19 = (bf16[1,2,224,512]{3,2,1,0:T(8,128)(2,1)}, bf16[1,2,224,512]{3,2,1,0:T(8,128)(2,1)S(1)}, u32[]{:S(2)}, u32[]{:S(2)}) collective-permute-start(bf16[1,2,224,512]{3,2,1,0:T(8,128)(2,1)} %get-tuple-element.91), channel_id=1, source_target_pairs={{0,2},{1,3},{2,0},{3,1},{4,6},{5,7},{6,4},{7,5}} | collective-permute-start | bytes 1376264 | tf_op jit(solution)/shard_map/ppermute | solution.py:332
  398.7 17.2 %collective-permute-start.20 = (bf16[1,2,224,512]{3,2,1,0:T(8,128)(2,1)}, bf16[1,2,224,512]{3,2,1,0:T(8,128)(2,1)S(1)}, u32[]{:S(2)}, u32[]{:S(2)}) collective-permute-start(bf16[1,2,224,512]{3,2,1,0:T(8,128)(2,1)} %get-tuple-element.92), channel_id=1, source_target_pairs={{0,3},{1,2},{2,1},{3,0},{4,7},{5,6},{6,5},{7,4}} | collective-permute-start | bytes 1376264 | tf_op jit(solution)/shard_map/ppermute | solution.py:332
  398.7 18.2 %collective-permute-start.28 = (bf16[2,2,224,512]{3,2,1,0:T(8,128)(2,1)}, bf16[2,2,224,512]{3,2,1,0:T(8,128)(2,1)S(1)}, u32[]{:S(2)}, u32[]{:S(2)}) collective-permute-start(bf16[2,2,224,512]{3,2,1,0:T(8,128)(2,1)} %get-tuple-element.98), channel_id=1, source_target_pairs={{0,1},{1,0},{2,3},{3,2},{4,5},{5,4},{6,7},{7,6}} | collective-permute-start | bytes 2752520 | tf_op jit(solution)/shard_map/ppermute | solution.py:332
  413.7 23.3 %collective-permute-start.29 = (bf16[2,2,224,512]{3,2,1,0:T(8,128)(2,1)S(1)}, bf16[2,2,224,512]{3,2,1,0:T(8,128)(2,1)}, u32[]{:S(2)}, u32[]{:S(2)}) collective-permute-start(bf16[2,2,224,512]{3,2,1,0:T(8,128)(2,1)S(1)} %copy-done.14), channel_id=1, source_target_pairs={{0,2},{1,3},{2,0},{3,1},{4,6},{5,7},{6,4},{7,5}} | collective-permute-start | bytes 2752520 | tf_op jit(solution)/shard_map/ppermute | solution.py:332
  414.7 40.5 %collective-permute-start.30 = (bf16[2,2,224,512]{3,2,1,0:T(8,128)(2,1)}, bf16[2,2,224,512]{3,2,1,0:T(8,128)(2,1)}, u32[]{:S(2)}, u32[]{:S(2)}) collective-permute-start(bf16[2,2,224,512]{3,2,1,0:T(8,128)(2,1)} %get-tuple-element.100), channel_id=1, source_target_pairs={{0,3},{1,2},{2,1},{3,0},{4,7},{5,6},{6,5},{7,4}} | collective-permute-start | bytes 2752520 | tf_op jit(solution)/shard_map/ppermute | solution.py:332
  415.1 41.2 %collective-permute-start.23 = (bf16[2,2,224,512]{3,2,1,0:T(8,128)(2,1)}, bf16[2,2,224,512]{3,2,1,0:T(8,128)(2,1)S(1)}, u32[]{:S(2)}, u32[]{:S(2)}) collective-permute-start(bf16[2,2,224,512]{3,2,1,0:T(8,128)(2,1)} %get-tuple-element.94), channel_id=1, source_target_pairs={{0,1},{1,0},{2,3},{3,2},{4,5},{5,4},{6,7},{7,6}} | collective-permute-start | bytes 2752520 | tf_op jit(solution)/shard_map/ppermute | solution.py:332
  415.9 60.5 %collective-permute-start.24 = (bf16[2,2,224,512]{3,2,1,0:T(8,128)(2,1)}, bf16[2,2,224,512]{3,2,1,0:T(8,128)(2,1)}, u32[]{:S(2)}, u32[]{:S(2)}) collective-permute-start(bf16[2,2,224,512]{3,2,1,0:T(8,128)(2,1)} %get-tuple-element.95), channel_id=1, source_target_pairs={{0,2},{1,3},{2,0},{3,1},{4,6},{5,7},{6,4},{7,5}} | collective-permute-start | bytes 2752520 | tf_op jit(solution)/shard_map/ppermute | solution.py:332
  416.9 77.7 %collective-permute-start.25 = (bf16[2,2,224,512]{3,2,1,0:T(8,128)(2,1)}, bf16[2,2,224,512]{3,2,1,0:T(8,128)(2,1)}, u32[]{:S(2)}, u32[]{:S(2)}) collective-permute-start(bf16[2,2,224,512]{3,2,1,0:T(8,128)(2,1)} %get-tuple-element.96), channel_id=1, source_target_pairs={{0,3},{1,2},{2,1},{3,0},{4,7},{5,6},{6,5},{7,4}} | collective-permute-start | bytes 2752520 | tf_op jit(solution)/shard_map/ppermute | solution.py:332
  437.0 235.7 %collective-permute-start.38 = (bf16[2048,512]{1,0:T(8,128)(2,1)}, bf16[2048,512]{1,0:T(8,128)(2,1)S(1)}, u32[]{:S(2)}, u32[]{:S(2)}) collective-permute-start(bf16[2048,512]{1,0:T(8,128)(2,1)} %collective-permute-done.34.ha_ref), channel_id=1, source_target_pairs={{0,2},{1,3},{2,0},{3,1},{4,6},{5,7},{6,4},{7,5}} | collective-permute-start | bytes 6291464 | tf_op jit(solution)/shard_map/ppermute | solution.py:332
  455.2 217.5 %collective-permute-start.40 = (bf16[2048,512]{1,0:T(8,128)(2,1)}, bf16[2048,512]{1,0:T(8,128)(2,1)}, u32[]{:S(2)}, u32[]{:S(2)}) collective-permute-start(bf16[2048,512]{1,0:T(8,128)(2,1)} %collective-permute-done.36.da_ref), channel_id=1, source_target_pairs={{0,2},{1,3},{2,0},{3,1},{4,6},{5,7},{6,4},{7,5}} | collective-permute-start | bytes 6291464 | tf_op jit(solution)/shard_map/ppermute | solution.py:332
  456.2 48.6 %copy-start.15 = (bf16[2,2,224,512]{3,2,1,0:T(8,128)(2,1)}, bf16[2,2,224,512]{3,2,1,0:T(8,128)(2,1)S(1)}, u32[]{:S(2)}) copy-start(bf16[2,2,224,512]{3,2,1,0:T(8,128)(2,1)S(1)} %collective-permute-done.23.refs_1_) | copy-start | bytes 2752516
  456.2 62.7 %collective-permute-start.13 = (bf16[2,2,224,512]{3,2,1,0:T(8,128)(2,1)}, bf16[2,2,224,512]{3,2,1,0:T(8,128)(2,1)}, u32[]{:S(2)}, u32[]{:S(2)}) collective-permute-start(bf16[2,2,224,512]{3,2,1,0:T(8,128)(2,1)} %get-tuple-element.86), channel_id=1, source_target_pairs={{0,1},{1,0},{2,3},{3,2},{4,5},{5,4},{6,7},{7,6}} | collective-permute-start | bytes 2752520 | tf_op jit(solution)/shard_map/ppermute | solution.py:332
  476.4 129.2 %collective-permute-start.14 = (bf16[2,2,224,512]{3,2,1,0:T(8,128)(2,1)}, bf16[2,2,224,512]{3,2,1,0:T(8,128)(2,1)}, u32[]{:S(2)}, u32[]{:S(2)}) collective-permute-start(bf16[2,2,224,512]{3,2,1,0:T(8,128)(2,1)} %get-tuple-element.87), channel_id=1, source_target_pairs={{0,2},{1,3},{2,0},{3,1},{4,6},{5,7},{6,4},{7,5}} | collective-permute-start | bytes 2752520 | tf_op jit(solution)/shard_map/ppermute | solution.py:332
  494.5 129.2 %collective-permute-start.15 = (bf16[2,2,224,512]{3,2,1,0:T(8,128)(2,1)}, bf16[2,2,224,512]{3,2,1,0:T(8,128)(2,1)}, u32[]{:S(2)}, u32[]{:S(2)}) collective-permute-start(bf16[2,2,224,512]{3,2,1,0:T(8,128)(2,1)} %get-tuple-element.88), channel_id=1, source_target_pairs={{0,3},{1,2},{2,1},{3,0},{4,7},{5,6},{6,5},{7,4}} | collective-permute-start | bytes 2752520 | tf_op jit(solution)/shard_map/ppermute | solution.py:332
  504.8 118.9 %copy-start.18 = (bf16[1,2,224,512]{3,2,1,0:T(8,128)(2,1)S(1)}, bf16[1,2,224,512]{3,2,1,0:T(8,128)(2,1)}, u32[]{:S(2)}) copy-start(bf16[1,2,224,512]{3,2,1,0:T(8,128)(2,1)} %get-tuple-element.84) | copy-start | bytes 1376260
  518.9 121.6 %collective-permute-start.8 = (bf16[1,2,224,512]{3,2,1,0:T(8,128)(2,1)}, bf16[1,2,224,512]{3,2,1,0:T(8,128)(2,1)S(1)}, u32[]{:S(2)}, u32[]{:S(2)}) collective-permute-start(bf16[1,2,224,512]{3,2,1,0:T(8,128)(2,1)} %get-tuple-element.82), channel_id=1, source_target_pairs={{0,1},{1,0},{2,3},{3,2},{4,5},{5,4},{6,7},{7,6}} | collective-permute-start | bytes 1376264 | tf_op jit(solution)/shard_map/ppermute | solution.py:332
  605.6 35.0 %collective-permute-start.9 = (bf16[1,2,224,512]{3,2,1,0:T(8,128)(2,1)}, bf16[1,2,224,512]{3,2,1,0:T(8,128)(2,1)S(1)}, u32[]{:S(2)}, u32[]{:S(2)}) collective-permute-start(bf16[1,2,224,512]{3,2,1,0:T(8,128)(2,1)} %get-tuple-element.83), channel_id=1, source_target_pairs={{0,2},{1,3},{2,0},{3,1},{4,6},{5,7},{6,4},{7,5}} | collective-permute-start | bytes 1376264 | tf_op jit(solution)/shard_map/ppermute | solution.py:332
  623.8 19.1 %collective-permute-start.10 = (bf16[1,2,224,512]{3,2,1,0:T(8,128)(2,1)S(1)}, bf16[1,2,224,512]{3,2,1,0:T(8,128)(2,1)S(1)}, u32[]{:S(2)}, u32[]{:S(2)}) collective-permute-start(bf16[1,2,224,512]{3,2,1,0:T(8,128)(2,1)S(1)} %copy-done.18), channel_id=1, source_target_pairs={{0,3},{1,2},{2,1},{3,0},{4,7},{5,6},{6,5},{7,4}} | collective-permute-start | bytes 1376264 | tf_op jit(solution)/shard_map/ppermute | solution.py:332
  670.2 3.0 collective-permute-start.31
  672.2 30.4 %collective-permute-start.35 = (bf16[2048,512]{1,0:T(8,128)(2,1)}, bf16[2048,512]{1,0:T(8,128)(2,1)}, u32[]{:S(2)}, u32[]{:S(2)}) collective-permute-start(bf16[2048,512]{1,0:T(8,128)(2,1)} %collective-permute-done.34.ha_ref), channel_id=1, source_target_pairs={{0,1},{1,0},{2,3},{3,2},{4,5},{5,4},{6,7},{7,6}} | collective-permute-start | bytes 6291464 | tf_op jit(solution)/shard_map/ppermute | solution.py:332
  672.2 30.4 %collective-permute-start.37 = (bf16[2048,512]{1,0:T(8,128)(2,1)}, bf16[2048,512]{1,0:T(8,128)(2,1)}, u32[]{:S(2)}, u32[]{:S(2)}) collective-permute-start(bf16[2048,512]{1,0:T(8,128)(2,1)} %collective-permute-done.36.da_ref), channel_id=1, source_target_pairs={{0,1},{1,0},{2,3},{3,2},{4,5},{5,4},{6,7},{7,6}} | collective-permute-start | bytes 6291464 | tf_op jit(solution)/shard_map/ppermute | solution.py:332
  672.7 48.6 %collective-permute-start.39 = (bf16[2048,512]{1,0:T(8,128)(2,1)S(1)}, bf16[2048,512]{1,0:T(8,128)(2,1)}, u32[]{:S(2)}, u32[]{:S(2)}) collective-permute-start(bf16[2048,512]{1,0:T(8,128)(2,1)S(1)} %collective-permute-done.38.ha_ref), channel_id=1, source_target_pairs={{0,1},{1,0},{2,3},{3,2},{4,5},{5,4},{6,7},{7,6}} | collective-permute-start | bytes 6291464 | tf_op jit(solution)/shard_map/ppermute | solution.py:332
  672.7 48.5 %collective-permute-start.41 = (bf16[2048,512]{1,0:T(8,128)(2,1)}, bf16[2048,512]{1,0:T(8,128)(2,1)}, u32[]{:S(2)}, u32[]{:S(2)}) collective-permute-start(bf16[2048,512]{1,0:T(8,128)(2,1)} %collective-permute-done.40.da_ref), channel_id=1, source_target_pairs={{0,1},{1,0},{2,3},{3,2},{4,5},{5,4},{6,7},{7,6}} | collective-permute-start | bytes 6291464 | tf_op jit(solution)/shard_map/ppermute | solution.py:332
  674.3 27.3 %collective-permute-start.32 = (f32[40,512]{1,0:T(8,128)S(1)}, f32[40,512]{1,0:T(8,128)S(1)}, u32[]{:S(2)}, u32[]{:S(2)}) collective-permute-start(f32[40,512]{1,0:T(8,128)S(1)} %add.37), channel_id=1, source_target_pairs={{0,2},{1,3},{2,0},{3,1},{4,6},{5,7},{6,4},{7,5}} | collective-permute-start | bytes 245768 | tf_op jit(solution)/shard_map/ppermute | solution.py:332
  701.6 17.7 %collective-permute-start.33 = (f32[40,512]{1,0:T(8,128)S(1)}, f32[40,512]{1,0:T(8,128)S(1)}, u32[]{:S(2)}, u32[]{:S(2)}) collective-permute-start(f32[40,512]{1,0:T(8,128)S(1)} %add.38), channel_id=1, source_target_pairs={{0,4},{1,5},{2,6},{3,7},{4,0},{5,1},{6,2},{7,3}} | collective-permute-start | bytes 245768 | tf_op jit(solution)/shard_map/ppermute | solution.py:332
  (13 other events, 129.8 us)
where the time goes:
time: 777 us; the launch traced here: 767 us
  waiting for transfers between devices  428 us (55%)
  Pallas kernels  261 us (34%)
  starting transfers between devices  35.1 us (5%)
  local copies, waits for them, and re-layouts  20.3 us (3%)
  blocking collectives  13.9 us (2%)
    ppermute x42, waiting for transfers between devices, permute(): return lax.ppermute(v, ('etp', 'ep'), pairs)  428 us
    pallas_call x4, Pallas kernels, gather(): kernel(functools.partial(gather_kernel, slots, n_local, n_experts), grid=...  66.8 us
    pallas_call x5, Pallas kernels, back(): kernel(functools.partial(row_kernel, slots), grid=(hi - lo,), in_specs=[a...  58.8 us
    pallas_call x2, Pallas kernels, grads(): kernel(functools.partial(grad_kernel, bool(acc)), grid=(n_local,), in_spe...  54.4 us
    pallas_call x3, Pallas kernels, combine(): kernel(functools.partial(combine_kernel, groups, bool(acc), slots, n_loca...  40.4 us
    ppermute x42, starting transfers between devices, permute(): return lax.ppermute(v, ('etp', 'ep'), pairs)  35.1 us
    pallas_call x1, Pallas kernels, layer(): kernel(functools.partial(slot_kernel, capacity, slots, n_local), grid=(n_...  16.5 us
  transfers between devices with their start and end apart: 42, of which 16 were waited for; matrix products, arithmetic and copies ran while one was open for 2% of the time, Pallas kernels for 28%

commit v1 on v0

--- a/solution.py
+++ b/solution.py
@@ -46,7 +46,7 @@
     return pl.CostEstimate(flops=int(flops), bytes_accessed=1 << 20, transcendentals=0)
 
 
-def route_kernel(n_experts, h_ref, wr_ref, ids_ref, p_ref, code_ref, win_ref, stat_ref):
+def route_kernel(n_experts, n_local, info_ref, h_ref, wr_ref, ids_ref, p_ref, code_ref, win_ref, stat_ref):
     step = pl.program_id(0)
 
     @pl.when(step == 0)
@@ -77,11 +77,16 @@
     wide = iota((TILE, 128), 1)
     code = jnp.zeros((TILE, 128), f32)
     rel = rank - start
-    for k, v in enumerate((e0.astype(f32), e1.astype(f32), pick(m0, rel), pick(m1, rel), p0 / s, p1 / s, s)):
+    name = iota((1, n_experts), 1)
+    base = ((((name // n_local) ^ info_ref[0]) * n_local + name % n_local) * WIN).astype(f32)
+    at = jnp.where(rel < WIN, base + rel, -1.0)
+    spread = jnp.zeros_like(rel) + base
+    for k, v in enumerate((e0.astype(f32), e1.astype(f32), pick(m0, at), pick(m1, at), p0 / s, p1 / s, s,
+                           pick(m0, spread), pick(m1, spread), pick(m0, rel), pick(m1, rel))):
         code = jnp.where(wide == k, v, code)
     code_ref[...] = code
     win_ref[pl.ds(step, 1), 0:n_experts] = start.astype(jnp.int32)
-    win_ref[pl.ds(step, 1), n_experts:n_experts + 1] = n_win.astype(jnp.int32)
+    win_ref[pl.ds(step, 1), 127:128] = n_win.astype(jnp.int32)
     stat_ref[0:1, 0:n_experts] = after
     stat_ref[1:2, 0:n_experts] = stat_ref[1:2, 0:n_experts] + jnp.sum(p, axis=0, keepdims=True)
 
@@ -96,7 +101,8 @@
             wr3_ref[:, k * width:(k + 1) * width] = piece
 
     steps = ids_ref.shape[1] // 2
-    expert = iota((n_local, TILE), 0) + info_ref[0]
+    near = info_ref[pl.program_id(0)]
+    expert = iota((n_local, TILE), 0) + info_ref[info_ref.shape[0] - 1]
     before = (iota((TILE, TILE), 0) < iota((TILE, TILE), 1)).astype(f32).astype(bf16)
     row = iota((TILE, TILE), 0).astype(f32)
     lane = iota((n_local, 128), 1)
@@ -104,7 +110,7 @@
     starts = jnp.zeros((n_local, 128), f32)
     other = jnp.zeros((n_local, TILE), f32)
     for i in range(steps):
-        e0, e1 = ids_ref[0, 2 * i:2 * i + 1, :], ids_ref[0, 2 * i + 1:2 * i + 2, :]
+        e0, e1 = ids_ref[near, 2 * i:2 * i + 1, :], ids_ref[near, 2 * i + 1:2 * i + 2, :]
         m0, m1 = expert == e0, expert == e1
         hit = jnp.where(m0 | m1, 1.0, 0.0).astype(f32)
         rank = nn(hit.astype(bf16), before) + carry
@@ -216,87 +222,132 @@
             y, dx = (py, pdx) if y is None else (y + py, dx + pdx)
         y, dx = y.astype(bf16), dx.astype(bf16)
         for b in range(2):
-            r_refs[2 * q + b][0, 0] = y[b * slots:(b + 1) * slots]
-            r_refs[2 * q + b][0, 1] = dx[b * slots:(b + 1) * slots]
-
-
-def combine_kernel(groups, accumulate, slots, n_local, info_ref, win_ref, code_ref, *refs):
+            if len(r_refs) == 8:
+                r_refs[2 * q + b][0] = y[b * slots:(b + 1) * slots]
+                r_refs[4 + 2 * q + b][0] = dx[b * slots:(b + 1) * slots]
+            else:
+                r_refs[2 * q + b][0, 0] = y[b * slots:(b + 1) * slots]
+                r_refs[2 * q + b][0, 1] = dx[b * slots:(b + 1) * slots]
+
+
+def names_of(groups, r_refs, part):
+    names = []
+    for gi, (lo, hi) in enumerate(groups):
+        for q in range(4):
+            ref = r_refs[4 * gi + q]
+            for el in range(hi - lo):
+                if len(ref.shape) == 4:
+                    names.append((q, lo + el, lambda at, ref=ref, el=el: ref[el, part, pl.ds(at, 16), :]))
+                else:
+                    names.append((q, lo + el, lambda at, ref=ref, el=el: ref[el, pl.ds(at, 16), :]))
+    return names
+
+
+def fetch(names, w, slots, n_local, info_ref, win_ref, dst_ref):
+    step = pl.program_id(0)
+    for i, (q, el, read) in enumerate(names):
+        first = win_ref[step, info_ref[q] * n_local + el]
+        for piece in range(0, WIN, 16):
+            at = pl.multiple_of(jnp.minimum(first + w * WIN + piece, slots - 16), 16)
+            dst_ref[i * WIN + piece:i * WIN + piece + 16, :] = read(at)
+
+
+def column(groups, n_local):
+    width = 4 * sum(hi - lo for lo, hi in groups) * WIN
+    lane = iota((1, width), 1)
+    out, done = jnp.zeros((1, width), jnp.int32), 0
+    for lo, hi in groups:
+        for q in range(4):
+            size = (hi - lo) * WIN
+            out = jnp.where((lane >= done) & (lane < done + size), lane - done + (q * n_local + lo) * WIN, out)
+            done += size
+    return out.astype(f32)
+
+
+def masks(code, w, col):
+    if isinstance(w, int):
+        return [jnp.where(col == code[:, 2 + k:3 + k], 1.0, 0.0) for k in range(2)]
+    low = (w * WIN).astype(f32)
+    out = []
+    for k in range(2):
+        rel = code[:, 9 + k:10 + k]
+        at = jnp.where((rel >= low) & (rel < low + WIN), code[:, 7 + k:8 + k] + rel - low, -1.0)
+        out.append(jnp.where(col == at, 1.0, 0.0))
+    return out
+
+
+def collect_y(code, w, col, rows_ref):
+    return nn(jnp.concatenate(masks(code, w, col), axis=0).astype(bf16), rows_ref[...])
+
+
+def collect_dx(code, w, col, rows_ref):
+    m0, m1 = masks(code, w, col)
+    return nn((m0 + m1).astype(bf16), rows_ref[...])
+
+
+def further(win_ref, body):
+    n_win = win_ref[pl.program_id(0), win_ref.shape[1] - 1]
+
+    @pl.when(n_win > 1)
+    def _():
+        def run(w, carry):
+            body(w)
+            return carry
+
+        lax.fori_loop(1, n_win, run, 0)
+
+
+def combine_kernel(groups, slots, n_local, info_ref, win_ref, code_ref, *refs):
     n_r = 4 * len(groups)
-    r_refs, rest = refs[:n_r], refs[n_r:-2]
-    y0_ref, y1_ref, dx_ref = rest[-3:]
-    yc_ref, xc_ref = refs[-2:]
-    step = pl.program_id(0)
+    y0_ref, y1_ref, dx_ref, rows_ref = refs[n_r:]
     code = code_ref[...]
     rows = code.shape[0]
-    n_experts = 4 * n_local
-    names = [(q, lo + el, r_refs[4 * gi + q], el) for gi, (lo, hi) in enumerate(groups) for q in range(4) for el in range(hi - lo)]
-    width = len(names) * WIN
-    lane = iota((rows, width), 1)
-    place = []
-    for k in range(2):
-        e = code[:, k:k + 1].astype(jnp.int32)
-        q, el = (e // n_local) ^ info_ref[0], e % n_local
-        index = jnp.full(e.shape, -(1 << 20), jnp.int32)
-        done = 0
-        for lo, hi in groups:
-            index = jnp.where((el >= lo) & (el < hi), done + q * (hi - lo) + (el - lo), index)
-            done += 4 * (hi - lo)
-        place.append(index * WIN)
-    rel = [code[:, k:k + 1].astype(jnp.int32) for k in (2, 3)]
-
-    def window(w, acc):
-        y, dx = acc
-        for i, (q, el_abs, r_ref, el) in enumerate(names):
-            first = win_ref[step, info_ref[q] * n_local + el_abs]
-            for piece in range(0, WIN, 16):
-                at = pl.multiple_of(jnp.minimum(first + w * WIN + piece, slots - 16), 16)
-                yc_ref[i * WIN + piece:i * WIN + piece + 16, :] = r_ref[el, 0, pl.ds(at, 16), :]
-                xc_ref[i * WIN + piece:i * WIN + piece + 16, :] = r_ref[el, 1, pl.ds(at, 16), :]
-        ms = []
-        for k in range(2):
-            inside = (rel[k] >= w * WIN) & (rel[k] < w * WIN + WIN)
-            at = jnp.where(inside, place[k] + rel[k] - w * WIN, -1)
-            ms.append(jnp.where(lane == at, 1.0, 0.0))
-        m0, m1 = ms
-        y = y + nn(jnp.concatenate([m0, m1], axis=0).astype(bf16), yc_ref[...])
-        dx = dx + nn((m0 + m1).astype(bf16), xc_ref[...])
-        return y, dx
-
-    d_model = y0_ref.shape[1]
-    y, dx = window(0, (jnp.zeros((2 * rows, d_model), f32), jnp.zeros((rows, d_model), f32)))
-    if accumulate:
-        y0_ref[...] = (rest[0][...].astype(f32) + y[:rows]).astype(bf16)
-        y1_ref[...] = (rest[1][...].astype(f32) + y[rows:]).astype(bf16)
-        dx_ref[...] = rest[2][...] + dx
-    else:
-        y0_ref[...] = y[:rows].astype(bf16)
-        y1_ref[...] = y[rows:].astype(bf16)
-        dx_ref[...] = dx
-    n_win = win_ref[step, n_experts]
-
-    @pl.when(n_win > 1)
-    def _():
-        def more(w, carry):
-            y, dx = window(w, (jnp.zeros((2 * rows, d_model), f32), jnp.zeros((rows, d_model), f32)))
-            y0_ref[...] = (y0_ref[...].astype(f32) + y[:rows]).astype(bf16)
-            y1_ref[...] = (y1_ref[...].astype(f32) + y[rows:]).astype(bf16)
-            dx_ref[...] = dx_ref[...] + dx
-            return carry
-
-        lax.fori_loop(1, n_win, more, 0)
-
-
-def final_kernel(h_ref, d_ref, y0_ref, y1_ref, dx_ref, code_ref, p_ref, coef_ref, wr_ref, stat_ref,
-                 out_ref, dh_ref, dr_ref):
-    n_experts = p_ref.shape[1]
+    col = column(groups, n_local)
+
+    def collect(w):
+        fetch(names_of(groups, refs[:n_r], 0), w, slots, n_local, info_ref, win_ref, rows_ref.at[0])
+        fetch(names_of(groups, refs[:n_r], 1), w, slots, n_local, info_ref, win_ref, rows_ref.at[1])
+        return collect_y(code, w, col, rows_ref.at[0]), collect_dx(code, w, col, rows_ref.at[1])
+
+    y, dx = collect(0)
+    y0_ref[...] = y[:rows].astype(bf16)
+    y1_ref[...] = y[rows:].astype(bf16)
+    dx_ref[...] = dx
+
+    def more(w):
+        y, dx = collect(w)
+        y0_ref[...] = (y0_ref[...].astype(f32) + y[:rows]).astype(bf16)
+        y1_ref[...] = (y1_ref[...].astype(f32) + y[rows:]).astype(bf16)
+        dx_ref[...] = dx_ref[...] + dx
+
+    further(win_ref, more)
+
+
+def final_y_kernel(groups, slots, n_local, info_ref, win_ref, code_ref, *refs):
+    n_r = 4 * len(groups)
+    y0_ref, y1_ref, h_ref, d_ref, p_ref, coef_ref, stat_ref, out_ref, dz_ref, dr_ref, rows_ref, y_ref = refs[n_r:]
     code, p = code_ref[...], p_ref[...]
+    n_experts = p.shape[1]
+    rows = code.shape[0]
+    col = column(groups, n_local)
+
+    def collect(w):
+        fetch(names_of(groups, refs[:n_r], 0), w, slots, n_local, info_ref, win_ref, rows_ref)
+        return collect_y(code, w, col, rows_ref)
+
+    y_ref[...] = collect(0)
+
+    def more(w):
+        y_ref[...] = y_ref[...] + collect(w)
+
+    further(win_ref, more)
+    y0 = y0_ref[...].astype(f32) + y_ref[:rows, :]
+    y1 = y1_ref[...].astype(f32) + y_ref[rows:, :]
     e0, e1 = code[:, 0:1].astype(jnp.int32), code[:, 1:2].astype(jnp.int32)
     g0, g1, s = code[:, 4:5], code[:, 5:6], code[:, 6:7]
     h = h_ref[...]
-    d = d_ref[...].astype(f32)
-    y0, y1 = y0_ref[...].astype(f32), y1_ref[...].astype(f32)
+    m = OUT_SCALE * d_ref[...].astype(f32)
     out_ref[...] = (h.astype(f32) + OUT_SCALE * (g0 * y0 + g1 * y1)).astype(bf16)
-    m = OUT_SCALE * d
     dg0 = jnp.sum(m * y0, axis=1, keepdims=True)
     dg1 = jnp.sum(m * y1, axis=1, keepdims=True)
     mean = g0 * dg0 + g1 * dg1
@@ -304,10 +355,8 @@
     dp = (jnp.where(lane == e0, (dg0 - mean) / s, 0.0) + jnp.where(lane == e1, (dg1 - mean) / s, 0.0)
           + coef_ref[...])
     dz = p * (dp - jnp.sum(p * dp, axis=1, keepdims=True))
+    dz_ref[...] = dz
     z3 = split3(dz)
-    w_hi, w_lo, _ = split3(wr_ref[...])
-    back = nt(z3[0], w_hi) + (nt(z3[1], w_hi) + nt(z3[0], w_lo))
-    dh_ref[...] = (d + dx_ref[...] + back).astype(bf16)
     part = tn(z3[0], h) + (tn(z3[1], h) + tn(z3[2], h))
 
     @pl.when(pl.program_id(0) == 0)
@@ -316,6 +365,32 @@
         dr_ref[n_experts:n_experts + 1, 0:128] = stat_ref[1:2, :]
 
     dr_ref[0:n_experts, :] = dr_ref[0:n_experts, :] + part
+
+
+def final_x_kernel(groups, slots, n_local, info_ref, win_ref, code_ref, *refs):
+    n_r = 4 * len(groups)
+    dx_ref, d_ref, dz_ref, wr_ref, dh_ref, rows_ref, x_ref, wt_ref = refs[n_r:]
+    code = code_ref[...]
+    col = column(groups, n_local)
+
+    @pl.when(pl.program_id(0) == 0)
+    def _():
+        wt_ref[...] = wr_ref[...].T
+
+    def collect(w):
+        fetch(names_of(groups, refs[:n_r], 1), w, slots, n_local, info_ref, win_ref, rows_ref)
+        return collect_dx(code, w, col, rows_ref)
+
+    x_ref[...] = dx_ref[...] + collect(0)
+
+    def more(w):
+        x_ref[...] = x_ref[...] + collect(w)
+
+    further(win_ref, more)
+    z_hi, z_lo, _ = split3(dz_ref[...])
+    w_hi, w_lo, _ = split3(wt_ref[...])
+    back = nn(z_hi, w_hi) + (nn(z_lo, w_hi) + nn(z_hi, w_lo))
+    dh_ref[...] = (d_ref[...].astype(f32) + x_ref[...] + back).astype(bf16)
 
 
 def solution(mesh):
@@ -343,6 +418,7 @@
         slots = 7 * tok_rows // (2 * n_experts)
         ep, etp = lax.axis_index("ep"), lax.axis_index("etp")
         steps = tok_rows // TILE
+        ep_info = jnp.stack([ep ^ q for q in range(4)]).astype(jnp.int32)
         sds = jax.ShapeDtypeStruct
         smem = pl.BlockSpec(memory_space=pltpu.SMEM)
 
@@ -356,38 +432,40 @@
             return pl.BlockSpec((1,) + shape, lambda i: (i + lo,) + (0,) * len(shape))
 
         tile_ids = expert_ids.reshape(steps, TILE, 2).transpose(0, 2, 1).reshape(2 * steps, TILE)
-        all_ids = lax.all_gather(tile_ids, all_axes)
+        near_ids = [tile_ids] + [permute(tile_ids, r // etp_size, r % etp_size) for r in range(1, n_dev)]
+        near_ids = jnp.stack(near_ids)
+        rank = ep * etp_size + etp
+        rank_info = jnp.concatenate([jnp.arange(n_dev, dtype=jnp.int32) ^ rank, (ep * n_local)[None]]).astype(jnp.int32)
         w13 = jnp.concatenate([w_gate, w_up], axis=2)
-        h_send, d_send, w13_send, w2_send, all_ids = lax.optimization_barrier((hidden, d_out, w13, w_down, all_ids))
-
-        hx, hy = permute(h_send, 2, 0), permute(h_send, 0, 1)
-        dx_, dy_ = permute(d_send, 2, 0), permute(d_send, 0, 1)
+
+        hx, hy = permute(hidden, 2, 0), permute(hidden, 0, 1)
+        dx_, dy_ = permute(d_out, 2, 0), permute(d_out, 0, 1)
         hd, dd = permute(hy, 2, 0), permute(dy_, 2, 0)
         core = lambda v: permute(v, 1, 0)
-        h_pairs = {(0, 0): (hidden, core(h_send)), (1, 0): (hx, core(hx)), (0, 1): (hy, core(hy)), (1, 1): (hd, core(hd))}
-        d_pairs = {(0, 0): (d_out, core(d_send)), (1, 0): (dx_, core(dx_)), (0, 1): (dy_, core(dy_)), (1, 1): (dd, core(dd))}
-        partner = [(permute(w13_send[lo:hi], 0, 1), permute(w2_send[lo:hi], 0, 1)) for lo, hi in CHUNKS]
+        h_pairs = {(0, 0): (hidden, core(hidden)), (1, 0): (hx, core(hx)), (0, 1): (hy, core(hy)), (1, 1): (hd, core(hd))}
+        d_pairs = {(0, 0): (d_out, core(d_out)), (1, 0): (dx_, core(dx_)), (0, 1): (dy_, core(dy_)), (1, 1): (dd, core(dd))}
+        partner = [(permute(w13[lo:hi], 0, 1), permute(w_down[lo:hi], 0, 1)) for lo, hi in CHUNKS]
 
         per_block = lambda *shape: pl.BlockSpec((1,) + shape, lambda i: (i,) + (0,) * len(shape))
         slot_rows, others, starts, wr3 = kernel(
             functools.partial(slot_kernel, capacity, slots, n_local),
             grid=(n_dev,),
-            in_specs=[smem, per_block(2 * steps, TILE), whole((d_model, n_experts))],
+            in_specs=[smem, whole(near_ids.shape), whole((d_model, n_experts))],
             out_specs=[per_block(steps * n_local, TILE), per_block(n_local, TILE), per_block(n_local, 128), whole((d_model, 128))],
             out_shape=[sds((n_dev, steps * n_local, TILE), f32), sds((n_dev, n_local, TILE), f32),
                        sds((n_dev, n_local, 128), jnp.int32), sds((d_model, 128), bf16)],
             scratch_shapes=[pltpu.VMEM((n_local, 128), f32)],
             compiler_params=params(), cost_estimate=cost(5e9),
-        )((ep * n_local).astype(jnp.int32)[None], all_ids, w_router)
+        )(rank_info, near_ids, w_router)
 
         probs, code, wins, stats = kernel(
-            functools.partial(route_kernel, n_experts),
+            functools.partial(route_kernel, n_experts, n_local),
             grid=(steps,),
-            in_specs=[tokens(d_model), whole((d_model, n_experts)), tokens(2)],
+            in_specs=[smem, tokens(d_model), whole((d_model, n_experts)), tokens(2)],
             out_specs=[tokens(n_experts), tokens(128), whole((8, 128)), whole((8, 128))],
             out_shape=[sds((tok_rows, n_experts), f32), sds((tok_rows, 128), f32), sds((8, 128), jnp.int32), sds((8, 128), f32)],
             compiler_params=params(), cost_estimate=cost(3e9),
-        )(hidden, w_router, expert_ids)
+        )(ep_info, hidden, w_router, expert_ids)
 
         def gather(pair):
             x, t = pair
@@ -433,45 +511,46 @@
                 grid=(hi - lo,),
                 in_specs=[at((2 * slots, d_model))] * 4 + [at((d_model, 2 * ff)), at((ff, d_model)),
                           expert_block((d_model, 2 * ff)), expert_block((ff, d_model))],
-                out_specs=[expert_block((2, slots, d_model))] * 4,
-                out_shape=[sds((hi - lo, 2, slots, d_model), bf16)] * 4,
+                out_specs=[expert_block((slots, d_model))] * 8 if index == last else [expert_block((2, slots, d_model))] * 4,
+                out_shape=[sds((hi - lo, slots, d_model), bf16)] * 8 if index == last else [sds((hi - lo, 2, slots, d_model), bf16)] * 4,
                 compiler_params=params(), cost_estimate=cost(6e9 * (hi - lo)),
             )(xa, xb, ca, cb, w13, w_down, *partner[index])
-            return [outs[0]] + [permute(outs[q], q, 0) for q in (1, 2, 3)]
-
+            return [outs[i] if i % 4 == 0 else permute(outs[i], i % 4, 0) for i in range(len(outs))]
+
+        last = len(CHUNKS) - 1
         returned = [back(i) for i in range(len(CHUNKS))]
-        total = jnp.sum((all_ids.reshape(-1)[:, None] == jnp.arange(n_experts)[None, :]).astype(f32), axis=0)[None, :]
+        total = jnp.sum((near_ids.reshape(-1)[:, None] == jnp.arange(n_experts)[None, :]).astype(f32), axis=0)[None, :]
         coef = (AUX_COEF * n_experts / n_tokens / (2 * n_tokens)) * total
-        ep_info = jnp.stack([ep ^ q for q in range(4)]).astype(jnp.int32)
-
-        def combine(chunk_ids, acc):
+
+        def token_kernel(body, chunk_ids, arrays, extra, extra_specs, out_specs, out_shape, scratch):
             groups = tuple(CHUNKS[i] for i in chunk_ids)
-            arrays = [r for i in chunk_ids for r in returned[i]]
-            acc_specs = [tokens(d_model)] * 3
-            width = 4 * sum(hi - lo for lo, hi in groups) * WIN
             return kernel(
-                functools.partial(combine_kernel, groups, bool(acc), slots, n_local),
+                functools.partial(body, groups, slots, n_local),
                 grid=(steps,),
-                in_specs=[smem, smem, tokens(128)] + [whole(r.shape) for r in arrays] + acc_specs[:len(acc)],
-                out_specs=acc_specs,
-                out_shape=[sds((tok_rows, d_model), bf16)] * 2 + [sds((tok_rows, d_model), f32)],
-                scratch_shapes=[pltpu.VMEM((width, d_model), bf16)] * 2,
-                compiler_params=params(), cost_estimate=cost(3e9 * len(chunk_ids)),
-            )(ep_info, wins, code, *arrays, *acc)
-
-        acc = combine((0, 1), ())
-        acc = combine((2, 3), tuple(acc))
-        y0, y1, dxs = combine((4,), tuple(acc))
-
-        output, d_hidden, d_rt = kernel(
-            final_kernel,
-            grid=(steps,),
-            in_specs=[tokens(d_model)] * 5 + [tokens(128), tokens(n_experts), whole((1, n_experts)), whole((d_model, n_experts)),
-                      whole((8, 128))],
-            out_specs=[tokens(d_model)] * 2 + [whole((n_experts + 8, d_model))],
-            out_shape=[sds((tok_rows, d_model), bf16)] * 2 + [sds((n_experts + 8, d_model), f32)],
-            compiler_params=params(), cost_estimate=cost(4e9),
-        )(hidden, d_out, y0, y1, dxs, code, probs, coef, w_router, stats)
+                in_specs=[smem, smem, tokens(128)] + [whole(r.shape) for r in arrays] + extra_specs,
+                out_specs=out_specs, out_shape=out_shape, scratch_shapes=scratch,
+                compiler_params=params(), cost_estimate=cost(8e9),
+            )(ep_info, wins, code, *arrays, *extra)
+
+        wide = tokens(d_model)
+        width = lambda ids: 4 * sum(CHUNKS[i][1] - CHUNKS[i][0] for i in ids) * WIN
+        early, late = (0, 1), (2, 3, last)
+        y0, y1, dxs = token_kernel(
+            combine_kernel, early, [r for i in early for r in returned[i]], (), [],
+            [wide] * 3, [sds((tok_rows, d_model), bf16)] * 2 + [sds((tok_rows, d_model), f32)],
+            [pltpu.VMEM((2, width(early), d_model), bf16)])
+        ready = [r for i in late[:-1] for r in returned[i]]
+        output, dz, d_rt = token_kernel(
+            final_y_kernel, late, ready + returned[last][:4], (y0, y1, hidden, d_out, probs, coef, stats),
+            [wide] * 4 + [tokens(n_experts), whole((1, n_experts)), whole((8, 128))],
+            [wide, tokens(n_experts), whole((n_experts + 8, d_model))],
+            [sds((tok_rows, d_model), bf16), sds((tok_rows, n_experts), f32), sds((n_experts + 8, d_model), f32)],
+            [pltpu.VMEM((width(late), d_model), bf16), pltpu.VMEM((2 * TILE, d_model), f32)])
+        (d_hidden,) = token_kernel(
+            final_x_kernel, late, ready + returned[last][4:], (dxs, d_out, dz, w_router),
+            [wide] * 2 + [tokens(n_experts), whole((d_model, n_experts))],
+            [wide], [sds((tok_rows, d_model), bf16)],
+            [pltpu.VMEM((width(late), d_model), bf16), pltpu.VMEM((TILE, d_model), f32), pltpu.VMEM((n_experts, d_model), f32)])
         for dep, detp in ((1, 0), (2, 0), (0, 1)):
             d_rt = d_rt + permute(d_rt, dep, detp)
         d_router = d_rt[:n_experts].T

time: 777 us -> 768 us (0.988)
  blocking collectives: 13.9 us -> 0 us
  starting transfers between devices: 35.1 us -> 46.4 us
  Pallas kernels: 261 us -> 250 us
    all_gather x1 -> x0, blocking collectives: 13.9 us -> none  [layer(): all_ids = lax.all_gather(tile_ids, all_axes)]
    ppermute x42 -> x52, starting transfers between devices: 35.1 us -> 46.4 us  [permute(): return lax.ppermute(v, ('etp', 'ep'), pairs)]
    pallas_call x5 -> x4, Pallas kernels: 64.1 us -> 53.2 us  [the longest x3 42.2 us: token_kernel(): kernel(functools.partial(body, groups, slots, n_local), grid=(steps,), in...]
    ppermute x42 -> x52, waiting for transfers between devices: 428 us -> 430 us  [permute(): return lax.ppermute(v, ('etp', 'ep'), pairs)]
  transfers between devices with their start and end apart: 42 -> 52, of which waited for: 16 -> 18; matrix products, arithmetic and copies ran while one was open for 2% -> 4% of each run, Pallas kernels for 28% -> 27%
where the time goes in v1:
time: 768 us; the launch traced here: 760 us
  waiting for transfers between devices  430 us (56%)
  Pallas kernels  250 us (33%)
  starting transfers between devices  46.4 us (6%)
  local copies, waits for them, and re-layouts  24.7 us (3%)
    ppermute x52, waiting for transfers between devices, permute(): return lax.ppermute(v, ('etp', 'ep'), pairs)  430 us
    pallas_call x4, Pallas kernels, gather(): kernel(functools.partial(gather_kernel, slots, n_local, n_experts), grid=...  67.3 us
    pallas_call x5, Pallas kernels, back(): kernel(functools.partial(row_kernel, slots), grid=(hi - lo,), in_specs=[a...  58.6 us
    pallas_call x2, Pallas kernels, grads(): kernel(functools.partial(grad_kernel, bool(acc)), grid=(n_local,), in_spe...  54.4 us
    ppermute x52, starting transfers between devices, permute(): return lax.ppermute(v, ('etp', 'ep'), pairs)  46.4 us
    pallas_call x3, Pallas kernels, token_kernel(): kernel(functools.partial(body, groups, slots, n_local), grid=(steps,), in...  42.2 us
    pallas_call x1, Pallas kernels, layer(): kernel(functools.partial(slot_kernel, capacity, slots, n_local), grid=(n_...  16.7 us
  transfers between devices with their start and end apart: 52, of which 18 were waited for; matrix products, arithmetic and copies ran while one was open for 4% of the time, Pallas kernels for 27%

profile of v1, /device:TPU:0, one launch (start us, length us, event | category | flops | bytes accessed | tf_op | source)
XLA Modules:
  0.0 760.4 jit_solution(16012881459677608542)
XLA Ops:
  1.4 3.7 collective-permute-start.6
  7.4 2.0 collective-permute-start.11
  10.1 2.1 copy.23.ids_ref
  12.2 1.7 copy.22.wr_ref.refs_15_
  13.8 2.0 fusion.6
  15.9 4.2 constant_dynamic-update-slice_fusion.9
  20.1 2.1 constant_dynamic-update-slice_fusion.8.wo_ref.w13_ref
  22.7 10.9 %shard_map.126 = (f32[2048,32]{1,0:T(8,128)}, f32[2048,128]{1,0:T(8,128)}, s32[8,128]{1,0:T(8,128)}, f32[8,128]{1,0:T(8,128)}) custom-call(s32[4]{0:T(128)} %pad_add_fusion.info_ref, bf16[2048,512]{1,0:T(8,128)(2,1)} %refs_14_.1, f32[512,32]{1,0:T(8,128)} %copy.22.wr_ref.refs_15_, s32[2048,2]{1,0:T(8,128)} %copy.23.ids_ref), custom_call_target="tpu_custom_call" | custom-call | flops 3000000000 | bytes 1048576 | tf_op jit(solution)/shard_map/pallas_call | solution.py:461
  33.7 2.7 fusion.4
  39.5 1.8 collective-permute-start.1
  41.2 58.7 %collective-permute-done.3 = s32[16,256]{1,0:T(8,128)S(1)} collective-permute-done((s32[16,256]{1,0:T(8,128)S(1)}, s32[16,256]{1,0:T(8,128)S(1)}, u32[]{:S(2)}, u32[]{:S(2)}) %collective-permute-start.3) | collective-permute-done | bytes 16416 | tf_op jit(solution)/shard_map/ppermute | solution.py:407
  99.9 1.5 collective-permute-start
  102.6 1.5 collective-permute-start.24
  106.0 3.9 fusion.3
  109.9 20.7 %collective-permute-done.24.w2p_ref = bf16[1,384,512]{2,1,0:T(8,128)(2,1)} collective-permute-done((bf16[1,384,512]{2,1,0:T(8,128)(2,1)}, bf16[1,384,512]{2,1,0:T(8,128)(2,1)}, u32[]{:S(2)}, u32[]{:S(2)}) %collective-permute-start.24) | collective-permute-done | bytes 393248 | tf_op jit(solution)/shard_map/ppermute | solution.py:407
  130.6 6.2 collective-permute-done.19.w2p_ref
  137.9 18.9 %collective-permute-done.29.w2p_ref = bf16[2,384,512]{2,1,0:T(8,128)(2,1)S(1)} collective-permute-done((bf16[2,384,512]{2,1,0:T(8,128)(2,1)S(1)}, bf16[2,384,512]{2,1,0:T(8,128)(2,1)S(1)}, u32[]{:S(2)}, u32[]{:S(2)}) %collective-permute-start.29) | collective-permute-done | bytes 786464 | tf_op jit(solution)/shard_map/ppermute | solution.py:407
  158.9 16.7 %shard_map.127 = (f32[8,64,256]{2,1,0:T(8,128)}, f32[8,8,256]{2,1,0:T(8,128)}, s32[8,8,128]{2,1,0:T(8,128)}, bf16[512,128]{1,0:T(8,128)(2,1)}) custom-call(s32[9]{0:T(128)} %pad_add_fusion.1.info_ref, s32[8,16,256]{2,1,0:T(8,128)} %copy-done.5, f32[512,32]{1,0:T(8,128)} %copy.22.wr_ref.refs_15_), custom_call_target="tpu_custom_call" | custom-call | flops 5000000000 | bytes 1048576 | tf_op jit(solution)/shard_map/pallas_call | solution.py:450
  179.7 16.7 %shard_map.128 = (bf16[8,448,512]{2,1,0:T(8,128)(2,1)}, bf16[8,448,512]{2,1,0:T(8,128)(2,1)}) custom-call(s32[3]{0:T(128)} %add_add_fusion.info_ref, s32[8,8,128]{2,1,0:T(8,128)} %get-tuple-element.61.start_ref, f32[8,64,256]{2,1,0:T(8,128)} %get-tuple-element.62.slot_ref, f32[8,8,256]{2,1,0:T(8,128)} %get-tuple-element.63.other_ref, ...), custom_call_target="tpu_custom_call" | custom-call | flops 8000000000 | bytes 1048576 | tf_op jit(solution)/shard_map/pallas_call | solution.py:476
  199.8 17.2 %shard_map.129 = (bf16[8,448,512]{2,1,0:T(8,128)(2,1)}, bf16[8,448,512]{2,1,0:T(8,128)(2,1)}) custom-call(s32[3]{0:T(128)} %add_add_fusion.1.info_ref, s32[8,8,128]{2,1,0:T(8,128)} %get-tuple-element.61.start_ref, f32[8,64,256]{2,1,0:T(8,128)} %get-tuple-element.62.slot_ref, f32[8,8,256]{2,1,0:T(8,128)} %get-tuple-element.63.other_ref, ...), custom_call_target="tpu_custom_call" | custom-call | flops 8000000000 | bytes 1048576 | tf_op jit(solution)/shard_map/pallas_call | solution.py:476
  217.0 41.5 %collective-permute-done.18.wp_ref = bf16[1,512,768]{2,1,0:T(8,128)(2,1)} collective-permute-done((bf16[1,512,768]{2,1,0:T(8,128)(2,1)}, bf16[1,512,768]{2,1,0:T(8,128)(2,1)}, u32[]{:S(2)}, u32[]{:S(2)}) %collective-permute-start.18) | collective-permute-done | bytes 786464 | tf_op jit(solution)/shard_map/ppermute | solution.py:407
  259.7 8.2 %shard_map.132 = (bf16[1,224,512]{2,1,0:T(8,128)(2,1)}, bf16[1,224,512]{2,1,0:T(8,128)(2,1)}, bf16[1,224,512]{2,1,0:T(8,128)(2,1)}, bf16[1,224,512]{2,1,0:T(8,12...) custom-call(bf16[8,448,512]{2,1,0:T(8,128)(2,1)} %get-tuple-element., ...), custom_call_target="tpu_custom_call" | custom-call | flops 6000000000 | bytes 1048576 | tf_op jit(solution)/shard_map/pallas_call | solution.py:509
  267.9 8.4 %shard_map.131 = (bf16[1,2,224,512]{3,2,1,0:T(8,128)(2,1)}, bf16[1,2,224,512]{3,2,1,0:T(8,128)(2,1)}, bf16[1,2,224,512]{3,2,1,0:T(8,128)(2,1)}, bf16[1,2,224,512]{3,2,1,0:T(8,128)(2,1)}) custom-call(bf16[8,448,512]{2,1,0:T(8,128)(2,1)} %get-tuple-element.65.xa_ref, bf16[8,448,512]{2,1,0:T(8,128)(2,1)} %get-tuple-element.66.xb_ref, ...), custom_call_target="tpu_custom_call" | custom-call | flops 6000000000 | bytes 1048576 | tf_op jit(solution)/shard_map/pallas_call | solution.py:509
  276.3 15.9 %collective-permute-done.33.wp_ref = bf16[2,512,768]{2,1,0:T(8,128)(2,1)} collective-permute-done((bf16[2,512,768]{2,1,0:T(8,128)(2,1)}, bf16[2,512,768]{2,1,0:T(8,128)(2,1)}, u32[]{:S(2)}, u32[]{:S(2)}) %collective-permute-start.33) | collective-permute-done | bytes 1572896 | tf_op jit(solution)/shard_map/ppermute | solution.py:407
  292.2 33.7 %collective-permute-done.28.wp_ref = bf16[2,512,768]{2,1,0:T(8,128)(2,1)} collective-permute-done((bf16[2,512,768]{2,1,0:T(8,128)(2,1)S(1)}, bf16[2,512,768]{2,1,0:T(8,128)(2,1)}, u32[]{:S(2)}, u32[]{:S(2)}) %collective-permute-start.28) | collective-permute-done | bytes 1572896 | tf_op jit(solution)/shard_map/ppermute | solution.py:407
  327.1 32.5 %collective-permute-done.13.wp_ref = bf16[2,512,768]{2,1,0:T(8,128)(2,1)} collective-permute-done((bf16[2,512,768]{2,1,0:T(8,128)(2,1)S(1)}, bf16[2,512,768]{2,1,0:T(8,128)(2,1)}, u32[]{:S(2)}, u32[]{:S(2)}) %collective-permute-start.13) | collective-permute-done | bytes 1572896 | tf_op jit(solution)/shard_map/ppermute | solution.py:407
  360.9 14.0 %shard_map.134 = (bf16[2,2,224,512]{3,2,1,0:T(8,128)(2,1)}, bf16[2,2,224,512]{3,2,1,0:T(8,128)(2,1)}, bf16[2,2,224,512]{3,2,1,0:T(8,128)(2,1)}, bf16[2,2,224,512]{3,2,1,0:T(8,128)(2,1)}) custom-call(bf16[8,448,512]{2,1,0:T(8,128)(2,1)} %get-tuple-element.65.xa_ref, bf16[8,448,512]{2,1,0:T(8,128)(2,1)} %get-tuple-element.66.xb_ref, ...), custom_call_target="tpu_custom_call" | custom-call | flops 12000000000 | bytes 1048576 | tf_op jit(solution)/shard_map/pallas_call | solution.py:509
  374.9 27.7 %collective-permute-done.46.da_ref = bf16[2048,512]{1,0:T(8,128)(2,1)} collective-permute-done((bf16[2048,512]{1,0:T(8,128)(2,1)}, bf16[2048,512]{1,0:T(8,128)(2,1)}, u32[]{:S(2)}, u32[]{:S(2)}) %collective-permute-start.46) | collective-permute-done | bytes 2097184 | tf_op jit(solution)/shard_map/ppermute | solution.py:407
  402.6 1.5 collective-permute-start.21
  404.8 1.5 collective-permute-start.36
  406.3 14.0 %shard_map.133 = (bf16[2,2,224,512]{3,2,1,0:T(8,128)(2,1)}, bf16[2,2,224,512]{3,2,1,0:T(8,128)(2,1)}, bf16[2,2,224,512]{3,2,1,0:T(8,128)(2,1)}, bf16[2,2,224,512]{3,2,1,0:T(8,128)(2,1)}) custom-call(bf16[8,448,512]{2,1,0:T(8,128)(2,1)} %get-tuple-element.65.xa_ref, bf16[8,448,512]{2,1,0:T(8,128)(2,1)} %get-tuple-element.66.xb_ref, ...), custom_call_target="tpu_custom_call" | custom-call | flops 12000000000 | bytes 1048576 | tf_op jit(solution)/shard_map/pallas_call | solution.py:509
  421.5 3.4 collective-permute-done.22.refs_7_
  427.0 18.6 %collective-permute-done.36.refs_6_ = bf16[2,2,224,512]{3,2,1,0:T(8,128)(2,1)} collective-permute-done((bf16[2,2,224,512]{3,2,1,0:T(8,128)(2,1)}, bf16[2,2,224,512]{3,2,1,0:T(8,128)(2,1)}, u32[]{:S(2)}, u32[]{:S(2)}) %collective-permute-start.36) | collective-permute-done | bytes 917536 | tf_op jit(solution)/shard_map/ppermute | solution.py:407
  447.1 17.2 %collective-permute-done.37.refs_7_ = bf16[2,2,224,512]{3,2,1,0:T(8,128)(2,1)} collective-permute-done((bf16[2,2,224,512]{3,2,1,0:T(8,128)(2,1)}, bf16[2,2,224,512]{3,2,1,0:T(8,128)(2,1)}, u32[]{:S(2)}, u32[]{:S(2)}) %collective-permute-start.37) | collective-permute-done | bytes 917536 | tf_op jit(solution)/shard_map/ppermute | solution.py:407
  464.3 1.9 collective-permute-start.32
  466.2 14.0 %shard_map.130 = (bf16[2,2,224,512]{3,2,1,0:T(8,128)(2,1)}, bf16[2,2,224,512]{3,2,1,0:T(8,128)(2,1)}, bf16[2,2,224,512]{3,2,1,0:T(8,128)(2,1)}, bf16[2,2,224,512]{3,2,1,0:T(8,128)(2,1)}) custom-call(bf16[8,448,512]{2,1,0:T(8,128)(2,1)} %get-tuple-element.65.xa_ref, bf16[8,448,512]{2,1,0:T(8,128)(2,1)} %get-tuple-element.66.xb_ref, ...), custom_call_target="tpu_custom_call" | custom-call | flops 12000000000 | bytes 1048576 | tf_op jit(solution)/shard_map/pallas_call | solution.py:509
  480.3 94.6 %collective-permute-done.31.refs_2_ = bf16[2,2,224,512]{3,2,1,0:T(8,128)(2,1)} collective-permute-done((bf16[2,2,224,512]{3,2,1,0:T(8,128)(2,1)}, bf16[2,2,224,512]{3,2,1,0:T(8,128)(2,1)}, u32[]{:S(2)}, u32[]{:S(2)}) %collective-permute-start.31) | collective-permute-done | bytes 917536 | tf_op jit(solution)/shard_map/ppermute | solution.py:407
  576.3 17.2 %collective-permute-done.32.refs_3_ = bf16[2,2,224,512]{3,2,1,0:T(8,128)(2,1)} collective-permute-done((bf16[2,2,224,512]{3,2,1,0:T(8,128)(2,1)}, bf16[2,2,224,512]{3,2,1,0:T(8,128)(2,1)}, u32[]{:S(2)}, u32[]{:S(2)}) %collective-permute-start.32) | collective-permute-done | bytes 917536 | tf_op jit(solution)/shard_map/ppermute | solution.py:407
  593.5 1.9 collective-permute-start.17
  595.9 12.0 %shard_map.135 = (bf16[2048,512]{1,0:T(8,128)(2,1)}, bf16[2048,512]{1,0:T(8,128)(2,1)}, f32[2048,512]{1,0:T(8,128)}) custom-call(s32[4]{0:T(128)} %pad_add_fusion.info_ref, s32[8,128]{1,0:T(8,128)} %get-tuple-element.59.win_ref, f32[2048,128]{1,0:T(8,128)} %get-tuple-element.60.code_ref, bf16[2,2,224,512]{3,2,1,0:T(8,128)(2,1)} %get-tuple-element.81.refs_0_, ...), custom_call_target="tpu_custom_call" | custom-call | flops 8000000000 | bytes 1048576 | tf_op jit(solution)/shard_map/pallas_call | solution.py:527
  608.0 6.2 collective-permute-done.16.refs_2_
  614.1 16.2 %collective-permute-done.17.refs_3_ = bf16[2,2,224,512]{3,2,1,0:T(8,128)(2,1)} collective-permute-done((bf16[2,2,224,512]{3,2,1,0:T(8,128)(2,1)}, bf16[2,2,224,512]{3,2,1,0:T(8,128)(2,1)}, u32[]{:S(2)}, u32[]{:S(2)}) %collective-permute-start.17) | collective-permute-done | bytes 917536 | tf_op jit(solution)/shard_map/ppermute | solution.py:407
  630.4 17.4 %shard_map.136 = (bf16[2048,512]{1,0:T(8,128)(2,1)}, f32[2048,32]{1,0:T(8,128)}, f32[40,512]{1,0:T(8,128)}) custom-call(s32[4]{0:T(128)} %pad_add_fusion.info_ref, s32[8,128]{1,0:T(8,128)} %get-tuple-element.59.win_ref, f32[2048,128]{1,0:T(8,128)} %get-tuple-element.60.code_ref, bf16[2,2,224,512]{3,2,1,0:T(8,128)(2,1)} %get-tuple-element.69.refs_0_, ...), custom_call_target="tpu_custom_call" | custom-call | flops 8000000000 | bytes 1048576 | tf_op jit(solution)/shard_map/pallas_call | solution.py:527
  652.8 26.7 %shard_map.140 = (f32[8,512,384]{2,1,0:T(8,128)}, f32[8,512,384]{2,1,0:T(8,128)}, f32[8,384,512]{2,1,0:T(8,128)}) custom-call(bf16[8,448,512]{2,1,0:T(8,128)(2,1)} %get-tuple-element.65.xa_ref, bf16[8,448,512]{2,1,0:T(8,128)(2,1)} %get-tuple-element.66.xb_ref, bf16[8,448,512]{2,1,0:T(8,128)(2,1)} %get-tuple-element.67.ca_ref, ...), custom_call_target="tpu_custom_call" | custom-call | flops 24999999488 | bytes 1048576 | tf_op jit(solution)/shard_map/pallas_call | solution.py:492
  681.5 16.7 %shard_map.138 = (bf16[8,448,512]{2,1,0:T(8,128)(2,1)}, bf16[8,448,512]{2,1,0:T(8,128)(2,1)}) custom-call(s32[3]{0:T(128)} %add_add_fusion.2.info_ref, s32[8,8,128]{2,1,0:T(8,128)} %get-tuple-element.61.start_ref, f32[8,64,256]{2,1,0:T(8,128)} %get-tuple-element.62.slot_ref, f32[8,8,256]{2,1,0:T(8,128)} %get-tuple-element.63.other_ref, ...), custom_call_target="tpu_custom_call" | custom-call | flops 8000000000 | bytes 1048576 | tf_op jit(solution)/shard_map/pallas_call | solution.py:476
  699.9 12.7 %shard_map.137 = bf16[2048,512]{1,0:T(8,128)(2,1)} custom-call(s32[4]{0:T(128)} %pad_add_fusion.info_ref, s32[8,128]{1,0:T(8,128)} %get-tuple-element.59.win_ref, f32[2048,128]{1,0:T(8,128)} %get-tuple-element.60.code_ref, bf16[2,2,224,512]{3,2,1,0:T(8,128)(2,1)} %get-tuple-element.69.refs_0_, bf16[2,2,224,512]{3,2,1,0:T(8,128)(2,1)} %copy-done.13, ...), custom_call_target="tpu_custom_call" | custom-call | flops 8000000000 | bytes 1048576 | tf_op jit(solution)/shard_map/pallas_call | solution.py:527
  714.6 16.7 %shard_map.139 = (bf16[8,448,512]{2,1,0:T(8,128)(2,1)}, bf16[8,448,512]{2,1,0:T(8,128)(2,1)}) custom-call(s32[3]{0:T(128)} %add_add_fusion.3.info_ref, s32[8,8,128]{2,1,0:T(8,128)} %get-tuple-element.61.start_ref, f32[8,64,256]{2,1,0:T(8,128)} %get-tuple-element.62.slot_ref, f32[8,8,256]{2,1,0:T(8,128)} %get-tuple-element.63.other_ref, ...), custom_call_target="tpu_custom_call" | custom-call | flops 8000000000 | bytes 1048576 | tf_op jit(solution)/shard_map/pallas_call | solution.py:476
  731.3 27.7 %shard_map.141 = (f32[8,512,384]{2,1,0:T(8,128)}, f32[8,512,384]{2,1,0:T(8,128)}, f32[8,384,512]{2,1,0:T(8,128)}) custom-call(bf16[8,448,512]{2,1,0:T(8,128)(2,1)} %get-tuple-element.101.xa_ref, bf16[8,448,512]{2,1,0:T(8,128)(2,1)} %get-tuple-element.102.xb_ref, ...), custom_call_target="tpu_custom_call", output_to_operand_aliasing={{0}: (6, {}), {1}: (7, {}), {2}: (8, {})} | custom-call | flops 24999999488 | bytes 1048576 | tf_op jit(solution)/shard_map/pallas_call | solution.py:492
  (163 shorter events, 42.0 us)
Async XLA Ops:
  1.4 37.1 %collective-permute-start.6 = (s32[16,256]{1,0:T(8,128)S(1)}, s32[16,256]{1,0:T(8,128)S(1)}, u32[]{:S(2)}, u32[]{:S(2)}) collective-permute-start(s32[16,256]{1,0:T(8,128)S(1)} %reshape.34), channel_id=1, source_target_pairs={{0,7},{1,6},{2,5},{3,4},{4,3},{5,2},{6,1},{7,0}} | collective-permute-start | bytes 49160 | tf_op jit(solution)/shard_map/ppermute | solution.py:407
  5.1 33.4 %collective-permute-start.5 = (s32[16,256]{1,0:T(8,128)S(1)}, s32[16,256]{1,0:T(8,128)S(1)}, u32[]{:S(2)}, u32[]{:S(2)}) collective-permute-start(s32[16,256]{1,0:T(8,128)S(1)} %reshape.34), channel_id=1, source_target_pairs={{0,3},{1,2},{2,1},{3,0},{4,7},{5,6},{6,5},{7,4}} | collective-permute-start | bytes 49160 | tf_op jit(solution)/shard_map/ppermute | solution.py:407
  5.9 33.6 %collective-permute-start.4 = (s32[16,256]{1,0:T(8,128)S(1)}, s32[16,256]{1,0:T(8,128)S(1)}, u32[]{:S(2)}, u32[]{:S(2)}) collective-permute-start(s32[16,256]{1,0:T(8,128)S(1)} %reshape.34), channel_id=1, source_target_pairs={{0,6},{1,7},{2,4},{3,5},{4,2},{5,3},{6,0},{7,1}} | collective-permute-start | bytes 49160 | tf_op jit(solution)/shard_map/ppermute | solution.py:407
  7.3 130.0 %collective-permute-start.9 = (bf16[2048,512]{1,0:T(8,128)(2,1)}, bf16[2048,512]{1,0:T(8,128)(2,1)}, u32[]{:S(2)}, u32[]{:S(2)}) collective-permute-start(bf16[2048,512]{1,0:T(8,128)(2,1)} %refs_14_.1), channel_id=1, source_target_pairs={{0,2},{1,3},{2,0},{3,1},{4,6},{5,7},{6,4},{7,5}} | collective-permute-start | bytes 6291464 | tf_op jit(solution)/shard_map/ppermute | solution.py:407
  7.4 130.2 %collective-permute-start.11 = (bf16[2048,512]{1,0:T(8,128)(2,1)}, bf16[2048,512]{1,0:T(8,128)(2,1)}, u32[]{:S(2)}, u32[]{:S(2)}) collective-permute-start(bf16[2048,512]{1,0:T(8,128)(2,1)} %refs_13_.1), channel_id=1, source_target_pairs={{0,2},{1,3},{2,0},{3,1},{4,6},{5,7},{6,4},{7,5}} | collective-permute-start | bytes 6291464 | tf_op jit(solution)/shard_map/ppermute | solution.py:407
  38.5 61.5 %collective-permute-start.3 = (s32[16,256]{1,0:T(8,128)S(1)}, s32[16,256]{1,0:T(8,128)S(1)}, u32[]{:S(2)}, u32[]{:S(2)}) collective-permute-start(s32[16,256]{1,0:T(8,128)S(1)} %reshape.34), channel_id=1, source_target_pairs={{0,2},{1,3},{2,0},{3,1},{4,6},{5,7},{6,4},{7,5}} | collective-permute-start | bytes 49160 | tf_op jit(solution)/shard_map/ppermute | solution.py:407
  38.5 62.9 %collective-permute-start.2 = (s32[16,256]{1,0:T(8,128)S(1)}, s32[16,256]{1,0:T(8,128)S(1)}, u32[]{:S(2)}, u32[]{:S(2)}) collective-permute-start(s32[16,256]{1,0:T(8,128)S(1)} %reshape.34), channel_id=1, source_target_pairs={{0,5},{1,4},{2,7},{3,6},{4,1},{5,0},{6,3},{7,2}} | collective-permute-start | bytes 49160 | tf_op jit(solution)/shard_map/ppermute | solution.py:407
  39.5 63.1 %collective-permute-start.1 = (s32[16,256]{1,0:T(8,128)S(1)}, s32[16,256]{1,0:T(8,128)S(1)}, u32[]{:S(2)}, u32[]{:S(2)}) collective-permute-start(s32[16,256]{1,0:T(8,128)S(1)} %reshape.34), channel_id=1, source_target_pairs={{0,1},{1,0},{2,3},{3,2},{4,5},{5,4},{6,7},{7,6}} | collective-permute-start | bytes 49160 | tf_op jit(solution)/shard_map/ppermute | solution.py:407
  101.5 35.3 %collective-permute-start.34 = (bf16[2,384,512]{2,1,0:T(8,128)(2,1)}, bf16[2,384,512]{2,1,0:T(8,128)(2,1)}, u32[]{:S(2)}, u32[]{:S(2)}) collective-permute-start(bf16[2,384,512]{2,1,0:T(8,128)(2,1)} %get-tuple-element.116), channel_id=1, source_target_pairs={{0,4},{1,5},{2,6},{3,7},{4,0},{5,1},{6,2},{7,3}} | collective-permute-start | bytes 2359304 | tf_op jit(solution)/shard_map/ppermute | solution.py:407
  102.6 28.1 %collective-permute-start.24 = (bf16[1,384,512]{2,1,0:T(8,128)(2,1)}, bf16[1,384,512]{2,1,0:T(8,128)(2,1)}, u32[]{:S(2)}, u32[]{:S(2)}) collective-permute-start(bf16[1,384,512]{2,1,0:T(8,128)(2,1)} %get-tuple-element.119), channel_id=1, source_target_pairs={{0,4},{1,5},{2,6},{3,7},{4,0},{5,1},{6,2},{7,3}} | collective-permute-start | bytes 1179656 | tf_op jit(solution)/shard_map/ppermute | solution.py:407
  104.1 32.7 %collective-permute-start.19 = (bf16[1,384,512]{2,1,0:T(8,128)(2,1)}, bf16[1,384,512]{2,1,0:T(8,128)(2,1)}, u32[]{:S(2)}, u32[]{:S(2)}) collective-permute-start(bf16[1,384,512]{2,1,0:T(8,128)(2,1)} %get-tuple-element.120), channel_id=1, source_target_pairs={{0,4},{1,5},{2,6},{3,7},{4,0},{5,1},{6,2},{7,3}} | collective-permute-start | bytes 1179656 | tf_op jit(solution)/shard_map/ppermute | solution.py:407
  130.6 47.0 %collective-permute-start.7 = (bf16[2048,512]{1,0:T(8,128)(2,1)}, bf16[2048,512]{1,0:T(8,128)(2,1)}, u32[]{:S(2)}, u32[]{:S(2)}) collective-permute-start(bf16[2048,512]{1,0:T(8,128)(2,1)} %refs_14_.1), channel_id=1, source_target_pairs={{0,1},{1,0},{2,3},{3,2},{4,5},{5,4},{6,7},{7,6}} | collective-permute-start | bytes 6291464 | tf_op jit(solution)/shard_map/ppermute | solution.py:407
  136.8 41.8 %collective-permute-start.8 = (bf16[2048,512]{1,0:T(8,128)(2,1)}, bf16[2048,512]{1,0:T(8,128)(2,1)}, u32[]{:S(2)}, u32[]{:S(2)}) collective-permute-start(bf16[2048,512]{1,0:T(8,128)(2,1)} %refs_13_.1), channel_id=1, source_target_pairs={{0,1},{1,0},{2,3},{3,2},{4,5},{5,4},{6,7},{7,6}} | collective-permute-start | bytes 6291464 | tf_op jit(solution)/shard_map/ppermute | solution.py:407
  136.8 20.0 %collective-permute-start.29 = (bf16[2,384,512]{2,1,0:T(8,128)(2,1)S(1)}, bf16[2,384,512]{2,1,0:T(8,128)(2,1)S(1)}, u32[]{:S(2)}, u32[]{:S(2)}) collective-permute-start(bf16[2,384,512]{2,1,0:T(8,128)(2,1)S(1)} %copy-done.4), channel_id=1, source_target_pairs={{0,4},{1,5},{2,6},{3,7},{4,0},{5,1},{6,2},{7,3}} | collective-permute-start | bytes 2359304 | tf_op jit(solution)/shard_map/ppermute | solution.py:407
  137.4 60.4 %collective-permute-start.10 = (bf16[2048,512]{1,0:T(8,128)(2,1)}, bf16[2048,512]{1,0:T(8,128)(2,1)}, u32[]{:S(2)}, u32[]{:S(2)}) collective-permute-start(bf16[2048,512]{1,0:T(8,128)(2,1)} %collective-permute-done.9.ha_ref), channel_id=1, source_target_pairs={{0,1},{1,0},{2,3},{3,2},{4,5},{5,4},{6,7},{7,6}} | collective-permute-start | bytes 6291464 | tf_op jit(solution)/shard_map/ppermute | solution.py:407
  137.6 61.0 %collective-permute-start.12 = (bf16[2048,512]{1,0:T(8,128)(2,1)}, bf16[2048,512]{1,0:T(8,128)(2,1)}, u32[]{:S(2)}, u32[]{:S(2)}) collective-permute-start(bf16[2048,512]{1,0:T(8,128)(2,1)} %collective-permute-done.11.da_ref), channel_id=1, source_target_pairs={{0,1},{1,0},{2,3},{3,2},{4,5},{5,4},{6,7},{7,6}} | collective-permute-start | bytes 6291464 | tf_op jit(solution)/shard_map/ppermute | solution.py:407
  156.8 19.2 %collective-permute-start.14 = (bf16[2,384,512]{2,1,0:T(8,128)(2,1)S(1)}, bf16[2,384,512]{2,1,0:T(8,128)(2,1)}, u32[]{:S(2)}, u32[]{:S(2)}) collective-permute-start(bf16[2,384,512]{2,1,0:T(8,128)(2,1)S(1)} %copy-done.3), channel_id=1, source_target_pairs={{0,4},{1,5},{2,6},{3,7},{4,0},{5,1},{6,2},{7,3}} | collective-permute-start | bytes 2359304 | tf_op jit(solution)/shard_map/ppermute | solution.py:407
  176.0 20.6 %collective-permute-start.23 = (bf16[1,512,768]{2,1,0:T(8,128)(2,1)}, bf16[1,512,768]{2,1,0:T(8,128)(2,1)S(1)}, u32[]{:S(2)}, u32[]{:S(2)}) collective-permute-start(bf16[1,512,768]{2,1,0:T(8,128)(2,1)} %get-tuple-element.114), channel_id=1, source_target_pairs={{0,4},{1,5},{2,6},{3,7},{4,0},{5,1},{6,2},{7,3}} | collective-permute-start | bytes 2359304 | tf_op jit(solution)/shard_map/ppermute | solution.py:407
  177.7 182.0 %collective-permute-start.44 = (bf16[2048,512]{1,0:T(8,128)(2,1)}, bf16[2048,512]{1,0:T(8,128)(2,1)}, u32[]{:S(2)}, u32[]{:S(2)}) collective-permute-start(bf16[2048,512]{1,0:T(8,128)(2,1)} %refs_14_.1), channel_id=1, source_target_pairs={{0,4},{1,5},{2,6},{3,7},{4,0},{5,1},{6,2},{7,3}} | collective-permute-start | bytes 6291464 | tf_op jit(solution)/shard_map/ppermute | solution.py:407
  178.5 80.0 %collective-permute-start.18 = (bf16[1,512,768]{2,1,0:T(8,128)(2,1)}, bf16[1,512,768]{2,1,0:T(8,128)(2,1)}, u32[]{:S(2)}, u32[]{:S(2)}) collective-permute-start(bf16[1,512,768]{2,1,0:T(8,128)(2,1)} %get-tuple-element.115), channel_id=1, source_target_pairs={{0,4},{1,5},{2,6},{3,7},{4,0},{5,1},{6,2},{7,3}} | collective-permute-start | bytes 2359304 | tf_op jit(solution)/shard_map/ppermute | solution.py:407
  196.6 95.6 %collective-permute-start.33 = (bf16[2,512,768]{2,1,0:T(8,128)(2,1)}, bf16[2,512,768]{2,1,0:T(8,128)(2,1)}, u32[]{:S(2)}, u32[]{:S(2)}) collective-permute-start(bf16[2,512,768]{2,1,0:T(8,128)(2,1)} %get-tuple-element.111), channel_id=1, source_target_pairs={{0,4},{1,5},{2,6},{3,7},{4,0},{5,1},{6,2},{7,3}} | collective-permute-start | bytes 4718600 | tf_op jit(solution)/shard_map/ppermute | solution.py:407
  197.8 128.1 %collective-permute-start.28 = (bf16[2,512,768]{2,1,0:T(8,128)(2,1)S(1)}, bf16[2,512,768]{2,1,0:T(8,128)(2,1)}, u32[]{:S(2)}, u32[]{:S(2)}) collective-permute-start(bf16[2,512,768]{2,1,0:T(8,128)(2,1)S(1)} %get-tuple-element.112), channel_id=1, source_target_pairs={{0,4},{1,5},{2,6},{3,7},{4,0},{5,1},{6,2},{7,3}} | collective-permute-start | bytes 4718600 | tf_op jit(solution)/shard_map/ppermute | solution.py:407
  198.6 161.0 %collective-permute-start.13 = (bf16[2,512,768]{2,1,0:T(8,128)(2,1)S(1)}, bf16[2,512,768]{2,1,0:T(8,128)(2,1)}, u32[]{:S(2)}, u32[]{:S(2)}) collective-permute-start(bf16[2,512,768]{2,1,0:T(8,128)(2,1)S(1)} %get-tuple-element.113), channel_id=1, source_target_pairs={{0,4},{1,5},{2,6},{3,7},{4,0},{5,1},{6,2},{7,3}} | collective-permute-start | bytes 4718600 | tf_op jit(solution)/shard_map/ppermute | solution.py:407
  258.5 144.1 %collective-permute-start.46 = (bf16[2048,512]{1,0:T(8,128)(2,1)}, bf16[2048,512]{1,0:T(8,128)(2,1)}, u32[]{:S(2)}, u32[]{:S(2)}) collective-permute-start(bf16[2048,512]{1,0:T(8,128)(2,1)} %refs_13_.1), channel_id=1, source_target_pairs={{0,4},{1,5},{2,6},{3,7},{4,0},{5,1},{6,2},{7,3}} | collective-permute-start | bytes 6291464 | tf_op jit(solution)/shard_map/ppermute | solution.py:407
  292.2 111.9 %collective-permute-start.25 = (bf16[1,224,512]{2,1,0:T(8,128)(2,1)S(1)}, bf16[1,224,512]{2,1,0:T(8,128)(2,1)S(1)}, u32[]{:S(2)}, u32[]{:S(2)}) collective-permute-start(bf16[1,224,512]{2,1,0:T(8,128)(2,1)S(1)} %copy-done.25), channel_id=1, source_target_pairs={{0,1},{1,0},{2,3},{3,2},{4,5},{5,4},{6,7},{7,6}} | collective-permute-start | bytes 688136 | tf_op jit(solution)/shard_map/ppermute | solution.py:407
  325.9 78.2 %collective-permute-start.26 = (bf16[1,224,512]{2,1,0:T(8,128)(2,1)S(1)}, bf16[1,224,512]{2,1,0:T(8,128)(2,1)S(1)}, u32[]{:S(2)}, u32[]{:S(2)}) collective-permute-start(bf16[1,224,512]{2,1,0:T(8,128)(2,1)S(1)} %copy-done.24), channel_id=1, source_target_pairs={{0,2},{1,3},{2,0},{3,1},{4,6},{5,7},{6,4},{7,5}} | collective-permute-start | bytes 688136 | tf_op jit(solution)/shard_map/ppermute | solution.py:407
  359.6 45.2 %collective-permute-start.27 = (bf16[1,224,512]{2,1,0:T(8,128)(2,1)}, bf16[1,224,512]{2,1,0:T(8,128)(2,1)S(1)}, u32[]{:S(2)}, u32[]{:S(2)}) collective-permute-start(bf16[1,224,512]{2,1,0:T(8,128)(2,1)} %get-tuple-element.80), channel_id=1, source_target_pairs={{0,3},{1,2},{2,1},{3,0},{4,7},{5,6},{6,5},{7,4}} | collective-permute-start | bytes 688136 | tf_op jit(solution)/shard_map/ppermute | solution.py:407
  359.6 46.6 %collective-permute-start.20 = (bf16[1,2,224,512]{3,2,1,0:T(8,128)(2,1)}, bf16[1,2,224,512]{3,2,1,0:T(8,128)(2,1)S(1)}, u32[]{:S(2)}, u32[]{:S(2)}) collective-permute-start(bf16[1,2,224,512]{3,2,1,0:T(8,128)(2,1)} %get-tuple-element.74), channel_id=1, source_target_pairs={{0,1},{1,0},{2,3},{3,2},{4,5},{5,4},{6,7},{7,6}} | collective-permute-start | bytes 1376264 | tf_op jit(solution)/shard_map/ppermute | solution.py:407
  404.1 20.8 %collective-permute-start.22 = (bf16[1,2,224,512]{3,2,1,0:T(8,128)(2,1)}, bf16[1,2,224,512]{3,2,1,0:T(8,128)(2,1)}, u32[]{:S(2)}, u32[]{:S(2)}) collective-permute-start(bf16[1,2,224,512]{3,2,1,0:T(8,128)(2,1)} %get-tuple-element.76), channel_id=1, source_target_pairs={{0,3},{1,2},{2,1},{3,0},{4,7},{5,6},{6,5},{7,4}} | collective-permute-start | bytes 1376264 | tf_op jit(solution)/shard_map/ppermute | solution.py:407
  404.1 21.4 %collective-permute-start.35 = (bf16[2,2,224,512]{3,2,1,0:T(8,128)(2,1)}, bf16[2,2,224,512]{3,2,1,0:T(8,128)(2,1)S(1)}, u32[]{:S(2)}, u32[]{:S(2)}) collective-permute-start(bf16[2,2,224,512]{3,2,1,0:T(8,128)(2,1)} %get-tuple-element.86), channel_id=1, source_target_pairs={{0,1},{1,0},{2,3},{3,2},{4,5},{5,4},{6,7},{7,6}} | collective-permute-start | bytes 2752520 | tf_op jit(solution)/shard_map/ppermute | solution.py:407
  404.8 40.8 %collective-permute-start.36 = (bf16[2,2,224,512]{3,2,1,0:T(8,128)(2,1)}, bf16[2,2,224,512]{3,2,1,0:T(8,128)(2,1)}, u32[]{:S(2)}, u32[]{:S(2)}) collective-permute-start(bf16[2,2,224,512]{3,2,1,0:T(8,128)(2,1)} %get-tuple-element.87), channel_id=1, source_target_pairs={{0,2},{1,3},{2,0},{3,1},{4,6},{5,7},{6,4},{7,5}} | collective-permute-start | bytes 2752520 | tf_op jit(solution)/shard_map/ppermute | solution.py:407
  406.3 58.0 %collective-permute-start.37 = (bf16[2,2,224,512]{3,2,1,0:T(8,128)(2,1)}, bf16[2,2,224,512]{3,2,1,0:T(8,128)(2,1)}, u32[]{:S(2)}, u32[]{:S(2)}) collective-permute-start(bf16[2,2,224,512]{3,2,1,0:T(8,128)(2,1)} %get-tuple-element.88), channel_id=1, source_target_pairs={{0,3},{1,2},{2,1},{3,0},{4,7},{5,6},{6,5},{7,4}} | collective-permute-start | bytes 2752520 | tf_op jit(solution)/shard_map/ppermute | solution.py:407
  420.3 230.0 %collective-permute-start.48 = (bf16[2048,512]{1,0:T(8,128)(2,1)}, bf16[2048,512]{1,0:T(8,128)(2,1)S(1)}, u32[]{:S(2)}, u32[]{:S(2)}) collective-permute-start(bf16[2048,512]{1,0:T(8,128)(2,1)} %collective-permute-done.44.ha_ref), channel_id=1, source_target_pairs={{0,2},{1,3},{2,0},{3,1},{4,6},{5,7},{6,4},{7,5}} | collective-permute-start | bytes 6291464 | tf_op jit(solution)/shard_map/ppermute | solution.py:407
  425.0 225.4 %collective-permute-start.50 = (bf16[2048,512]{1,0:T(8,128)(2,1)}, bf16[2048,512]{1,0:T(8,128)(2,1)}, u32[]{:S(2)}, u32[]{:S(2)}) collective-permute-start(bf16[2048,512]{1,0:T(8,128)(2,1)} %collective-permute-done.46.da_ref), channel_id=1, source_target_pairs={{0,2},{1,3},{2,0},{3,1},{4,6},{5,7},{6,4},{7,5}} | collective-permute-start | bytes 6291464 | tf_op jit(solution)/shard_map/ppermute | solution.py:407
  425.5 54.7 %collective-permute-start.30 = (bf16[2,2,224,512]{3,2,1,0:T(8,128)(2,1)}, bf16[2,2,224,512]{3,2,1,0:T(8,128)(2,1)}, u32[]{:S(2)}, u32[]{:S(2)}) collective-permute-start(bf16[2,2,224,512]{3,2,1,0:T(8,128)(2,1)} %get-tuple-element.82), channel_id=1, source_target_pairs={{0,1},{1,0},{2,3},{3,2},{4,5},{5,4},{6,7},{7,6}} | collective-permute-start | bytes 2752520 | tf_op jit(solution)/shard_map/ppermute | solution.py:407
  445.6 129.2 %collective-permute-start.31 = (bf16[2,2,224,512]{3,2,1,0:T(8,128)(2,1)}, bf16[2,2,224,512]{3,2,1,0:T(8,128)(2,1)}, u32[]{:S(2)}, u32[]{:S(2)}) collective-permute-start(bf16[2,2,224,512]{3,2,1,0:T(8,128)(2,1)} %get-tuple-element.83), channel_id=1, source_target_pairs={{0,2},{1,3},{2,0},{3,1},{4,6},{5,7},{6,4},{7,5}} | collective-permute-start | bytes 2752520 | tf_op jit(solution)/shard_map/ppermute | solution.py:407
  464.3 129.2 %collective-permute-start.32 = (bf16[2,2,224,512]{3,2,1,0:T(8,128)(2,1)}, bf16[2,2,224,512]{3,2,1,0:T(8,128)(2,1)}, u32[]{:S(2)}, u32[]{:S(2)}) collective-permute-start(bf16[2,2,224,512]{3,2,1,0:T(8,128)(2,1)} %get-tuple-element.84), channel_id=1, source_target_pairs={{0,3},{1,2},{2,1},{3,0},{4,7},{5,6},{6,5},{7,4}} | collective-permute-start | bytes 2752520 | tf_op jit(solution)/shard_map/ppermute | solution.py:407
  480.2 127.7 %collective-permute-start.15 = (bf16[2,2,224,512]{3,2,1,0:T(8,128)(2,1)}, bf16[2,2,224,512]{3,2,1,0:T(8,128)(2,1)S(1)}, u32[]{:S(2)}, u32[]{:S(2)}) collective-permute-start(bf16[2,2,224,512]{3,2,1,0:T(8,128)(2,1)} %get-tuple-element.70), channel_id=1, source_target_pairs={{0,1},{1,0},{2,3},{3,2},{4,5},{5,4},{6,7},{7,6}} | collective-permute-start | bytes 2752520 | tf_op jit(solution)/shard_map/ppermute | solution.py:407
  574.8 39.3 %collective-permute-start.16 = (bf16[2,2,224,512]{3,2,1,0:T(8,128)(2,1)}, bf16[2,2,224,512]{3,2,1,0:T(8,128)(2,1)}, u32[]{:S(2)}, u32[]{:S(2)}) collective-permute-start(bf16[2,2,224,512]{3,2,1,0:T(8,128)(2,1)} %get-tuple-element.71), channel_id=1, source_target_pairs={{0,2},{1,3},{2,0},{3,1},{4,6},{5,7},{6,4},{7,5}} | collective-permute-start | bytes 2752520 | tf_op jit(solution)/shard_map/ppermute | solution.py:407
  593.5 36.9 %collective-permute-start.17 = (bf16[2,2,224,512]{3,2,1,0:T(8,128)(2,1)}, bf16[2,2,224,512]{3,2,1,0:T(8,128)(2,1)}, u32[]{:S(2)}, u32[]{:S(2)}) collective-permute-start(bf16[2,2,224,512]{3,2,1,0:T(8,128)(2,1)} %get-tuple-element.72), channel_id=1, source_target_pairs={{0,3},{1,2},{2,1},{3,0},{4,7},{5,6},{6,5},{7,4}} | collective-permute-start | bytes 2752520 | tf_op jit(solution)/shard_map/ppermute | solution.py:407
  649.8 29.8 %collective-permute-start.45 = (bf16[2048,512]{1,0:T(8,128)(2,1)}, bf16[2048,512]{1,0:T(8,128)(2,1)}, u32[]{:S(2)}, u32[]{:S(2)}) collective-permute-start(bf16[2048,512]{1,0:T(8,128)(2,1)} %collective-permute-done.44.ha_ref), channel_id=1, source_target_pairs={{0,1},{1,0},{2,3},{3,2},{4,5},{5,4},{6,7},{7,6}} | collective-permute-start | bytes 6291464 | tf_op jit(solution)/shard_map/ppermute | solution.py:407
  649.8 29.8 %collective-permute-start.47 = (bf16[2048,512]{1,0:T(8,128)(2,1)}, bf16[2048,512]{1,0:T(8,128)(2,1)}, u32[]{:S(2)}, u32[]{:S(2)}) collective-permute-start(bf16[2048,512]{1,0:T(8,128)(2,1)} %collective-permute-done.46.da_ref), channel_id=1, source_target_pairs={{0,1},{1,0},{2,3},{3,2},{4,5},{5,4},{6,7},{7,6}} | collective-permute-start | bytes 6291464 | tf_op jit(solution)/shard_map/ppermute | solution.py:407
  650.3 64.3 %collective-permute-start.49 = (bf16[2048,512]{1,0:T(8,128)(2,1)S(1)}, bf16[2048,512]{1,0:T(8,128)(2,1)}, u32[]{:S(2)}, u32[]{:S(2)}) collective-permute-start(bf16[2048,512]{1,0:T(8,128)(2,1)S(1)} %collective-permute-done.48.ha_ref), channel_id=1, source_target_pairs={{0,1},{1,0},{2,3},{3,2},{4,5},{5,4},{6,7},{7,6}} | collective-permute-start | bytes 6291464 | tf_op jit(solution)/shard_map/ppermute | solution.py:407
  650.3 64.2 %collective-permute-start.51 = (bf16[2048,512]{1,0:T(8,128)(2,1)}, bf16[2048,512]{1,0:T(8,128)(2,1)}, u32[]{:S(2)}, u32[]{:S(2)}) collective-permute-start(bf16[2048,512]{1,0:T(8,128)(2,1)} %collective-permute-done.50.da_ref), channel_id=1, source_target_pairs={{0,1},{1,0},{2,3},{3,2},{4,5},{5,4},{6,7},{7,6}} | collective-permute-start | bytes 6291464 | tf_op jit(solution)/shard_map/ppermute | solution.py:407
  651.9 28.9 %collective-permute-start.42 = (f32[40,512]{1,0:T(8,128)S(1)}, f32[40,512]{1,0:T(8,128)S(1)}, u32[]{:S(2)}, u32[]{:S(2)}) collective-permute-start(f32[40,512]{1,0:T(8,128)S(1)} %add.38), channel_id=1, source_target_pairs={{0,2},{1,3},{2,0},{3,1},{4,6},{5,7},{6,4},{7,5}} | collective-permute-start | bytes 245768 | tf_op jit(solution)/shard_map/ppermute | solution.py:407
  679.6 18.6 %collective-permute-start.38 = (bf16[1,224,512]{2,1,0:T(8,128)(2,1)S(1)}, bf16[1,224,512]{2,1,0:T(8,128)(2,1)S(1)}, u32[]{:S(2)}, u32[]{:S(2)}) collective-permute-start(bf16[1,224,512]{2,1,0:T(8,128)(2,1)S(1)} %copy-done.20), channel_id=1, source_target_pairs={{0,1},{1,0},{2,3},{3,2},{4,5},{5,4},{6,7},{7,6}} | collective-permute-start | bytes 688136 | tf_op jit(solution)/shard_map/ppermute | solution.py:407
  679.6 19.5 %collective-permute-start.39 = (bf16[1,224,512]{2,1,0:T(8,128)(2,1)S(1)}, bf16[1,224,512]{2,1,0:T(8,128)(2,1)S(1)}, u32[]{:S(2)}, u32[]{:S(2)}) collective-permute-start(bf16[1,224,512]{2,1,0:T(8,128)(2,1)S(1)} %copy-done.19), channel_id=1, source_target_pairs={{0,2},{1,3},{2,0},{3,1},{4,6},{5,7},{6,4},{7,5}} | collective-permute-start | bytes 688136 | tf_op jit(solution)/shard_map/ppermute | solution.py:407
  680.7 18.4 %collective-permute-start.40 = (bf16[1,224,512]{2,1,0:T(8,128)(2,1)S(1)}, bf16[1,224,512]{2,1,0:T(8,128)(2,1)S(1)}, u32[]{:S(2)}, u32[]{:S(2)}) collective-permute-start(bf16[1,224,512]{2,1,0:T(8,128)(2,1)S(1)} %copy-done.18), channel_id=1, source_target_pairs={{0,3},{1,2},{2,1},{3,0},{4,7},{5,6},{6,5},{7,4}} | collective-permute-start | bytes 688136 | tf_op jit(solution)/shard_map/ppermute | solution.py:407
  (33 other events, 633.6 us)

commit v2 on v1

--- a/solution.py
+++ b/solution.py
@@ -34,6 +34,22 @@
     return hi, mid, (rest - mid.astype(f32)).astype(bf16)
 
 
+def ind(mask):
+    return jnp.where(mask, 1.0, 0.0).astype(f32)
+
+
+def rsum(v):
+    return jnp.sum(v, axis=1, keepdims=True)
+
+
+def csum(v):
+    return jnp.sum(v, axis=0, keepdims=True)
+
+
+def cols(v, *at):
+    return [v[:, k:k + 1] for k in at]
+
+
 def iota(shape, dim):
     return lax.broadcasted_iota(jnp.int32, shape, dim)
 
@@ -58,20 +74,20 @@
     h = h_ref[...]
     z = (nn(h, w_lo) + nn(h, w_mid)) + nn(h, w_hi)
     z = jnp.exp(z - jnp.max(z, axis=1, keepdims=True))
-    p = z / jnp.sum(z, axis=1, keepdims=True)
+    p = z / rsum(z)
     p_ref[...] = p
     ids = ids_ref[...]
     lane = iota((TILE, n_experts), 1)
     e0, e1 = ids[:, 0:1], ids[:, 1:2]
     m0, m1 = lane == e0, lane == e1
-    hist = jnp.where(m0 | m1, 1.0, 0.0).astype(f32)
+    hist = ind(m0 | m1)
     before = (iota((TILE, TILE), 1) < iota((TILE, TILE), 0)).astype(f32).astype(bf16)
     seen = stat_ref[0:1, 0:n_experts]
-    after = seen + jnp.sum(hist, axis=0, keepdims=True)
+    after = seen + csum(hist)
     start = jnp.floor(seen * (1.0 / 16)) * 16
     n_win = jnp.max(jnp.floor((after - start + (WIN - 1)) * (1.0 / WIN) + 1e-3), axis=1, keepdims=True)
     rank = nn(before, hist.astype(bf16)) + seen
-    pick = lambda m, v: jnp.sum(jnp.where(m, v, 0.0), axis=1, keepdims=True)
+    pick = lambda m, v: rsum(jnp.where(m, v, 0.0))
     p0, p1 = pick(m0, p), pick(m1, p)
     s = p0 + p1
     wide = iota((TILE, 128), 1)
@@ -88,7 +104,7 @@
     win_ref[pl.ds(step, 1), 0:n_experts] = start.astype(jnp.int32)
     win_ref[pl.ds(step, 1), 127:128] = n_win.astype(jnp.int32)
     stat_ref[0:1, 0:n_experts] = after
-    stat_ref[1:2, 0:n_experts] = stat_ref[1:2, 0:n_experts] + jnp.sum(p, axis=0, keepdims=True)
+    stat_ref[1:2, 0:n_experts] = stat_ref[1:2, 0:n_experts] + csum(p)
 
 
 def slot_kernel(capacity, slots, n_local, info_ref, ids_ref, wr_ref, slot_ref, other_ref, start_ref, wr3_ref, total_ref):
@@ -112,15 +128,15 @@
     for i in range(steps):
         e0, e1 = ids_ref[near, 2 * i:2 * i + 1, :], ids_ref[near, 2 * i + 1:2 * i + 2, :]
         m0, m1 = expert == e0, expert == e1
-        hit = jnp.where(m0 | m1, 1.0, 0.0).astype(f32)
+        hit = ind(m0 | m1)
         rank = nn(hit.astype(bf16), before) + carry
         slot_ref[0, i * n_local:(i + 1) * n_local, :] = jnp.where(m0 | m1, rank, -1.0)
         starts = jnp.where(lane == i, carry, starts)
         for m, e in ((m0, e1), (m1, e0)):
-            pos = jnp.sum(jnp.where(m, rank + 1.0, 0.0), axis=0, keepdims=True) - 1.0
-            one = jnp.where(row == pos, 1.0, 0.0).astype(bf16)
+            pos = csum(jnp.where(m, rank + 1.0, 0.0)) - 1.0
+            one = ind(row == pos).astype(bf16)
             other = other + nt(jnp.where(m, e.astype(f32), 0.0).astype(bf16), one)
-        carry = carry + jnp.sum(hit, axis=1, keepdims=True)
+        carry = carry + rsum(hit)
     other_ref[0] = other
     prefix = total_ref[:, 0:1]
     room = jnp.clip(capacity - prefix, 0.0, float(slots))
@@ -146,7 +162,7 @@
                 for e in range(n_local):
                     slot = slot_ref[j, pl.ds(step * n_local + e, 1), :]
                     hit = (row + (first[e] + w * WIN)).astype(f32) == slot
-                    m_ref[e * WIN:(e + 1) * WIN, :] = jnp.where(hit, 1.0, 0.0).astype(bf16)
+                    m_ref[e * WIN:(e + 1) * WIN, :] = ind(hit).astype(bf16)
                 m = m_ref[...]
                 for src, dst in ((h_ref, xs_ref), (d_ref, ds_ref)):
                     r = nn(m, src[...]).astype(bf16)
@@ -174,10 +190,10 @@
             x_ref[0, b * slots:(b + 1) * slots, :] = x
             z = nn(x, wr3_ref[...])
             other = other_ref[j].T[0:slots, :]
-            other = jnp.sum(jnp.where(iota((slots, n_local), 1) == e, other, 0.0), axis=1, keepdims=True)
+            other = rsum(jnp.where(iota((slots, n_local), 1) == e, other, 0.0))
             name = lane % n_experts
-            here = jnp.sum(jnp.where(name == info_ref[2] + e, z, 0.0), axis=1, keepdims=True)
-            there = jnp.sum(jnp.where(name == other.astype(jnp.int32), z, 0.0), axis=1, keepdims=True)
+            here = rsum(jnp.where(name == info_ref[2] + e, z, 0.0))
+            there = rsum(jnp.where(name == other.astype(jnp.int32), z, 0.0))
             g = 1.0 / (1.0 + jnp.exp(there - here))
             c_ref[0, b * slots:(b + 1) * slots, :] = (g * (OUT_SCALE * d)).astype(bf16)
 
@@ -272,7 +288,7 @@
     for k in range(2):
         rel = code[:, 9 + k:10 + k]
         at = jnp.where((rel >= low) & (rel < low + WIN), code[:, 7 + k:8 + k] + rel - low, -1.0)
-        out.append(jnp.where(col == at, 1.0, 0.0))
+        out.append(ind(col == at))
     return out
 
 
@@ -335,26 +351,26 @@
         fetch(names_of(groups, refs[:n_r], 0), w, slots, n_local, info_ref, win_ref, rows_ref)
         return collect_y(code, w, col, rows_ref)
 
-    y_ref[...] = collect(0)
+    y_ref[...] = jnp.zeros_like(y_ref)
 
     def more(w):
         y_ref[...] = y_ref[...] + collect(w)
 
     further(win_ref, more)
-    y0 = y0_ref[...].astype(f32) + y_ref[:rows, :]
-    y1 = y1_ref[...].astype(f32) + y_ref[rows:, :]
-    e0, e1 = code[:, 0:1].astype(jnp.int32), code[:, 1:2].astype(jnp.int32)
-    g0, g1, s = code[:, 4:5], code[:, 5:6], code[:, 6:7]
+    y = y_ref[...] + collect(0)
+    y0 = y0_ref[...].astype(f32) + y[:rows]
+    y1 = y1_ref[...].astype(f32) + y[rows:]
+    e0, e1, g0, g1, s = cols(code, 0, 1, 4, 5, 6)
     h = h_ref[...]
     m = OUT_SCALE * d_ref[...].astype(f32)
     out_ref[...] = (h.astype(f32) + OUT_SCALE * (g0 * y0 + g1 * y1)).astype(bf16)
-    dg0 = jnp.sum(m * y0, axis=1, keepdims=True)
-    dg1 = jnp.sum(m * y1, axis=1, keepdims=True)
+    dg0 = rsum(m * y0)
+    dg1 = rsum(m * y1)
     mean = g0 * dg0 + g1 * dg1
-    lane = iota(p.shape, 1)
+    lane = iota(p.shape, 1).astype(f32)
     dp = (jnp.where(lane == e0, (dg0 - mean) / s, 0.0) + jnp.where(lane == e1, (dg1 - mean) / s, 0.0)
           + coef_ref[...])
-    dz = p * (dp - jnp.sum(p * dp, axis=1, keepdims=True))
+    dz = p * (dp - rsum(p * dp))
     dz_ref[...] = dz
     z3 = split3(dz)
     part = tn(z3[0], h) + (tn(z3[1], h) + tn(z3[2], h))
@@ -381,16 +397,17 @@
         fetch(names_of(groups, refs[:n_r], 1), w, slots, n_local, info_ref, win_ref, rows_ref)
         return collect_dx(code, w, col, rows_ref)
 
-    x_ref[...] = dx_ref[...] + collect(0)
+    x_ref[...] = dx_ref[...]
 
     def more(w):
         x_ref[...] = x_ref[...] + collect(w)
 
     further(win_ref, more)
+    dx = x_ref[...] + collect(0)
     z_hi, z_lo, _ = split3(dz_ref[...])
     w_hi, w_lo, _ = split3(wt_ref[...])
     back = nn(z_hi, w_hi) + (nn(z_lo, w_hi) + nn(z_hi, w_lo))
-    dh_ref[...] = (d_ref[...].astype(f32) + x_ref[...] + back).astype(bf16)
+    dh_ref[...] = (d_ref[...].astype(f32) + dx + back).astype(bf16)
 
 
 def solution(mesh):
@@ -484,23 +501,24 @@
             )(info, starts, slot_rows, others, wr3, *h_pairs[pair], *d_pairs[pair])
 
         rows = {pair: gather(pair) for pair in h_pairs}
-        row_block = expert_block((2 * slots, d_model))
-        g13, g2 = expert_block((d_model, ff)), expert_block((ff, d_model))
-
-        def grads(first, second, acc):
+
+        def grads(first, second, acc, lo, hi):
             (xa, ca), (xb, cb) = rows[first], rows[second]
+            at = lambda shape: expert_block(shape, lo)
+            g13, g2 = at((d_model, ff)), at((ff, d_model))
             return kernel(
                 functools.partial(grad_kernel, bool(acc)),
-                grid=(n_local,),
-                in_specs=[row_block] * 4 + [expert_block((d_model, 2 * ff)), expert_block((ff, d_model))] + [g13, g13, g2][:len(acc)],
+                grid=(hi - lo,),
+                in_specs=[at((2 * slots, d_model))] * 4 + [at((d_model, 2 * ff)), at((ff, d_model))] + [g13, g13, g2][:len(acc)],
                 out_specs=[g13, g13, g2],
                 out_shape=[sds((n_local, d_model, ff), f32)] * 2 + [sds((n_local, ff, d_model), f32)],
                 input_output_aliases={6 + k: k for k in range(len(acc))},
-                compiler_params=params(), cost_estimate=cost(25e9),
+                compiler_params=params(), cost_estimate=cost(3e9 * (hi - lo)),
             )(xa, xb, ca, cb, w13, w_down, *acc)
 
-        grad = grads((0, 0), (1, 0), ())
-        g_gate, g_up, g_down = grads((0, 1), (1, 1), tuple(grad))
+        grad = grads((0, 0), (1, 0), (), 0, n_local)
+        grad = grads((0, 1), (1, 1), tuple(grad), 0, n_local // 2)
+        g_gate, g_up, g_down = grads((0, 1), (1, 1), tuple(grad), n_local // 2, n_local)
 
         def back(index):
             lo, hi = CHUNKS[index]
@@ -511,13 +529,14 @@
                 grid=(hi - lo,),
                 in_specs=[at((2 * slots, d_model))] * 4 + [at((d_model, 2 * ff)), at((ff, d_model)),
                           expert_block((d_model, 2 * ff)), expert_block((ff, d_model))],
-                out_specs=[expert_block((slots, d_model))] * 8 if index == last else [expert_block((2, slots, d_model))] * 4,
-                out_shape=[sds((hi - lo, slots, d_model), bf16)] * 8 if index == last else [sds((hi - lo, 2, slots, d_model), bf16)] * 4,
+                out_specs=[expert_block((slots, d_model))] * 8 if index >= split else [expert_block((2, slots, d_model))] * 4,
+                out_shape=[sds((hi - lo, slots, d_model), bf16)] * 8 if index >= split else [sds((hi - lo, 2, slots, d_model), bf16)] * 4,
                 compiler_params=params(), cost_estimate=cost(6e9 * (hi - lo)),
             )(xa, xb, ca, cb, w13, w_down, *partner[index])
             return [outs[i] if i % 4 == 0 else permute(outs[i], i % 4, 0) for i in range(len(outs))]
 
         last = len(CHUNKS) - 1
+        split = last - 1
         returned = [back(i) for i in range(len(CHUNKS))]
         total = jnp.sum((near_ids.reshape(-1)[:, None] == jnp.arange(n_experts)[None, :]).astype(f32), axis=0)[None, :]
         coef = (AUX_COEF * n_experts / n_tokens / (2 * n_tokens)) * total
@@ -539,15 +558,15 @@
             combine_kernel, early, [r for i in early for r in returned[i]], (), [],
             [wide] * 3, [sds((tok_rows, d_model), bf16)] * 2 + [sds((tok_rows, d_model), f32)],
             [pltpu.VMEM((2, width(early), d_model), bf16)])
-        ready = [r for i in late[:-1] for r in returned[i]]
+        half = lambda k: [r for i in late for r in (returned[i] if len(returned[i]) == 4 else returned[i][4 * k:4 * k + 4])]
         output, dz, d_rt = token_kernel(
-            final_y_kernel, late, ready + returned[last][:4], (y0, y1, hidden, d_out, probs, coef, stats),
+            final_y_kernel, late, half(0), (y0, y1, hidden, d_out, probs, coef, stats),
             [wide] * 4 + [tokens(n_experts), whole((1, n_experts)), whole((8, 128))],
             [wide, tokens(n_experts), whole((n_experts + 8, d_model))],
             [sds((tok_rows, d_model), bf16), sds((tok_rows, n_experts), f32), sds((n_experts + 8, d_model), f32)],
             [pltpu.VMEM((width(late), d_model), bf16), pltpu.VMEM((2 * TILE, d_model), f32)])
         (d_hidden,) = token_kernel(
-            final_x_kernel, late, ready + returned[last][4:], (dxs, d_out, dz, w_router),
+            final_x_kernel, late, half(1), (dxs, d_out, dz, w_router),
             [wide] * 2 + [tokens(n_experts), whole((d_model, n_experts))],
             [wide], [sds((tok_rows, d_model), bf16)],
             [pltpu.VMEM((width(late), d_model), bf16), pltpu.VMEM((TILE, d_model), f32), pltpu.VMEM((n_experts, d_model), f32)])

time: 768 us -> 782 us (1.018)
  waiting for transfers between devices: 430 us -> 445 us
    ppermute x52 -> x55, waiting for transfers between devices: 430 us -> 445 us  [permute(): return lax.ppermute(v, ('etp', 'ep'), pairs)]
    pallas_call x2 -> x3, Pallas kernels: 54.4 us -> 58.3 us  [grads(): kernel(functools.partial(grad_kernel, bool(acc)), grid=(hi - lo,), in_spe...]
    ppermute x52 -> x55, starting transfers between devices: 46.4 us -> 47.2 us  [permute(): return lax.ppermute(v, ('etp', 'ep'), pairs)]
  transfers between devices with their start and end apart: 52 -> 55, of which waited for: 18 -> 17; matrix products, arithmetic and copies ran while one was open for 4% -> 3% of each run, Pallas kernels for 27% -> 26%
where the time goes in v2:
time: 782 us; the launch traced here: 773 us
  waiting for transfers between devices  445 us (57%)
  Pallas kernels  251 us (32%)
  starting transfers between devices  47.2 us (6%)
  local copies, waits for them, and re-layouts  20.9 us (3%)
    ppermute x55, waiting for transfers between devices, permute(): return lax.ppermute(v, ('etp', 'ep'), pairs)  445 us
    pallas_call x4, Pallas kernels, gather(): kernel(functools.partial(gather_kernel, slots, n_local, n_experts), grid=...  66.9 us
    pallas_call x5, Pallas kernels, back(): kernel(functools.partial(row_kernel, slots), grid=(hi - lo,), in_specs=[a...  58.8 us
    pallas_call x3, Pallas kernels, grads(): kernel(functools.partial(grad_kernel, bool(acc)), grid=(hi - lo,), in_spe...  58.3 us
    ppermute x55, starting transfers between devices, permute(): return lax.ppermute(v, ('etp', 'ep'), pairs)  47.2 us
    pallas_call x3, Pallas kernels, token_kernel(): kernel(functools.partial(body, groups, slots, n_local), grid=(steps,), in...  39.5 us
    pallas_call x1, Pallas kernels, layer(): kernel(functools.partial(slot_kernel, capacity, slots, n_local), grid=(n_...  16.6 us
  transfers between devices with their start and end apart: 55, of which 17 were waited for; matrix products, arithmetic and copies ran while one was open for 3% of the time, Pallas kernels for 26%

profile of v2, /device:TPU:0, one launch (start us, length us, event | category | flops | bytes accessed | tf_op | source)
XLA Modules:
  0.0 773.3 jit_solution(15784378142513360010)
XLA Ops:
  0.6 3.3 collective-permute-start.9
  5.2 1.8 collective-permute-start
  8.4 2.4 constant_dynamic-update-slice_fusion.9
  19.5 1.7 copy.25.wr_ref.refs_15_
  23.5 2.2 collective-permute-done.2
  25.7 1.5 collective-permute-start.3
  27.8 67.3 %collective-permute-done.3 = s32[16,256]{1,0:T(8,128)S(1)} collective-permute-done((s32[16,256]{1,0:T(8,128)S(1)}, s32[16,256]{1,0:T(8,128)S(1)}, u32[]{:S(2)}, u32[]{:S(2)}) %collective-permute-start.3) | collective-permute-done | bytes 16416 | tf_op jit(solution)/shard_map/ppermute | solution.py:424
  95.1 2.7 collective-permute-start.4
  100.3 2.6 collective-permute-done.5
  104.7 2.3 collective-permute-done.6
  107.0 1.9 collective-permute-start.33
  109.5 16.6 %shard_map.127 = (f32[8,64,256]{2,1,0:T(8,128)}, f32[8,8,256]{2,1,0:T(8,128)}, s32[8,8,128]{2,1,0:T(8,128)}, bf16[512,128]{1,0:T(8,128)(2,1)}) custom-call(s32[9]{0:T(128)} %pad_add_fusion.1.info_ref, s32[8,16,256]{2,1,0:T(8,128)} %constant_dynamic-update-slice_fusion.ids_ref, f32[512,32]{1,0:T(8,128)} %copy.25.wr_ref.refs_15_), custom_call_target="tpu_custom_call" | custom-call | flops 5000000000 | bytes 1048576 | tf_op jit(solution)/shard_map/pallas_call | solution.py:467
  126.2 1.9 collective-permute-start.29
  128.1 16.7 %shard_map.128 = (bf16[8,448,512]{2,1,0:T(8,128)(2,1)}, bf16[8,448,512]{2,1,0:T(8,128)(2,1)}) custom-call(s32[3]{0:T(128)} %add_add_fusion.info_ref, s32[8,8,128]{2,1,0:T(8,128)} %get-tuple-element.68.start_ref, f32[8,64,256]{2,1,0:T(8,128)} %get-tuple-element.69.slot_ref, f32[8,8,256]{2,1,0:T(8,128)} %get-tuple-element.70.other_ref, ...), custom_call_target="tpu_custom_call" | custom-call | flops 8000000000 | bytes 1048576 | tf_op jit(solution)/shard_map/pallas_call | solution.py:493
  145.1 1.9 collective-permute-start.19
  146.9 16.7 %shard_map.129 = (bf16[8,448,512]{2,1,0:T(8,128)(2,1)}, bf16[8,448,512]{2,1,0:T(8,128)(2,1)}) custom-call(s32[3]{0:T(128)} %add_add_fusion.1.info_ref, s32[8,8,128]{2,1,0:T(8,128)} %get-tuple-element.68.start_ref, f32[8,64,256]{2,1,0:T(8,128)} %get-tuple-element.69.slot_ref, f32[8,8,256]{2,1,0:T(8,128)} %get-tuple-element.70.other_ref, ...), custom_call_target="tpu_custom_call" | custom-call | flops 8000000000 | bytes 1048576 | tf_op jit(solution)/shard_map/pallas_call | solution.py:493
  163.6 23.0 %collective-permute-done.24.w2p_ref = bf16[1,384,512]{2,1,0:T(8,128)(2,1)} collective-permute-done((bf16[1,384,512]{2,1,0:T(8,128)(2,1)S(1)}, bf16[1,384,512]{2,1,0:T(8,128)(2,1)}, u32[]{:S(2)}, u32[]{:S(2)}) %collective-permute-start.24) | collective-permute-done | bytes 393248 | tf_op jit(solution)/shard_map/ppermute | solution.py:424
  186.7 1.9 collective-permute-start.47
  188.6 6.5 collective-permute-done.19.w2p_ref
  195.1 1.9 collective-permute-start.23
  197.1 1.9 collective-permute-start.28
  199.2 14.3 %shard_map.134 = (bf16[2,2,224,512]{3,2,1,0:T(8,128)(2,1)}, bf16[2,2,224,512]{3,2,1,0:T(8,128)(2,1)}, bf16[2,2,224,512]{3,2,1,0:T(8,128)(2,1)}, bf16[2,2,224,512]{3,2,1,0:T(8,128)(2,1)}) custom-call(bf16[8,448,512]{2,1,0:T(8,128)(2,1)} %get-tuple-element.72.xa_ref, bf16[8,448,512]{2,1,0:T(8,128)(2,1)} %get-tuple-element.73.xb_ref, ...), custom_call_target="tpu_custom_call" | custom-call | flops 12000000000 | bytes 1048576 | tf_op jit(solution)/shard_map/pallas_call | solution.py:527
  213.5 43.4 %collective-permute-done.23.wp_ref = bf16[1,512,768]{2,1,0:T(8,128)(2,1)} collective-permute-done((bf16[1,512,768]{2,1,0:T(8,128)(2,1)}, bf16[1,512,768]{2,1,0:T(8,128)(2,1)}, u32[]{:S(2)}, u32[]{:S(2)}) %collective-permute-start.23) | collective-permute-done | bytes 786464 | tf_op jit(solution)/shard_map/ppermute | solution.py:424
  256.9 1.9 collective-permute-start.49
  258.8 15.0 %collective-permute-done.18.wp_ref = bf16[1,512,768]{2,1,0:T(8,128)(2,1)} collective-permute-done((bf16[1,512,768]{2,1,0:T(8,128)(2,1)}, bf16[1,512,768]{2,1,0:T(8,128)(2,1)}, u32[]{:S(2)}, u32[]{:S(2)}) %collective-permute-start.18) | collective-permute-done | bytes 786464 | tf_op jit(solution)/shard_map/ppermute | solution.py:424
  273.8 1.9 collective-permute-start.14
  275.6 8.2 %shard_map.132 = (bf16[1,224,512]{2,1,0:T(8,128)(2,1)}, bf16[1,224,512]{2,1,0:T(8,128)(2,1)}, bf16[1,224,512]{2,1,0:T(8,128)(2,1)}, bf16[1,224,512]{2,1,0:T(8,12...) custom-call(bf16[8,448,512]{2,1,0:T(8,128)(2,1)} %get-tuple-element., ...), custom_call_target="tpu_custom_call" | custom-call | flops 6000000000 | bytes 1048576 | tf_op jit(solution)/shard_map/pallas_call | solution.py:527
  283.8 8.2 %shard_map.131 = (bf16[1,224,512]{2,1,0:T(8,128)(2,1)}, bf16[1,224,512]{2,1,0:T(8,128)(2,1)}, bf16[1,224,512]{2,1,0:T(8,128)(2,1)}, bf16[1,224,512]{2,1,0:T(8,12...) custom-call(bf16[8,448,512]{2,1,0:T(8,128)(2,1)} %get-tuple-element., ...), custom_call_target="tpu_custom_call" | custom-call | flops 6000000000 | bytes 1048576 | tf_op jit(solution)/shard_map/pallas_call | solution.py:527
  292.1 110.2 %collective-permute-done.14.w2p_ref = bf16[2,384,512]{2,1,0:T(8,128)(2,1)} collective-permute-done((bf16[2,384,512]{2,1,0:T(8,128)(2,1)}, bf16[2,384,512]{2,1,0:T(8,128)(2,1)}, u32[]{:S(2)}, u32[]{:S(2)}) %collective-permute-start.14) | collective-permute-done | bytes 786464 | tf_op jit(solution)/shard_map/ppermute | solution.py:424
  404.5 14.3 %shard_map.133 = (bf16[2,2,224,512]{3,2,1,0:T(8,128)(2,1)}, bf16[2,2,224,512]{3,2,1,0:T(8,128)(2,1)}, bf16[2,2,224,512]{3,2,1,0:T(8,128)(2,1)}, bf16[2,2,224,512]{3,2,1,0:T(8,128)(2,1)}) custom-call(bf16[8,448,512]{2,1,0:T(8,128)(2,1)} %get-tuple-element.72.xa_ref, bf16[8,448,512]{2,1,0:T(8,128)(2,1)} %get-tuple-element.73.xb_ref, ...), custom_call_target="tpu_custom_call" | custom-call | flops 12000000000 | bytes 1048576 | tf_op jit(solution)/shard_map/pallas_call | solution.py:527
  422.4 13.8 %shard_map.130 = (bf16[2,2,224,512]{3,2,1,0:T(8,128)(2,1)}, bf16[2,2,224,512]{3,2,1,0:T(8,128)(2,1)}, bf16[2,2,224,512]{3,2,1,0:T(8,128)(2,1)}, bf16[2,2,224,512]{3,2,1,0:T(8,128)(2,1)}) custom-call(bf16[8,448,512]{2,1,0:T(8,128)(2,1)} %get-tuple-element.72.xa_ref, bf16[8,448,512]{2,1,0:T(8,128)(2,1)} %get-tuple-element.73.xb_ref, ...), custom_call_target="tpu_custom_call" | custom-call | flops 12000000000 | bytes 1048576 | tf_op jit(solution)/shard_map/pallas_call | solution.py:527
  438.4 13.7 %collective-permute-done.36.refs_6_ = bf16[2,2,224,512]{3,2,1,0:T(8,128)(2,1)} collective-permute-done((bf16[2,2,224,512]{3,2,1,0:T(8,128)(2,1)S(1)}, bf16[2,2,224,512]{3,2,1,0:T(8,128)(2,1)}, u32[]{:S(2)}, u32[]{:S(2)}) %collective-permute-start.36) | collective-permute-done | bytes 917536 | tf_op jit(solution)/shard_map/ppermute | solution.py:424
  452.1 18.0 %collective-permute-done.37.refs_7_ = bf16[2,2,224,512]{3,2,1,0:T(8,128)(2,1)} collective-permute-done((bf16[2,2,224,512]{3,2,1,0:T(8,128)(2,1)S(1)}, bf16[2,2,224,512]{3,2,1,0:T(8,128)(2,1)}, u32[]{:S(2)}, u32[]{:S(2)}) %collective-permute-start.37) | collective-permute-done | bytes 917536 | tf_op jit(solution)/shard_map/ppermute | solution.py:424
  473.2 11.0 %shard_map.126 = (f32[2048,32]{1,0:T(8,128)}, f32[2048,128]{1,0:T(8,128)}, s32[8,128]{1,0:T(8,128)}, f32[8,128]{1,0:T(8,128)}) custom-call(s32[4]{0:T(128)} %pad_add_fusion.info_ref, bf16[2048,512]{1,0:T(8,128)(2,1)} %refs_14_.1, f32[512,32]{1,0:T(8,128)} %copy.25.wr_ref.refs_15_, s32[2048,2]{1,0:T(8,128)} %copy.26.ids_ref), custom_call_target="tpu_custom_call" | custom-call | flops 3000000000 | bytes 1048576 | tf_op jit(solution)/shard_map/pallas_call | solution.py:478
  485.2 6.2 collective-permute-done.31.refs_2_
  491.4 18.0 %collective-permute-done.32.refs_3_ = bf16[2,2,224,512]{3,2,1,0:T(8,128)(2,1)} collective-permute-done((bf16[2,2,224,512]{3,2,1,0:T(8,128)(2,1)}, bf16[2,2,224,512]{3,2,1,0:T(8,128)(2,1)}, u32[]{:S(2)}, u32[]{:S(2)}) %collective-permute-start.32) | collective-permute-done | bytes 917536 | tf_op jit(solution)/shard_map/ppermute | solution.py:424
  511.7 19.0 %collective-permute-done.16.refs_2_ = bf16[2,2,224,512]{3,2,1,0:T(8,128)(2,1)} collective-permute-done((bf16[2,2,224,512]{3,2,1,0:T(8,128)(2,1)}, bf16[2,2,224,512]{3,2,1,0:T(8,128)(2,1)}, u32[]{:S(2)}, u32[]{:S(2)}) %collective-permute-start.16) | collective-permute-done | bytes 917536 | tf_op jit(solution)/shard_map/ppermute | solution.py:424
  531.3 12.0 %shard_map.135 = (bf16[2048,512]{1,0:T(8,128)(2,1)}, bf16[2048,512]{1,0:T(8,128)(2,1)}, f32[2048,512]{1,0:T(8,128)}) custom-call(s32[4]{0:T(128)} %pad_add_fusion.info_ref, s32[8,128]{1,0:T(8,128)} %get-tuple-element.66.win_ref, f32[2048,128]{1,0:T(8,128)} %get-tuple-element.67.code_ref, bf16[2,2,224,512]{3,2,1,0:T(8,128)(2,1)} %get-tuple-element.88.refs_0_, ...), custom_call_target="tpu_custom_call" | custom-call | flops 8000000000 | bytes 1048576 | tf_op jit(solution)/shard_map/pallas_call | solution.py:546
  543.3 95.3 %collective-permute-done.17.refs_3_ = bf16[2,2,224,512]{3,2,1,0:T(8,128)(2,1)} collective-permute-done((bf16[2,2,224,512]{3,2,1,0:T(8,128)(2,1)}, bf16[2,2,224,512]{3,2,1,0:T(8,128)(2,1)}, u32[]{:S(2)}, u32[]{:S(2)}) %collective-permute-start.17) | collective-permute-done | bytes 917536 | tf_op jit(solution)/shard_map/ppermute | solution.py:424
  638.6 15.8 %shard_map.136 = (bf16[2048,512]{1,0:T(8,128)(2,1)}, f32[2048,32]{1,0:T(8,128)}, f32[40,512]{1,0:T(8,128)}) custom-call(s32[4]{0:T(128)} %pad_add_fusion.info_ref, s32[8,128]{1,0:T(8,128)} %get-tuple-element.66.win_ref, f32[2048,128]{1,0:T(8,128)} %get-tuple-element.67.code_ref, bf16[2,2,224,512]{3,2,1,0:T(8,128)(2,1)} %get-tuple-element.76.refs_0_, ...), custom_call_target="tpu_custom_call" | custom-call | flops 8000000000 | bytes 1048576 | tf_op jit(solution)/shard_map/pallas_call | solution.py:546
  654.4 1.5 collective-permute-start.44
  662.2 26.7 %shard_map.140 = (f32[8,512,384]{2,1,0:T(8,128)}, f32[8,512,384]{2,1,0:T(8,128)}, f32[8,384,512]{2,1,0:T(8,128)}) custom-call(bf16[8,448,512]{2,1,0:T(8,128)(2,1)} %get-tuple-element.72.xa_ref, bf16[8,448,512]{2,1,0:T(8,128)(2,1)} %get-tuple-element.73.xb_ref, bf16[8,448,512]{2,1,0:T(8,128)(2,1)} %get-tuple-element.74.ca_ref, ...), custom_call_target="tpu_custom_call" | custom-call | flops 24000000000 | bytes 1048576 | tf_op jit(solution)/shard_map/pallas_call | solution.py:509
  689.1 1.7 collective-permute-start.39
  690.8 16.7 %shard_map.138 = (bf16[8,448,512]{2,1,0:T(8,128)(2,1)}, bf16[8,448,512]{2,1,0:T(8,128)(2,1)}) custom-call(s32[3]{0:T(128)} %add_add_fusion.2.info_ref, s32[8,8,128]{2,1,0:T(8,128)} %get-tuple-element.68.start_ref, f32[8,64,256]{2,1,0:T(8,128)} %get-tuple-element.69.slot_ref, f32[8,8,256]{2,1,0:T(8,128)} %get-tuple-element.70.other_ref, ...), custom_call_target="tpu_custom_call" | custom-call | flops 8000000000 | bytes 1048576 | tf_op jit(solution)/shard_map/pallas_call | solution.py:493
  709.8 11.7 %shard_map.137 = bf16[2048,512]{1,0:T(8,128)(2,1)} custom-call(s32[4]{0:T(128)} %pad_add_fusion.info_ref, s32[8,128]{1,0:T(8,128)} %get-tuple-element.66.win_ref, f32[2048,128]{1,0:T(8,128)} %get-tuple-element.67.code_ref, bf16[2,2,224,512]{3,2,1,0:T(8,128)(2,1)} %get-tuple-element.76.refs_0_, bf16[2,2,224,512]{3,2,1,0:T(8,128)(2,1)} %copy-done.7, ...), custom_call_target="tpu_custom_call" | custom-call | flops 8000000000 | bytes 1048576 | tf_op jit(solution)/shard_map/pallas_call | solution.py:546
  723.5 16.8 %shard_map.139 = (bf16[8,448,512]{2,1,0:T(8,128)(2,1)}, bf16[8,448,512]{2,1,0:T(8,128)(2,1)}) custom-call(s32[3]{0:T(128)} %add_add_fusion.3.info_ref, s32[8,8,128]{2,1,0:T(8,128)} %get-tuple-element.68.start_ref, f32[8,64,256]{2,1,0:T(8,128)} %get-tuple-element.69.slot_ref, f32[8,8,256]{2,1,0:T(8,128)} %get-tuple-element.70.other_ref, ...), custom_call_target="tpu_custom_call" | custom-call | flops 8000000000 | bytes 1048576 | tf_op jit(solution)/shard_map/pallas_call | solution.py:493
  740.2 15.7 %shard_map.141 = (f32[8,512,384]{2,1,0:T(8,128)}, f32[8,512,384]{2,1,0:T(8,128)}, f32[8,384,512]{2,1,0:T(8,128)}) custom-call(bf16[8,448,512]{2,1,0:T(8,128)(2,1)} %get-tuple-element.112.xa_ref, bf16[8,448,512]{2,1,0:T(8,128)(2,1)} %get-tuple-element.113.xb_ref, ...), custom_call_target="tpu_custom_call", output_to_operand_aliasing={{0}: (6, {}), {1}: (7, {}), {2}: (8, {})} | custom-call | flops 12000000000 | bytes 1048576 | tf_op jit(solution)/shard_map/pallas_call | solution.py:509
  755.9 15.9 %shard_map.142 = (f32[8,512,384]{2,1,0:T(8,128)}, f32[8,512,384]{2,1,0:T(8,128)}, f32[8,384,512]{2,1,0:T(8,128)}) custom-call(bf16[8,448,512]{2,1,0:T(8,128)(2,1)} %get-tuple-element.112.xa_ref, bf16[8,448,512]{2,1,0:T(8,128)(2,1)} %get-tuple-element.113.xb_ref, ...), custom_call_target="tpu_custom_call", output_to_operand_aliasing={{0}: (6, {}), {1}: (7, {}), {2}: (8, {})} | custom-call | flops 12000000000 | bytes 1048576 | tf_op jit(solution)/shard_map/pallas_call | solution.py:509
  (162 shorter events, 44.6 us)
Async XLA Ops:
  0.6 97.2 %collective-permute-start.9 = (bf16[2048,512]{1,0:T(8,128)(2,1)}, bf16[2048,512]{1,0:T(8,128)(2,1)}, u32[]{:S(2)}, u32[]{:S(2)}) collective-permute-start(bf16[2048,512]{1,0:T(8,128)(2,1)} %refs_14_.1), channel_id=1, source_target_pairs={{0,2},{1,3},{2,0},{3,1},{4,6},{5,7},{6,4},{7,5}} | collective-permute-start | bytes 6291464 | tf_op jit(solution)/shard_map/ppermute | solution.py:424
  4.0 122.1 %collective-permute-start.7 = (bf16[2048,512]{1,0:T(8,128)(2,1)}, bf16[2048,512]{1,0:T(8,128)(2,1)}, u32[]{:S(2)}, u32[]{:S(2)}) collective-permute-start(bf16[2048,512]{1,0:T(8,128)(2,1)} %refs_14_.1), channel_id=1, source_target_pairs={{0,1},{1,0},{2,3},{3,2},{4,5},{5,4},{6,7},{7,6}} | collective-permute-start | bytes 6291464 | tf_op jit(solution)/shard_map/ppermute | solution.py:424
  4.0 93.8 %collective-permute-start.11 = (bf16[2048,512]{1,0:T(8,128)(2,1)}, bf16[2048,512]{1,0:T(8,128)(2,1)}, u32[]{:S(2)}, u32[]{:S(2)}) collective-permute-start(bf16[2048,512]{1,0:T(8,128)(2,1)} %refs_13_.1), channel_id=1, source_target_pairs={{0,2},{1,3},{2,0},{3,1},{4,6},{5,7},{6,4},{7,5}} | collective-permute-start | bytes 6291464 | tf_op jit(solution)/shard_map/ppermute | solution.py:424
  4.0 122.2 %collective-permute-start.8 = (bf16[2048,512]{1,0:T(8,128)(2,1)}, bf16[2048,512]{1,0:T(8,128)(2,1)}, u32[]{:S(2)}, u32[]{:S(2)}) collective-permute-start(bf16[2048,512]{1,0:T(8,128)(2,1)} %refs_13_.1), channel_id=1, source_target_pairs={{0,1},{1,0},{2,3},{3,2},{4,5},{5,4},{6,7},{7,6}} | collective-permute-start | bytes 6291464 | tf_op jit(solution)/shard_map/ppermute | solution.py:424
  5.2 16.0 %collective-permute-start = (s32[16,256]{1,0:T(8,128)S(1)}, s32[16,256]{1,0:T(8,128)}, u32[]{:S(2)}, u32[]{:S(2)}) collective-permute-start(s32[16,256]{1,0:T(8,128)S(1)} %reshape.34), channel_id=1, source_target_pairs={{0,4},{1,5},{2,6},{3,7},{4,0},{5,1},{6,2},{7,3}} | collective-permute-start | bytes 49160 | tf_op jit(solution)/shard_map/ppermute | solution.py:424
  25.7 69.4 %collective-permute-start.3 = (s32[16,256]{1,0:T(8,128)S(1)}, s32[16,256]{1,0:T(8,128)S(1)}, u32[]{:S(2)}, u32[]{:S(2)}) collective-permute-start(s32[16,256]{1,0:T(8,128)S(1)} %reshape.34), channel_id=1, source_target_pairs={{0,2},{1,3},{2,0},{3,1},{4,6},{5,7},{6,4},{7,5}} | collective-permute-start | bytes 49160 | tf_op jit(solution)/shard_map/ppermute | solution.py:424
  97.8 47.1 %collective-permute-start.10 = (bf16[2048,512]{1,0:T(8,128)(2,1)}, bf16[2048,512]{1,0:T(8,128)(2,1)}, u32[]{:S(2)}, u32[]{:S(2)}) collective-permute-start(bf16[2048,512]{1,0:T(8,128)(2,1)} %collective-permute-done.9.ha_ref), channel_id=1, source_target_pairs={{0,1},{1,0},{2,3},{3,2},{4,5},{5,4},{6,7},{7,6}} | collective-permute-start | bytes 6291464 | tf_op jit(solution)/shard_map/ppermute | solution.py:424
  97.8 47.3 %collective-permute-start.12 = (bf16[2048,512]{1,0:T(8,128)(2,1)}, bf16[2048,512]{1,0:T(8,128)(2,1)}, u32[]{:S(2)}, u32[]{:S(2)}) collective-permute-start(bf16[2048,512]{1,0:T(8,128)(2,1)} %collective-permute-done.11.da_ref), channel_id=1, source_target_pairs={{0,1},{1,0},{2,3},{3,2},{4,5},{5,4},{6,7},{7,6}} | collective-permute-start | bytes 6291464 | tf_op jit(solution)/shard_map/ppermute | solution.py:424
  107.0 92.1 %collective-permute-start.33 = (bf16[2,512,768]{2,1,0:T(8,128)(2,1)}, bf16[2,512,768]{2,1,0:T(8,128)(2,1)}, u32[]{:S(2)}, u32[]{:S(2)}) collective-permute-start(bf16[2,512,768]{2,1,0:T(8,128)(2,1)} %get-tuple-element.125), channel_id=1, source_target_pairs={{0,4},{1,5},{2,6},{3,7},{4,0},{5,1},{6,2},{7,3}} | collective-permute-start | bytes 4718600 | tf_op jit(solution)/shard_map/ppermute | solution.py:424
  126.1 70.9 %collective-permute-start.34 = (bf16[2,384,512]{2,1,0:T(8,128)(2,1)}, bf16[2,384,512]{2,1,0:T(8,128)(2,1)}, u32[]{:S(2)}, u32[]{:S(2)}) collective-permute-start(bf16[2,384,512]{2,1,0:T(8,128)(2,1)} %get-tuple-element.130), channel_id=1, source_target_pairs={{0,4},{1,5},{2,6},{3,7},{4,0},{5,1},{6,2},{7,3}} | collective-permute-start | bytes 2359304 | tf_op jit(solution)/shard_map/ppermute | solution.py:424
  126.2 70.9 %collective-permute-start.29 = (bf16[2,384,512]{2,1,0:T(8,128)(2,1)}, bf16[2,384,512]{2,1,0:T(8,128)(2,1)}, u32[]{:S(2)}, u32[]{:S(2)}) collective-permute-start(bf16[2,384,512]{2,1,0:T(8,128)(2,1)} %get-tuple-element.131), channel_id=1, source_target_pairs={{0,4},{1,5},{2,6},{3,7},{4,0},{5,1},{6,2},{7,3}} | collective-permute-start | bytes 2359304 | tf_op jit(solution)/shard_map/ppermute | solution.py:424
  144.9 41.8 %collective-permute-start.24 = (bf16[1,384,512]{2,1,0:T(8,128)(2,1)S(1)}, bf16[1,384,512]{2,1,0:T(8,128)(2,1)}, u32[]{:S(2)}, u32[]{:S(2)}) collective-permute-start(bf16[1,384,512]{2,1,0:T(8,128)(2,1)S(1)} %copy-done.3), channel_id=1, source_target_pairs={{0,4},{1,5},{2,6},{3,7},{4,0},{5,1},{6,2},{7,3}} | collective-permute-start | bytes 1179656 | tf_op jit(solution)/shard_map/ppermute | solution.py:424
  145.1 50.1 %collective-permute-start.19 = (bf16[1,384,512]{2,1,0:T(8,128)(2,1)S(1)}, bf16[1,384,512]{2,1,0:T(8,128)(2,1)}, u32[]{:S(2)}, u32[]{:S(2)}) collective-permute-start(bf16[1,384,512]{2,1,0:T(8,128)(2,1)S(1)} %get-tuple-element.134), channel_id=1, source_target_pairs={{0,4},{1,5},{2,6},{3,7},{4,0},{5,1},{6,2},{7,3}} | collective-permute-start | bytes 1179656 | tf_op jit(solution)/shard_map/ppermute | solution.py:424
  186.7 217.5 %collective-permute-start.47 = (bf16[2048,512]{1,0:T(8,128)(2,1)}, bf16[2048,512]{1,0:T(8,128)(2,1)}, u32[]{:S(2)}, u32[]{:S(2)}) collective-permute-start(bf16[2048,512]{1,0:T(8,128)(2,1)} %refs_14_.1), channel_id=1, source_target_pairs={{0,4},{1,5},{2,6},{3,7},{4,0},{5,1},{6,2},{7,3}} | collective-permute-start | bytes 6291464 | tf_op jit(solution)/shard_map/ppermute | solution.py:424
  195.1 61.8 %collective-permute-start.23 = (bf16[1,512,768]{2,1,0:T(8,128)(2,1)}, bf16[1,512,768]{2,1,0:T(8,128)(2,1)}, u32[]{:S(2)}, u32[]{:S(2)}) collective-permute-start(bf16[1,512,768]{2,1,0:T(8,128)(2,1)} %get-tuple-element.128), channel_id=1, source_target_pairs={{0,4},{1,5},{2,6},{3,7},{4,0},{5,1},{6,2},{7,3}} | collective-permute-start | bytes 2359304 | tf_op jit(solution)/shard_map/ppermute | solution.py:424
  197.0 76.7 %collective-permute-start.18 = (bf16[1,512,768]{2,1,0:T(8,128)(2,1)}, bf16[1,512,768]{2,1,0:T(8,128)(2,1)}, u32[]{:S(2)}, u32[]{:S(2)}) collective-permute-start(bf16[1,512,768]{2,1,0:T(8,128)(2,1)} %get-tuple-element.129), channel_id=1, source_target_pairs={{0,4},{1,5},{2,6},{3,7},{4,0},{5,1},{6,2},{7,3}} | collective-permute-start | bytes 2359304 | tf_op jit(solution)/shard_map/ppermute | solution.py:424
  197.1 205.1 %collective-permute-start.28 = (bf16[2,512,768]{2,1,0:T(8,128)(2,1)S(1)}, bf16[2,512,768]{2,1,0:T(8,128)(2,1)}, u32[]{:S(2)}, u32[]{:S(2)}) collective-permute-start(bf16[2,512,768]{2,1,0:T(8,128)(2,1)S(1)} %get-tuple-element.126), channel_id=1, source_target_pairs={{0,4},{1,5},{2,6},{3,7},{4,0},{5,1},{6,2},{7,3}} | collective-permute-start | bytes 4718600 | tf_op jit(solution)/shard_map/ppermute | solution.py:424
  199.0 203.8 %collective-permute-start.13 = (bf16[2,512,768]{2,1,0:T(8,128)(2,1)S(1)}, bf16[2,512,768]{2,1,0:T(8,128)(2,1)}, u32[]{:S(2)}, u32[]{:S(2)}) collective-permute-start(bf16[2,512,768]{2,1,0:T(8,128)(2,1)S(1)} %get-tuple-element.127), channel_id=1, source_target_pairs={{0,4},{1,5},{2,6},{3,7},{4,0},{5,1},{6,2},{7,3}} | collective-permute-start | bytes 4718600 | tf_op jit(solution)/shard_map/ppermute | solution.py:424
  256.9 161.8 %collective-permute-start.49 = (bf16[2048,512]{1,0:T(8,128)(2,1)}, bf16[2048,512]{1,0:T(8,128)(2,1)}, u32[]{:S(2)}, u32[]{:S(2)}) collective-permute-start(bf16[2048,512]{1,0:T(8,128)(2,1)} %refs_13_.1), channel_id=1, source_target_pairs={{0,4},{1,5},{2,6},{3,7},{4,0},{5,1},{6,2},{7,3}} | collective-permute-start | bytes 6291464 | tf_op jit(solution)/shard_map/ppermute | solution.py:424
  273.8 128.5 %collective-permute-start.14 = (bf16[2,384,512]{2,1,0:T(8,128)(2,1)}, bf16[2,384,512]{2,1,0:T(8,128)(2,1)}, u32[]{:S(2)}, u32[]{:S(2)}) collective-permute-start(bf16[2,384,512]{2,1,0:T(8,128)(2,1)} %get-tuple-element.132), channel_id=1, source_target_pairs={{0,4},{1,5},{2,6},{3,7},{4,0},{5,1},{6,2},{7,3}} | collective-permute-start | bytes 2359304 | tf_op jit(solution)/shard_map/ppermute | solution.py:424
  402.3 17.0 %collective-permute-start.25 = (bf16[1,224,512]{2,1,0:T(8,128)(2,1)}, bf16[1,224,512]{2,1,0:T(8,128)(2,1)S(1)}, u32[]{:S(2)}, u32[]{:S(2)}) collective-permute-start(bf16[1,224,512]{2,1,0:T(8,128)(2,1)} %get-tuple-element.85), channel_id=1, source_target_pairs={{0,1},{1,0},{2,3},{3,2},{4,5},{5,4},{6,7},{7,6}} | collective-permute-start | bytes 688136 | tf_op jit(solution)/shard_map/ppermute | solution.py:424
  402.3 18.0 %collective-permute-start.26 = (bf16[1,224,512]{2,1,0:T(8,128)(2,1)}, bf16[1,224,512]{2,1,0:T(8,128)(2,1)S(1)}, u32[]{:S(2)}, u32[]{:S(2)}) collective-permute-start(bf16[1,224,512]{2,1,0:T(8,128)(2,1)} %get-tuple-element.86), channel_id=1, source_target_pairs={{0,2},{1,3},{2,0},{3,1},{4,6},{5,7},{6,4},{7,5}} | collective-permute-start | bytes 688136 | tf_op jit(solution)/shard_map/ppermute | solution.py:424
  402.8 18.1 %collective-permute-start.27 = (bf16[1,224,512]{2,1,0:T(8,128)(2,1)}, bf16[1,224,512]{2,1,0:T(8,128)(2,1)S(1)}, u32[]{:S(2)}, u32[]{:S(2)}) collective-permute-start(bf16[1,224,512]{2,1,0:T(8,128)(2,1)} %get-tuple-element.87), channel_id=1, source_target_pairs={{0,3},{1,2},{2,1},{3,0},{4,7},{5,6},{6,5},{7,4}} | collective-permute-start | bytes 688136 | tf_op jit(solution)/shard_map/ppermute | solution.py:424
  404.1 17.3 %collective-permute-start.20 = (bf16[1,224,512]{2,1,0:T(8,128)(2,1)}, bf16[1,224,512]{2,1,0:T(8,128)(2,1)S(1)}, u32[]{:S(2)}, u32[]{:S(2)}) collective-permute-start(bf16[1,224,512]{2,1,0:T(8,128)(2,1)} %get-tuple-element.81), channel_id=1, source_target_pairs={{0,1},{1,0},{2,3},{3,2},{4,5},{5,4},{6,7},{7,6}} | collective-permute-start | bytes 688136 | tf_op jit(solution)/shard_map/ppermute | solution.py:424
  418.7 17.5 %collective-permute-start.21 = (bf16[1,224,512]{2,1,0:T(8,128)(2,1)}, bf16[1,224,512]{2,1,0:T(8,128)(2,1)S(1)}, u32[]{:S(2)}, u32[]{:S(2)}) collective-permute-start(bf16[1,224,512]{2,1,0:T(8,128)(2,1)} %get-tuple-element.82), channel_id=1, source_target_pairs={{0,2},{1,3},{2,0},{3,1},{4,6},{5,7},{6,4},{7,5}} | collective-permute-start | bytes 688136 | tf_op jit(solution)/shard_map/ppermute | solution.py:424
  419.3 17.7 %collective-permute-start.22 = (bf16[1,224,512]{2,1,0:T(8,128)(2,1)}, bf16[1,224,512]{2,1,0:T(8,128)(2,1)}, u32[]{:S(2)}, u32[]{:S(2)}) collective-permute-start(bf16[1,224,512]{2,1,0:T(8,128)(2,1)} %get-tuple-element.83), channel_id=1, source_target_pairs={{0,3},{1,2},{2,1},{3,0},{4,7},{5,6},{6,5},{7,4}} | collective-permute-start | bytes 688136 | tf_op jit(solution)/shard_map/ppermute | solution.py:424
  420.2 17.3 %collective-permute-start.35 = (bf16[2,2,224,512]{3,2,1,0:T(8,128)(2,1)S(1)}, bf16[2,2,224,512]{3,2,1,0:T(8,128)(2,1)}, u32[]{:S(2)}, u32[]{:S(2)}) collective-permute-start(bf16[2,2,224,512]{3,2,1,0:T(8,128)(2,1)S(1)} %copy-done.10), channel_id=1, source_target_pairs={{0,1},{1,0},{2,3},{3,2},{4,5},{5,4},{6,7},{7,6}} | collective-permute-start | bytes 2752520 | tf_op jit(solution)/shard_map/ppermute | solution.py:424
  420.9 31.2 %collective-permute-start.36 = (bf16[2,2,224,512]{3,2,1,0:T(8,128)(2,1)S(1)}, bf16[2,2,224,512]{3,2,1,0:T(8,128)(2,1)}, u32[]{:S(2)}, u32[]{:S(2)}) collective-permute-start(bf16[2,2,224,512]{3,2,1,0:T(8,128)(2,1)S(1)} %copy-done.9), channel_id=1, source_target_pairs={{0,2},{1,3},{2,0},{3,1},{4,6},{5,7},{6,4},{7,5}} | collective-permute-start | bytes 2752520 | tf_op jit(solution)/shard_map/ppermute | solution.py:424
  421.5 48.6 %collective-permute-start.37 = (bf16[2,2,224,512]{3,2,1,0:T(8,128)(2,1)S(1)}, bf16[2,2,224,512]{3,2,1,0:T(8,128)(2,1)}, u32[]{:S(2)}, u32[]{:S(2)}) collective-permute-start(bf16[2,2,224,512]{3,2,1,0:T(8,128)(2,1)S(1)} %copy-done.8), channel_id=1, source_target_pairs={{0,3},{1,2},{2,1},{3,0},{4,7},{5,6},{6,5},{7,4}} | collective-permute-start | bytes 2752520 | tf_op jit(solution)/shard_map/ppermute | solution.py:424
  436.2 48.1 %collective-permute-start.30 = (bf16[2,2,224,512]{3,2,1,0:T(8,128)(2,1)}, bf16[2,2,224,512]{3,2,1,0:T(8,128)(2,1)}, u32[]{:S(2)}, u32[]{:S(2)}) collective-permute-start(bf16[2,2,224,512]{3,2,1,0:T(8,128)(2,1)} %get-tuple-element.89), channel_id=1, source_target_pairs={{0,1},{1,0},{2,3},{3,2},{4,5},{5,4},{6,7},{7,6}} | collective-permute-start | bytes 2752520 | tf_op jit(solution)/shard_map/ppermute | solution.py:424
  437.0 54.4 %collective-permute-start.31 = (bf16[2,2,224,512]{3,2,1,0:T(8,128)(2,1)}, bf16[2,2,224,512]{3,2,1,0:T(8,128)(2,1)}, u32[]{:S(2)}, u32[]{:S(2)}) collective-permute-start(bf16[2,2,224,512]{3,2,1,0:T(8,128)(2,1)} %get-tuple-element.90), channel_id=1, source_target_pairs={{0,2},{1,3},{2,0},{3,1},{4,6},{5,7},{6,4},{7,5}} | collective-permute-start | bytes 2752520 | tf_op jit(solution)/shard_map/ppermute | solution.py:424
  437.5 71.9 %collective-permute-start.32 = (bf16[2,2,224,512]{3,2,1,0:T(8,128)(2,1)}, bf16[2,2,224,512]{3,2,1,0:T(8,128)(2,1)}, u32[]{:S(2)}, u32[]{:S(2)}) collective-permute-start(bf16[2,2,224,512]{3,2,1,0:T(8,128)(2,1)} %get-tuple-element.91), channel_id=1, source_target_pairs={{0,3},{1,2},{2,1},{3,0},{4,7},{5,6},{6,5},{7,4}} | collective-permute-start | bytes 2752520 | tf_op jit(solution)/shard_map/ppermute | solution.py:424
  452.1 58.5 %collective-permute-start.15 = (bf16[2,2,224,512]{3,2,1,0:T(8,128)(2,1)}, bf16[2,2,224,512]{3,2,1,0:T(8,128)(2,1)S(1)}, u32[]{:S(2)}, u32[]{:S(2)}) collective-permute-start(bf16[2,2,224,512]{3,2,1,0:T(8,128)(2,1)} %get-tuple-element.77), channel_id=1, source_target_pairs={{0,1},{1,0},{2,3},{3,2},{4,5},{5,4},{6,7},{7,6}} | collective-permute-start | bytes 2752520 | tf_op jit(solution)/shard_map/ppermute | solution.py:424
  470.1 60.7 %collective-permute-start.16 = (bf16[2,2,224,512]{3,2,1,0:T(8,128)(2,1)}, bf16[2,2,224,512]{3,2,1,0:T(8,128)(2,1)}, u32[]{:S(2)}, u32[]{:S(2)}) collective-permute-start(bf16[2,2,224,512]{3,2,1,0:T(8,128)(2,1)} %get-tuple-element.78), channel_id=1, source_target_pairs={{0,2},{1,3},{2,0},{3,1},{4,6},{5,7},{6,4},{7,5}} | collective-permute-start | bytes 2752520 | tf_op jit(solution)/shard_map/ppermute | solution.py:424
  484.3 175.2 %collective-permute-start.51 = (bf16[2048,512]{1,0:T(8,128)(2,1)}, bf16[2048,512]{1,0:T(8,128)(2,1)S(1)}, u32[]{:S(2)}, u32[]{:S(2)}) collective-permute-start(bf16[2048,512]{1,0:T(8,128)(2,1)} %collective-permute-done.47.ha_ref), channel_id=1, source_target_pairs={{0,2},{1,3},{2,0},{3,1},{4,6},{5,7},{6,4},{7,5}} | collective-permute-start | bytes 6291464 | tf_op jit(solution)/shard_map/ppermute | solution.py:424
  491.4 168.2 %collective-permute-start.48 = (bf16[2048,512]{1,0:T(8,128)(2,1)}, bf16[2048,512]{1,0:T(8,128)(2,1)}, u32[]{:S(2)}, u32[]{:S(2)}) collective-permute-start(bf16[2048,512]{1,0:T(8,128)(2,1)} %collective-permute-done.47.ha_ref), channel_id=1, source_target_pairs={{0,1},{1,0},{2,3},{3,2},{4,5},{5,4},{6,7},{7,6}} | collective-permute-start | bytes 6291464 | tf_op jit(solution)/shard_map/ppermute | solution.py:424
  509.4 151.7 %collective-permute-start.53 = (bf16[2048,512]{1,0:T(8,128)(2,1)}, bf16[2048,512]{1,0:T(8,128)(2,1)}, u32[]{:S(2)}, u32[]{:S(2)}) collective-permute-start(bf16[2048,512]{1,0:T(8,128)(2,1)} %collective-permute-done.49.da_ref), channel_id=1, source_target_pairs={{0,2},{1,3},{2,0},{3,1},{4,6},{5,7},{6,4},{7,5}} | collective-permute-start | bytes 6291464 | tf_op jit(solution)/shard_map/ppermute | solution.py:424
  510.6 151.1 %collective-permute-start.50 = (bf16[2048,512]{1,0:T(8,128)(2,1)}, bf16[2048,512]{1,0:T(8,128)(2,1)}, u32[]{:S(2)}, u32[]{:S(2)}) collective-permute-start(bf16[2048,512]{1,0:T(8,128)(2,1)} %collective-permute-done.49.da_ref), channel_id=1, source_target_pairs={{0,1},{1,0},{2,3},{3,2},{4,5},{5,4},{6,7},{7,6}} | collective-permute-start | bytes 6291464 | tf_op jit(solution)/shard_map/ppermute | solution.py:424
  530.8 107.8 %collective-permute-start.17 = (bf16[2,2,224,512]{3,2,1,0:T(8,128)(2,1)}, bf16[2,2,224,512]{3,2,1,0:T(8,128)(2,1)}, u32[]{:S(2)}, u32[]{:S(2)}) collective-permute-start(bf16[2,2,224,512]{3,2,1,0:T(8,128)(2,1)} %get-tuple-element.79), channel_id=1, source_target_pairs={{0,3},{1,2},{2,1},{3,0},{4,7},{5,6},{6,5},{7,4}} | collective-permute-start | bytes 2752520 | tf_op jit(solution)/shard_map/ppermute | solution.py:424
  659.5 29.4 %collective-permute-start.42 = (bf16[1,224,512]{2,1,0:T(8,128)(2,1)S(1)}, bf16[1,224,512]{2,1,0:T(8,128)(2,1)}, u32[]{:S(2)}, u32[]{:S(2)}) collective-permute-start(bf16[1,224,512]{2,1,0:T(8,128)(2,1)S(1)} %copy-done.15), channel_id=1, source_target_pairs={{0,2},{1,3},{2,0},{3,1},{4,6},{5,7},{6,4},{7,5}} | collective-permute-start | bytes 688136 | tf_op jit(solution)/shard_map/ppermute | solution.py:424
  659.6 29.4 %collective-permute-start.43 = (bf16[1,224,512]{2,1,0:T(8,128)(2,1)S(1)}, bf16[1,224,512]{2,1,0:T(8,128)(2,1)}, u32[]{:S(2)}, u32[]{:S(2)}) collective-permute-start(bf16[1,224,512]{2,1,0:T(8,128)(2,1)S(1)} %copy-done.14), channel_id=1, source_target_pairs={{0,3},{1,2},{2,1},{3,0},{4,7},{5,6},{6,5},{7,4}} | collective-permute-start | bytes 688136 | tf_op jit(solution)/shard_map/ppermute | solution.py:424
  661.1 62.3 %collective-permute-start.52 = (bf16[2048,512]{1,0:T(8,128)(2,1)S(1)}, bf16[2048,512]{1,0:T(8,128)(2,1)}, u32[]{:S(2)}, u32[]{:S(2)}) collective-permute-start(bf16[2048,512]{1,0:T(8,128)(2,1)S(1)} %collective-permute-done.51.ha_ref), channel_id=1, source_target_pairs={{0,1},{1,0},{2,3},{3,2},{4,5},{5,4},{6,7},{7,6}} | collective-permute-start | bytes 6291464 | tf_op jit(solution)/shard_map/ppermute | solution.py:424
  661.8 61.7 %collective-permute-start.54 = (bf16[2048,512]{1,0:T(8,128)(2,1)}, bf16[2048,512]{1,0:T(8,128)(2,1)}, u32[]{:S(2)}, u32[]{:S(2)}) collective-permute-start(bf16[2048,512]{1,0:T(8,128)(2,1)} %collective-permute-done.53.da_ref), channel_id=1, source_target_pairs={{0,1},{1,0},{2,3},{3,2},{4,5},{5,4},{6,7},{7,6}} | collective-permute-start | bytes 6291464 | tf_op jit(solution)/shard_map/ppermute | solution.py:424
  661.8 29.0 %collective-permute-start.45 = (f32[40,512]{1,0:T(8,128)S(1)}, f32[40,512]{1,0:T(8,128)S(1)}, u32[]{:S(2)}, u32[]{:S(2)}) collective-permute-start(f32[40,512]{1,0:T(8,128)S(1)} %add.38), channel_id=1, source_target_pairs={{0,2},{1,3},{2,0},{3,1},{4,6},{5,7},{6,4},{7,5}} | collective-permute-start | bytes 245768 | tf_op jit(solution)/shard_map/ppermute | solution.py:424
  688.9 18.6 %collective-permute-start.38 = (bf16[1,224,512]{2,1,0:T(8,128)(2,1)S(1)}, bf16[1,224,512]{2,1,0:T(8,128)(2,1)S(1)}, u32[]{:S(2)}, u32[]{:S(2)}) collective-permute-start(bf16[1,224,512]{2,1,0:T(8,128)(2,1)S(1)} %copy-done.13), channel_id=1, source_target_pairs={{0,1},{1,0},{2,3},{3,2},{4,5},{5,4},{6,7},{7,6}} | collective-permute-start | bytes 688136 | tf_op jit(solution)/shard_map/ppermute | solution.py:424
  689.1 20.0 %collective-permute-start.39 = (bf16[1,224,512]{2,1,0:T(8,128)(2,1)S(1)}, bf16[1,224,512]{2,1,0:T(8,128)(2,1)S(1)}, u32[]{:S(2)}, u32[]{:S(2)}) collective-permute-start(bf16[1,224,512]{2,1,0:T(8,128)(2,1)S(1)} %copy-done.12), channel_id=1, source_target_pairs={{0,2},{1,3},{2,0},{3,1},{4,6},{5,7},{6,4},{7,5}} | collective-permute-start | bytes 688136 | tf_op jit(solution)/shard_map/ppermute | solution.py:424
  690.8 18.2 %collective-permute-start.40 = (bf16[1,224,512]{2,1,0:T(8,128)(2,1)S(1)}, bf16[1,224,512]{2,1,0:T(8,128)(2,1)S(1)}, u32[]{:S(2)}, u32[]{:S(2)}) collective-permute-start(bf16[1,224,512]{2,1,0:T(8,128)(2,1)S(1)} %copy-done.11), channel_id=1, source_target_pairs={{0,3},{1,2},{2,1},{3,0},{4,7},{5,6},{6,5},{7,4}} | collective-permute-start | bytes 688136 | tf_op jit(solution)/shard_map/ppermute | solution.py:424
  707.6 14.0 %collective-permute-start.46 = (f32[40,512]{1,0:T(8,128)S(1)}, f32[40,512]{1,0:T(8,128)S(1)}, u32[]{:S(2)}, u32[]{:S(2)}) collective-permute-start(f32[40,512]{1,0:T(8,128)S(1)} %add.39), channel_id=1, source_target_pairs={{0,4},{1,5},{2,6},{3,7},{4,0},{5,1},{6,2},{7,3}} | collective-permute-start | bytes 245768 | tf_op jit(solution)/shard_map/ppermute | solution.py:424
  (32 other events, 488.7 us)

commit v3 on v2

--- a/solution.py
+++ b/solution.py
@@ -8,10 +8,12 @@
 
 AUX_COEF = 0.01
 OUT_SCALE = 2.0
-CHUNKS = ((0, 2), (2, 4), (4, 6), (6, 7), (7, 8))
+SIZES = (2, 2, 1, 1, 1, 1)
+CHUNKS = tuple((sum(SIZES[:i]), sum(SIZES[:i]) + n) for i, n in enumerate(SIZES))
 
 f32, bf16 = jnp.float32, jnp.bfloat16
 TILE = 256
+GROUP = 2
 WIN = 48
 
 
@@ -36,6 +38,10 @@
 
 def ind(mask):
     return jnp.where(mask, 1.0, 0.0).astype(f32)
+
+
+def keep(mask, v):
+    return jnp.where(mask, v, 0.0)
 
 
 def rsum(v):
@@ -78,7 +84,7 @@
     p_ref[...] = p
     ids = ids_ref[...]
     lane = iota((TILE, n_experts), 1)
-    e0, e1 = ids[:, 0:1], ids[:, 1:2]
+    e0, e1 = cols(ids, 0, 1)
     m0, m1 = lane == e0, lane == e1
     hist = ind(m0 | m1)
     before = (iota((TILE, TILE), 1) < iota((TILE, TILE), 0)).astype(f32).astype(bf16)
@@ -87,7 +93,7 @@
     start = jnp.floor(seen * (1.0 / 16)) * 16
     n_win = jnp.max(jnp.floor((after - start + (WIN - 1)) * (1.0 / WIN) + 1e-3), axis=1, keepdims=True)
     rank = nn(before, hist.astype(bf16)) + seen
-    pick = lambda m, v: rsum(jnp.where(m, v, 0.0))
+    pick = lambda m, v: rsum(keep(m, v))
     p0, p1 = pick(m0, p), pick(m1, p)
     s = p0 + p1
     wide = iota((TILE, 128), 1)
@@ -133,9 +139,9 @@
         slot_ref[0, i * n_local:(i + 1) * n_local, :] = jnp.where(m0 | m1, rank, -1.0)
         starts = jnp.where(lane == i, carry, starts)
         for m, e in ((m0, e1), (m1, e0)):
-            pos = csum(jnp.where(m, rank + 1.0, 0.0)) - 1.0
+            pos = csum(keep(m, rank + 1.0)) - 1.0
             one = ind(row == pos).astype(bf16)
-            other = other + nt(jnp.where(m, e.astype(f32), 0.0).astype(bf16), one)
+            other = other + nt(keep(m, e.astype(f32)).astype(bf16), one)
         carry = carry + rsum(hit)
     other_ref[0] = other
     prefix = total_ref[:, 0:1]
@@ -148,54 +154,67 @@
 def gather_kernel(slots, n_local, n_experts, info_ref, start_ref, slot_ref, other_ref, wr3_ref, ha_ref, hb_ref, da_ref, db_ref,
                   x_ref, c_ref, m_ref, xs_ref, ds_ref):
     step = pl.program_id(0)
-    steps = pl.num_programs(0) - n_local
+    group = x_ref.shape[0]
+    steps = pl.num_programs(0) - n_local // group
 
     @pl.when(step < steps)
     def _():
         row = iota((WIN, TILE), 0)
-        for b, (h_ref, d_ref) in enumerate(((ha_ref, da_ref), (hb_ref, db_ref))):
-            j = info_ref[b]
-            first = [(start_ref[j, e, step] // 16) * 16 for e in range(n_local)]
-            span = functools.reduce(jnp.maximum, [start_ref[j, e, step + 1] - first[e] for e in range(n_local)])
-
-            def window(w, carry):
-                for e in range(n_local):
-                    slot = slot_ref[j, pl.ds(step * n_local + e, 1), :]
-                    hit = (row + (first[e] + w * WIN)).astype(f32) == slot
-                    m_ref[e * WIN:(e + 1) * WIN, :] = ind(hit).astype(bf16)
-                m = m_ref[...]
-                for src, dst in ((h_ref, xs_ref), (d_ref, ds_ref)):
-                    r = nn(m, src[...]).astype(bf16)
+
+        def one_tile(sub, carry):
+            tile = step * group + sub
+            part = pl.ds(pl.multiple_of(sub * TILE, TILE), TILE)
+            for b, (h_ref, d_ref) in enumerate(((ha_ref, da_ref), (hb_ref, db_ref))):
+                j = info_ref[b]
+                first = [(start_ref[j, e, tile] // 16) * 16 for e in range(n_local)]
+                span = functools.reduce(jnp.maximum, [start_ref[j, e, tile + 1] - first[e] for e in range(n_local)])
+
+                def window(w, carry):
                     for e in range(n_local):
-                        at = pl.multiple_of(jnp.minimum(first[e] + w * WIN, slots + 16), 16)
-                        old = dst[b, e, pl.ds(at, 16), :]
-                        keep = iota((16, 1), 0) + at < start_ref[j, e, step]
-                        head = r[e * WIN:e * WIN + 16].astype(f32)
-                        dst[b, e, pl.ds(at, 16), :] = jnp.where(keep, old.astype(f32), head).astype(bf16)
-                        dst[b, e, pl.ds(pl.multiple_of(at + 16, 16), WIN - 16), :] = r[e * WIN + 16:(e + 1) * WIN]
-                return carry
-
-            lax.fori_loop(0, (span + WIN - 1) // WIN, window, 0)
+                        slot = slot_ref[j, pl.ds(tile * n_local + e, 1), :]
+                        hit = (row + (first[e] + w * WIN)).astype(f32) == slot
+                        m_ref[e * WIN:(e + 1) * WIN, :] = ind(hit).astype(bf16)
+                    m = m_ref[...]
+                    for src, dst in ((h_ref, xs_ref), (d_ref, ds_ref)):
+                        r = nn(m, src[part, :]).astype(bf16)
+                        for e in range(n_local):
+                            at = pl.multiple_of(jnp.minimum(first[e] + w * WIN, slots + 16), 16)
+                            old = dst[b, e, pl.ds(at, 16), :]
+                            older = iota((16, 1), 0) + at < start_ref[j, e, tile]
+                            head = r[e * WIN:e * WIN + 16].astype(f32)
+                            dst[b, e, pl.ds(at, 16), :] = jnp.where(older, old.astype(f32), head).astype(bf16)
+                            dst[b, e, pl.ds(pl.multiple_of(at + 16, 16), WIN - 16), :] = r[e * WIN + 16:(e + 1) * WIN]
+                    return carry
+
+                lax.fori_loop(0, (span + WIN - 1) // WIN, window, 0)
+            return carry
+
+        lax.fori_loop(0, group, one_tile, 0)
 
     @pl.when(step >= steps)
     def _():
-        e = step - steps
         lane = iota((slots, 128), 1)
-        for b in range(2):
-            j = info_ref[b]
-            kept = iota((slots, 1), 0) < start_ref[j, e, steps + 1]
-            x = jnp.where(kept, xs_ref[b, e, 0:slots, :].astype(f32), 0.0)
-            d = jnp.where(kept, ds_ref[b, e, 0:slots, :].astype(f32), 0.0)
-            x = x.astype(bf16)
-            x_ref[0, b * slots:(b + 1) * slots, :] = x
-            z = nn(x, wr3_ref[...])
-            other = other_ref[j].T[0:slots, :]
-            other = rsum(jnp.where(iota((slots, n_local), 1) == e, other, 0.0))
-            name = lane % n_experts
-            here = rsum(jnp.where(name == info_ref[2] + e, z, 0.0))
-            there = rsum(jnp.where(name == other.astype(jnp.int32), z, 0.0))
-            g = 1.0 / (1.0 + jnp.exp(there - here))
-            c_ref[0, b * slots:(b + 1) * slots, :] = (g * (OUT_SCALE * d)).astype(bf16)
+
+        def one_expert(sub, carry):
+            e = (step - steps) * group + sub
+            for b in range(2):
+                j = info_ref[b]
+                kept = iota((slots, 1), 0) < start_ref[j, e, steps * group + 1]
+                x = jnp.where(kept, xs_ref[b, e, 0:slots, :].astype(f32), 0.0)
+                d = jnp.where(kept, ds_ref[b, e, 0:slots, :].astype(f32), 0.0)
+                x = x.astype(bf16)
+                x_ref[sub, b * slots:(b + 1) * slots, :] = x
+                z = nn(x, wr3_ref[...])
+                other = other_ref[j].T[0:slots, :]
+                other = rsum(keep(iota((slots, n_local), 1) == e, other))
+                name = lane % n_experts
+                here = rsum(keep(name == info_ref[2] + e, z))
+                there = rsum(keep(name == other.astype(jnp.int32), z))
+                g = jax.nn.sigmoid(here - there)
+                c_ref[sub, b * slots:(b + 1) * slots, :] = (g * (OUT_SCALE * d)).astype(bf16)
+            return carry
+
+        lax.fori_loop(0, group, one_expert, 0)
 
 
 def act(ab, du):
@@ -260,7 +279,7 @@
 
 
 def fetch(names, w, slots, n_local, info_ref, win_ref, dst_ref):
-    step = pl.program_id(0)
+    step = pl.program_id(0) + info_ref[4]
     for i, (q, el, read) in enumerate(names):
         first = win_ref[step, info_ref[q] * n_local + el]
         for piece in range(0, WIN, 16):
@@ -282,12 +301,12 @@
 
 def masks(code, w, col):
     if isinstance(w, int):
-        return [jnp.where(col == code[:, 2 + k:3 + k], 1.0, 0.0) for k in range(2)]
+        return [ind(col == v) for v in cols(code, 2, 3)]
     low = (w * WIN).astype(f32)
     out = []
     for k in range(2):
-        rel = code[:, 9 + k:10 + k]
-        at = jnp.where((rel >= low) & (rel < low + WIN), code[:, 7 + k:8 + k] + rel - low, -1.0)
+        base, rel = cols(code, 7 + k, 9 + k)
+        at = jnp.where((rel >= low) & (rel < low + WIN), base + rel - low, -1.0)
         out.append(ind(col == at))
     return out
 
@@ -301,8 +320,8 @@
     return nn((m0 + m1).astype(bf16), rows_ref[...])
 
 
-def further(win_ref, body):
-    n_win = win_ref[pl.program_id(0), win_ref.shape[1] - 1]
+def further(info_ref, win_ref, body):
+    n_win = win_ref[pl.program_id(0) + info_ref[4], win_ref.shape[1] - 1]
 
     @pl.when(n_win > 1)
     def _():
@@ -336,7 +355,7 @@
         y1_ref[...] = (y1_ref[...].astype(f32) + y[rows:]).astype(bf16)
         dx_ref[...] = dx_ref[...] + dx
 
-    further(win_ref, more)
+    further(info_ref, win_ref, more)
 
 
 def final_y_kernel(groups, slots, n_local, info_ref, win_ref, code_ref, *refs):
@@ -356,7 +375,7 @@
     def more(w):
         y_ref[...] = y_ref[...] + collect(w)
 
-    further(win_ref, more)
+    further(info_ref, win_ref, more)
     y = y_ref[...] + collect(0)
     y0 = y0_ref[...].astype(f32) + y[:rows]
     y1 = y1_ref[...].astype(f32) + y[rows:]
@@ -368,7 +387,7 @@
     dg1 = rsum(m * y1)
     mean = g0 * dg0 + g1 * dg1
     lane = iota(p.shape, 1).astype(f32)
-    dp = (jnp.where(lane == e0, (dg0 - mean) / s, 0.0) + jnp.where(lane == e1, (dg1 - mean) / s, 0.0)
+    dp = (keep(lane == e0, (dg0 - mean) / s) + keep(lane == e1, (dg1 - mean) / s)
           + coef_ref[...])
     dz = p * (dp - rsum(p * dp))
     dz_ref[...] = dz
@@ -385,7 +404,8 @@
 
 def final_x_kernel(groups, slots, n_local, info_ref, win_ref, code_ref, *refs):
     n_r = 4 * len(groups)
-    dx_ref, d_ref, dz_ref, wr_ref, dh_ref, rows_ref, x_ref, wt_ref = refs[n_r:]
+    dx_ref, d_ref, dz_ref, wr_ref = refs[n_r:n_r + 4]
+    dh_ref, rows_ref, x_ref, wt_ref = refs[-4:]
     code = code_ref[...]
     col = column(groups, n_local)
 
@@ -402,7 +422,7 @@
     def more(w):
         x_ref[...] = x_ref[...] + collect(w)
 
-    further(win_ref, more)
+    further(info_ref, win_ref, more)
     dx = x_ref[...] + collect(0)
     z_hi, z_lo, _ = split3(dz_ref[...])
     w_hi, w_lo, _ = split3(wt_ref[...])
@@ -424,7 +444,7 @@
         return lax.ppermute(v, ("etp", "ep"), pairs)
 
     def kernel(body, **kw):
-        return pl.pallas_call(body, **kw)
+        return pl.pallas_call(body, compiler_params=params(), cost_estimate=cost(8e9), **kw)
 
     def layer(hidden, w_router, expert_ids, d_out, w_gate, w_up, w_down):
         tok_rows, d_model = hidden.shape
@@ -435,15 +455,15 @@
         slots = 7 * tok_rows // (2 * n_experts)
         ep, etp = lax.axis_index("ep"), lax.axis_index("etp")
         steps = tok_rows // TILE
-        ep_info = jnp.stack([ep ^ q for q in range(4)]).astype(jnp.int32)
+        ep_info = jnp.stack([ep ^ q for q in range(4)] + [jnp.zeros_like(ep)]).astype(jnp.int32)
         sds = jax.ShapeDtypeStruct
         smem = pl.BlockSpec(memory_space=pltpu.SMEM)
 
         def whole(shape):
             return pl.BlockSpec(shape, lambda i: (0,) * len(shape))
 
-        def tokens(width, tile=TILE):
-            return pl.BlockSpec((tile, width), lambda i: (i, 0))
+        def tokens(width, start=0):
+            return pl.BlockSpec((TILE, width), lambda i: (i + start, 0))
 
         def expert_block(shape, lo=0):
             return pl.BlockSpec((1,) + shape, lambda i: (i + lo,) + (0,) * len(shape))
@@ -459,8 +479,9 @@
         dx_, dy_ = permute(d_out, 2, 0), permute(d_out, 0, 1)
         hd, dd = permute(hy, 2, 0), permute(dy_, 2, 0)
         core = lambda v: permute(v, 1, 0)
-        h_pairs = {(0, 0): (hidden, core(hidden)), (1, 0): (hx, core(hx)), (0, 1): (hy, core(hy)), (1, 1): (hd, core(hd))}
-        d_pairs = {(0, 0): (d_out, core(d_out)), (1, 0): (dx_, core(dx_)), (0, 1): (dy_, core(dy_)), (1, 1): (dd, core(dd))}
+        pairs = ((0, 0), (1, 0), (0, 1), (1, 1))
+        h_pairs = {pair: (v, core(v)) for pair, v in zip(pairs, (hidden, hx, hy, hd))}
+        d_pairs = {pair: (v, core(v)) for pair, v in zip(pairs, (d_out, dx_, dy_, dd))}
         partner = [(permute(w13[lo:hi], 0, 1), permute(w_down[lo:hi], 0, 1)) for lo, hi in CHUNKS]
 
         per_block = lambda *shape: pl.BlockSpec((1,) + shape, lambda i: (i,) + (0,) * len(shape))
@@ -472,7 +493,6 @@
             out_shape=[sds((n_dev, steps * n_local, TILE), f32), sds((n_dev, n_local, TILE), f32),
                        sds((n_dev, n_local, 128), jnp.int32), sds((d_model, 128), bf16)],
             scratch_shapes=[pltpu.VMEM((n_local, 128), f32)],
-            compiler_params=params(), cost_estimate=cost(5e9),
         )(rank_info, near_ids, w_router)
 
         probs, code, wins, stats = kernel(
@@ -481,23 +501,22 @@
             in_specs=[smem, tokens(d_model), whole((d_model, n_experts)), tokens(2)],
             out_specs=[tokens(n_experts), tokens(128), whole((8, 128)), whole((8, 128))],
             out_shape=[sds((tok_rows, n_experts), f32), sds((tok_rows, 128), f32), sds((8, 128), jnp.int32), sds((8, 128), f32)],
-            compiler_params=params(), cost_estimate=cost(3e9),
         )(ep_info, hidden, w_router, expert_ids)
 
         def gather(pair):
             x, t = pair
             info = jnp.stack([(ep ^ (2 * x)) * etp_size + (etp ^ t), (ep ^ (2 * x + 1)) * etp_size + (etp ^ t), ep * n_local]).astype(jnp.int32)
             block = sds((n_local, 2 * slots, d_model), bf16)
-            tile = pl.BlockSpec((TILE, d_model), lambda i: (jnp.minimum(i, steps - 1), 0))
-            out = pl.BlockSpec((1, 2 * slots, d_model), lambda i: (jnp.maximum(i - steps, 0), 0, 0))
+            fills = steps // GROUP
+            tile = pl.BlockSpec((GROUP * TILE, d_model), lambda i: (jnp.minimum(i, fills - 1), 0))
+            out = pl.BlockSpec((GROUP, 2 * slots, d_model), lambda i: (jnp.maximum(i - fills, 0), 0, 0))
             return kernel(
                 functools.partial(gather_kernel, slots, n_local, n_experts),
-                grid=(steps + n_local,),
+                grid=(fills + n_local // GROUP,),
                 in_specs=[smem, smem, whole(slot_rows.shape), whole(others.shape), whole(wr3.shape)] + [tile] * 4,
                 out_specs=[out] * 2,
                 out_shape=[block, block],
                 scratch_shapes=[pltpu.VMEM((n_local * WIN, TILE), bf16)] + [pltpu.VMEM((2, n_local, slots + 64, d_model), bf16)] * 2,
-                compiler_params=params(), cost_estimate=cost(8e9),
             )(info, starts, slot_rows, others, wr3, *h_pairs[pair], *d_pairs[pair])
 
         rows = {pair: gather(pair) for pair in h_pairs}
@@ -513,7 +532,6 @@
                 out_specs=[g13, g13, g2],
                 out_shape=[sds((n_local, d_model, ff), f32)] * 2 + [sds((n_local, ff, d_model), f32)],
                 input_output_aliases={6 + k: k for k in range(len(acc))},
-                compiler_params=params(), cost_estimate=cost(3e9 * (hi - lo)),
             )(xa, xb, ca, cb, w13, w_down, *acc)
 
         grad = grads((0, 0), (1, 0), (), 0, n_local)
@@ -531,7 +549,6 @@
                           expert_block((d_model, 2 * ff)), expert_block((ff, d_model))],
                 out_specs=[expert_block((slots, d_model))] * 8 if index >= split else [expert_block((2, slots, d_model))] * 4,
                 out_shape=[sds((hi - lo, slots, d_model), bf16)] * 8 if index >= split else [sds((hi - lo, 2, slots, d_model), bf16)] * 4,
-                compiler_params=params(), cost_estimate=cost(6e9 * (hi - lo)),
             )(xa, xb, ca, cb, w13, w_down, *partner[index])
             return [outs[i] if i % 4 == 0 else permute(outs[i], i % 4, 0) for i in range(len(outs))]
 
@@ -541,19 +558,21 @@
         total = jnp.sum((near_ids.reshape(-1)[:, None] == jnp.arange(n_experts)[None, :]).astype(f32), axis=0)[None, :]
         coef = (AUX_COEF * n_experts / n_tokens / (2 * n_tokens)) * total
 
-        def token_kernel(body, chunk_ids, arrays, extra, extra_specs, out_specs, out_shape, scratch):
+        def token_kernel(body, chunk_ids, arrays, extra, extra_specs, out_specs, out_shape, scratch,
+                         start=0, count=steps, **kw):
             groups = tuple(CHUNKS[i] for i in chunk_ids)
             return kernel(
                 functools.partial(body, groups, slots, n_local),
-                grid=(steps,),
-                in_specs=[smem, smem, tokens(128)] + [whole(r.shape) for r in arrays] + extra_specs,
+                grid=(count,),
+                in_specs=[smem, smem, tokens(128, start=start)] + [whole(r.shape) for r in arrays] + extra_specs,
                 out_specs=out_specs, out_shape=out_shape, scratch_shapes=scratch,
-                compiler_params=params(), cost_estimate=cost(8e9),
-            )(ep_info, wins, code, *arrays, *extra)
+                **kw,
+            )(ep_info.at[4].add(start), wins, code, *arrays, *extra)
 
         wide = tokens(d_model)
         width = lambda ids: 4 * sum(CHUNKS[i][1] - CHUNKS[i][0] for i in ids) * WIN
-        early, late = (0, 1), (2, 3, last)
+        early = range(split - 1)
+        late = (split - 1, split, last)
         y0, y1, dxs = token_kernel(
             combine_kernel, early, [r for i in early for r in returned[i]], (), [],
             [wide] * 3, [sds((tok_rows, d_model), bf16)] * 2 + [sds((tok_rows, d_model), f32)],
@@ -565,11 +584,18 @@
             [wide, tokens(n_experts), whole((n_experts + 8, d_model))],
             [sds((tok_rows, d_model), bf16), sds((tok_rows, n_experts), f32), sds((n_experts + 8, d_model), f32)],
             [pltpu.VMEM((width(late), d_model), bf16), pltpu.VMEM((2 * TILE, d_model), f32)])
-        (d_hidden,) = token_kernel(
-            final_x_kernel, late, half(1), (dxs, d_out, dz, w_router),
-            [wide] * 2 + [tokens(n_experts), whole((d_model, n_experts))],
-            [wide], [sds((tok_rows, d_model), bf16)],
-            [pltpu.VMEM((width(late), d_model), bf16), pltpu.VMEM((TILE, d_model), f32), pltpu.VMEM((n_experts, d_model), f32)])
+        mid = steps // 2
+        d_hidden = []
+        for start in (0, mid):
+            wide = tokens(d_model, start)
+            kw = {"input_output_aliases": {3 + len(half(1)) + 4: 0}} if d_hidden else {}
+            d_hidden = token_kernel(
+                final_x_kernel, late, half(1), (dxs, d_out, dz, w_router, *d_hidden),
+                [wide] * 2 + [tokens(n_experts, start), whole((d_model, n_experts))] + [wide] * len(d_hidden),
+                [wide], [sds((tok_rows, d_model), bf16)],
+                [pltpu.VMEM((width(late), d_model), bf16), pltpu.VMEM((TILE, d_model), f32), pltpu.VMEM((n_experts, d_model), f32)],
+                start, mid, **kw)
+        (d_hidden,) = d_hidden
         for dep, detp in ((1, 0), (2, 0), (0, 1)):
             d_rt = d_rt + permute(d_rt, dep, detp)
         d_router = d_rt[:n_experts].T

time: 782 us -> 779 us (level)
  waiting for transfers between devices: 445 us -> 432 us
  local copies, waits for them, and re-layouts: 20.9 us -> 31.8 us
    ppermute x55 -> x60, waiting for transfers between devices: 445 us -> 432 us  [permute(): return lax.ppermute(v, ('etp', 'ep'), pairs)]
    pallas_call x3 -> x4, Pallas kernels: 39.5 us -> 43 us  [token_kernel(): kernel(functools.partial(body, groups, slots, n_local), grid=(count,), in...]
    unnamed x61 -> x82, local copies, waits for them, and re-layouts: 12.5 us -> 15.8 us
    pallas_call x5 -> x6, Pallas kernels: 58.8 us -> 61.1 us  [back(): kernel(functools.partial(row_kernel, slots), grid=(hi - lo,), in_specs=[a...]
    ppermute x55 -> x60, starting transfers between devices: 47.2 us -> 48.7 us  [permute(): return lax.ppermute(v, ('etp', 'ep'), pairs)]
  transfers between devices with their start and end apart: 55 -> 60, of which waited for: 17 -> 18; matrix products, arithmetic and copies ran while one was open for 3% -> 4% of each run, Pallas kernels for 26% -> 27%
where the time goes in v3:
time: 779 us; the launch traced here: 774 us
  waiting for transfers between devices  432 us (55%)
  Pallas kernels  253 us (32%)
  starting transfers between devices  48.7 us (6%)
  local copies, waits for them, and re-layouts  31.8 us (4%)
    ppermute x60, waiting for transfers between devices, permute(): return lax.ppermute(v, ('etp', 'ep'), pairs)  432 us
    pallas_call x4, Pallas kernels, gather(): kernel(functools.partial(gather_kernel, slots, n_local, n_experts), grid=...  62.5 us
    pallas_call x6, Pallas kernels, back(): kernel(functools.partial(row_kernel, slots), grid=(hi - lo,), in_specs=[a...  61.1 us
    pallas_call x3, Pallas kernels, grads(): kernel(functools.partial(grad_kernel, bool(acc)), grid=(hi - lo,), in_spe...  58.4 us
    ppermute x60, starting transfers between devices, permute(): return lax.ppermute(v, ('etp', 'ep'), pairs)  48.7 us
    pallas_call x4, Pallas kernels, token_kernel(): kernel(functools.partial(body, groups, slots, n_local), grid=(count,), in...  43 us
    pallas_call x1, Pallas kernels, layer(): kernel(functools.partial(slot_kernel, capacity, slots, n_local), grid=(n_...  16.6 us
    unnamed x82, local copies, waits for them, and re-layouts  15.8 us
  transfers between devices with their start and end apart: 60, of which 18 were waited for; matrix products, arithmetic and copies ran while one was open for 4% of the time, Pallas kernels for 27%

profile of v3, /device:TPU:0, one launch (start us, length us, event | category | flops | bytes accessed | tf_op | source)
XLA Modules:
  0.0 773.8 jit_solution(15459971478018626802)
XLA Ops:
  2.1 3.7 collective-permute-start.6
  10.2 2.4 fusion.5
  12.6 2.1 constant_dynamic-update-slice_fusion.9
  15.6 2.0 constant_dynamic-update-slice_fusion.8.wo_ref.w13_ref
  21.5 3.6 fusion.3
  25.0 2.1 fusion.4
  27.7 1.7 copy.27.wr_ref.refs_15_
  33.7 67.0 %collective-permute-done.3 = s32[16,256]{1,0:T(8,128)S(1)} collective-permute-done((s32[16,256]{1,0:T(8,128)}, s32[16,256]{1,0:T(8,128)S(1)}, u32[]{:S(2)}, u32[]{:S(2)}) %collective-permute-start.3) | collective-permute-done | bytes 16416 | tf_op jit(solution)/shard_map/ppermute | solution.py:444
  101.9 3.7 collective-permute-done.4
  106.9 2.1 collective-permute-done.5
  111.4 7.7 collective-permute-done.39.w2p_ref
  120.5 16.6 %shard_map.127 = (f32[8,64,256]{2,1,0:T(8,128)}, f32[8,8,256]{2,1,0:T(8,128)}, s32[8,8,128]{2,1,0:T(8,128)}, bf16[512,128]{1,0:T(8,128)(2,1)}) custom-call(s32[9]{0:T(128)} %pad_add_fusion.info_ref, s32[8,16,256]{2,1,0:T(8,128)} %constant_dynamic-update-slice_fusion.ids_ref, f32[512,32]{1,0:T(8,128)} %copy.27.wr_ref.refs_15_), custom_call_target="tpu_custom_call" | custom-call | flops 8000000000 | bytes 1048576 | tf_op jit(solution)/shard_map/pallas_call | solution.py:488
  140.6 15.6 %shard_map.128 = (bf16[8,448,512]{2,1,0:T(8,128)(2,1)}, bf16[8,448,512]{2,1,0:T(8,128)(2,1)}) custom-call(s32[3]{0:T(128)} %add_add_fusion.info_ref, s32[8,8,128]{2,1,0:T(8,128)} %get-tuple-element.112.start_ref, f32[8,64,256]{2,1,0:T(8,128)} %get-tuple-element.113.slot_ref, f32[8,8,256]{2,1,0:T(8,128)} %get-tuple-element.114.other_ref, ...), custom_call_target="tpu_custom_call" | custom-call | flops 8000000000 | bytes 1048576 | tf_op jit(solution)/shard_map/pallas_call | solution.py:513
  161.1 15.7 %shard_map.129 = (bf16[8,448,512]{2,1,0:T(8,128)(2,1)}, bf16[8,448,512]{2,1,0:T(8,128)(2,1)}) custom-call(s32[3]{0:T(128)} %add_add_fusion.1.info_ref, s32[8,8,128]{2,1,0:T(8,128)} %get-tuple-element.112.start_ref, f32[8,64,256]{2,1,0:T(8,128)} %get-tuple-element.113.slot_ref, f32[8,8,256]{2,1,0:T(8,128)} %get-tuple-element.114.other_ref, ...), custom_call_target="tpu_custom_call" | custom-call | flops 8000000000 | bytes 1048576 | tf_op jit(solution)/shard_map/pallas_call | solution.py:513
  177.4 8.4 %shard_map.135 = (bf16[1,2,224,512]{3,2,1,0:T(8,128)(2,1)}, bf16[1,2,224,512]{3,2,1,0:T(8,128)(2,1)}, bf16[1,2,224,512]{3,2,1,0:T(8,128)(2,1)}, bf16[1,2,224,512]{3,2,1,0:T(8,128)(2,1)}) custom-call(bf16[8,448,512]{2,1,0:T(8,128)(2,1)} %get-tuple-element.116.xa_ref, bf16[8,448,512]{2,1,0:T(8,128)(2,1)} %get-tuple-element.117.xb_ref, ...), custom_call_target="tpu_custom_call" | custom-call | flops 8000000000 | bytes 1048576 | tf_op jit(solution)/shard_map/pallas_call | solution.py:545
  185.8 5.6 collective-permute-done.34.w2p_ref
  192.8 15.4 %collective-permute-done.29.w2p_ref = bf16[2,384,512]{2,1,0:T(8,128)(2,1)} collective-permute-done((bf16[2,384,512]{2,1,0:T(8,128)(2,1)}, bf16[2,384,512]{2,1,0:T(8,128)(2,1)}, u32[]{:S(2)}, u32[]{:S(2)}) %collective-permute-start.29) | collective-permute-done | bytes 786464 | tf_op jit(solution)/shard_map/ppermute | solution.py:444
  209.6 15.4 %collective-permute-done.23.wp_ref = bf16[1,512,768]{2,1,0:T(8,128)(2,1)} collective-permute-done((bf16[1,512,768]{2,1,0:T(8,128)(2,1)}, bf16[1,512,768]{2,1,0:T(8,128)(2,1)}, u32[]{:S(2)}, u32[]{:S(2)}) %collective-permute-start.23) | collective-permute-done | bytes 786464 | tf_op jit(solution)/shard_map/ppermute | solution.py:444
  226.5 15.4 %collective-permute-done.18.wp_ref = bf16[1,512,768]{2,1,0:T(8,128)(2,1)} collective-permute-done((bf16[1,512,768]{2,1,0:T(8,128)(2,1)}, bf16[1,512,768]{2,1,0:T(8,128)(2,1)}, u32[]{:S(2)}, u32[]{:S(2)}) %collective-permute-start.18) | collective-permute-done | bytes 786464 | tf_op jit(solution)/shard_map/ppermute | solution.py:444
  243.3 8.2 %shard_map.132 = (bf16[1,224,512]{2,1,0:T(8,128)(2,1)}, bf16[1,224,512]{2,1,0:T(8,128)(2,1)}, bf16[1,224,512]{2,1,0:T(8,128)(2,1)}, bf16[1,224,512]{2,1,0:T(8,12...) custom-call(bf16[8,448,512]{2,1,0:T(8,128)(2,1)} %get-tuple-element., ...), custom_call_target="tpu_custom_call" | custom-call | flops 8000000000 | bytes 1048576 | tf_op jit(solution)/shard_map/pallas_call | solution.py:545
  251.6 8.2 %shard_map.131 = (bf16[1,224,512]{2,1,0:T(8,128)(2,1)}, bf16[1,224,512]{2,1,0:T(8,128)(2,1)}, bf16[1,224,512]{2,1,0:T(8,128)(2,1)}, bf16[1,224,512]{2,1,0:T(8,12...) custom-call(bf16[8,448,512]{2,1,0:T(8,128)(2,1)} %get-tuple-element., ...), custom_call_target="tpu_custom_call" | custom-call | flops 8000000000 | bytes 1048576 | tf_op jit(solution)/shard_map/pallas_call | solution.py:545
  259.8 122.6 %collective-permute-done.13.wp_ref = bf16[1,512,768]{2,1,0:T(8,128)(2,1)} collective-permute-done((bf16[1,512,768]{2,1,0:T(8,128)(2,1)}, bf16[1,512,768]{2,1,0:T(8,128)(2,1)}, u32[]{:S(2)}, u32[]{:S(2)}) %collective-permute-start.13) | collective-permute-done | bytes 786464 | tf_op jit(solution)/shard_map/ppermute | solution.py:444
  382.6 1.9 collective-permute-start.26
  384.5 8.3 %shard_map.130 = (bf16[1,2,224,512]{3,2,1,0:T(8,128)(2,1)}, bf16[1,2,224,512]{3,2,1,0:T(8,128)(2,1)}, bf16[1,2,224,512]{3,2,1,0:T(8,128)(2,1)}, bf16[1,2,224,512]{3,2,1,0:T(8,128)(2,1)}) custom-call(bf16[8,448,512]{2,1,0:T(8,128)(2,1)} %get-tuple-element.116.xa_ref, bf16[8,448,512]{2,1,0:T(8,128)(2,1)} %get-tuple-element.117.xb_ref, ...), custom_call_target="tpu_custom_call" | custom-call | flops 8000000000 | bytes 1048576 | tf_op jit(solution)/shard_map/pallas_call | solution.py:545
  392.8 20.0 %collective-permute-done.28.wp_ref = bf16[2,512,768]{2,1,0:T(8,128)(2,1)} collective-permute-done((bf16[2,512,768]{2,1,0:T(8,128)(2,1)S(1)}, bf16[2,512,768]{2,1,0:T(8,128)(2,1)}, u32[]{:S(2)}, u32[]{:S(2)}) %collective-permute-start.28) | collective-permute-done | bytes 1572896 | tf_op jit(solution)/shard_map/ppermute | solution.py:444
  412.9 3.2 collective-permute-start.27
  418.7 13.8 %shard_map.134 = (bf16[2,2,224,512]{3,2,1,0:T(8,128)(2,1)}, bf16[2,2,224,512]{3,2,1,0:T(8,128)(2,1)}, bf16[2,2,224,512]{3,2,1,0:T(8,128)(2,1)}, bf16[2,2,224,512]{3,2,1,0:T(8,128)(2,1)}) custom-call(bf16[8,448,512]{2,1,0:T(8,128)(2,1)} %get-tuple-element.116.xa_ref, bf16[8,448,512]{2,1,0:T(8,128)(2,1)} %get-tuple-element.117.xb_ref, ...), custom_call_target="tpu_custom_call" | custom-call | flops 8000000000 | bytes 1048576 | tf_op jit(solution)/shard_map/pallas_call | solution.py:545
  433.6 1.7 collective-permute-start.42
  436.4 14.2 %shard_map.133 = (bf16[2,2,224,512]{3,2,1,0:T(8,128)(2,1)}, bf16[2,2,224,512]{3,2,1,0:T(8,128)(2,1)}, bf16[2,2,224,512]{3,2,1,0:T(8,128)(2,1)}, bf16[2,2,224,512]{3,2,1,0:T(8,128)(2,1)}) custom-call(bf16[8,448,512]{2,1,0:T(8,128)(2,1)} %get-tuple-element.116.xa_ref, bf16[8,448,512]{2,1,0:T(8,128)(2,1)} %get-tuple-element.117.xb_ref, ...), custom_call_target="tpu_custom_call" | custom-call | flops 8000000000 | bytes 1048576 | tf_op jit(solution)/shard_map/pallas_call | solution.py:545
  450.6 1.7 collective-permute-start.36
  452.3 2.4 collective-permute-done.42.refs_11_
  457.8 8.0 %collective-permute-done.16.refs_2_ = bf16[1,2,224,512]{3,2,1,0:T(8,128)(2,1)S(1)} collective-permute-done((bf16[1,2,224,512]{3,2,1,0:T(8,128)(2,1)}, bf16[1,2,224,512]{3,2,1,0:T(8,128)(2,1)S(1)}, u32[]{:S(2)}, u32[]{:S(2)}) %collective-permute-start.16) | collective-permute-done | bytes 458784 | tf_op jit(solution)/shard_map/ppermute | solution.py:444
  466.2 11.3 %shard_map.126 = (f32[2048,32]{1,0:T(8,128)}, f32[2048,128]{1,0:T(8,128)}, s32[8,128]{1,0:T(8,128)}, f32[8,128]{1,0:T(8,128)}) custom-call(s32[5]{0:T(128)} %stack.85.info_ref, bf16[2048,512]{1,0:T(8,128)(2,1)} %refs_14_.1, f32[512,32]{1,0:T(8,128)} %copy.27.wr_ref.refs_15_, s32[2048,2]{1,0:T(8,128)} %copy.28.ids_ref), custom_call_target="tpu_custom_call" | custom-call | flops 8000000000 | bytes 1048576 | tf_op jit(solution)/shard_map/pallas_call | solution.py:498
  477.6 8.0 %collective-permute-done.36.refs_6_ = bf16[2,2,224,512]{3,2,1,0:T(8,128)(2,1)} collective-permute-done((bf16[2,2,224,512]{3,2,1,0:T(8,128)(2,1)S(1)}, bf16[2,2,224,512]{3,2,1,0:T(8,128)(2,1)}, u32[]{:S(2)}, u32[]{:S(2)}) %collective-permute-start.36) | collective-permute-done | bytes 917536 | tf_op jit(solution)/shard_map/ppermute | solution.py:444
  485.9 18.0 %collective-permute-done.37.refs_7_ = bf16[2,2,224,512]{3,2,1,0:T(8,128)(2,1)} collective-permute-done((bf16[2,2,224,512]{3,2,1,0:T(8,128)(2,1)}, bf16[2,2,224,512]{3,2,1,0:T(8,128)(2,1)}, u32[]{:S(2)}, u32[]{:S(2)}) %collective-permute-start.37) | collective-permute-done | bytes 917536 | tf_op jit(solution)/shard_map/ppermute | solution.py:444
  507.8 17.1 %collective-permute-done.31.refs_2_ = bf16[2,2,224,512]{3,2,1,0:T(8,128)(2,1)} collective-permute-done((bf16[2,2,224,512]{3,2,1,0:T(8,128)(2,1)}, bf16[2,2,224,512]{3,2,1,0:T(8,128)(2,1)}, u32[]{:S(2)}, u32[]{:S(2)}) %collective-permute-start.31) | collective-permute-done | bytes 917536 | tf_op jit(solution)/shard_map/ppermute | solution.py:444
  524.9 18.4 %collective-permute-done.32.refs_3_ = bf16[2,2,224,512]{3,2,1,0:T(8,128)(2,1)} collective-permute-done((bf16[2,2,224,512]{3,2,1,0:T(8,128)(2,1)}, bf16[2,2,224,512]{3,2,1,0:T(8,128)(2,1)}, u32[]{:S(2)}, u32[]{:S(2)}) %collective-permute-start.32) | collective-permute-done | bytes 917536 | tf_op jit(solution)/shard_map/ppermute | solution.py:444
  544.3 13.9 %shard_map.136 = (bf16[2048,512]{1,0:T(8,128)(2,1)}, bf16[2048,512]{1,0:T(8,128)(2,1)}, f32[2048,512]{1,0:T(8,128)}) custom-call(s32[5]{0:T(128)} %copy-done.8, s32[8,128]{1,0:T(8,128)} %get-tuple-element.110.win_ref, f32[2048,128]{1,0:T(8,128)} %get-tuple-element.111.code_ref, bf16[2,2,224,512]{3,2,1,0:T(8,128)(2,1)} %get-tuple-element.132.refs_0_, ...), custom_call_target="tpu_custom_call" | custom-call | flops 8000000000 | bytes 1048576 | tf_op jit(solution)/shard_map/pallas_call | solution.py:564
  558.2 84.6 %collective-permute-done.17.refs_3_ = bf16[1,2,224,512]{3,2,1,0:T(8,128)(2,1)S(1)} collective-permute-done((bf16[1,2,224,512]{3,2,1,0:T(8,128)(2,1)}, bf16[1,2,224,512]{3,2,1,0:T(8,128)(2,1)S(1)}, u32[]{:S(2)}, u32[]{:S(2)}) %collective-permute-start.17) | collective-permute-done | bytes 458784 | tf_op jit(solution)/shard_map/ppermute | solution.py:444
  643.6 15.0 %shard_map.137 = (bf16[2048,512]{1,0:T(8,128)(2,1)}, f32[2048,32]{1,0:T(8,128)}, f32[40,512]{1,0:T(8,128)}) custom-call(s32[5]{0:T(128)} %copy-done.8, s32[8,128]{1,0:T(8,128)} %get-tuple-element.110.win_ref, f32[2048,128]{1,0:T(8,128)} %get-tuple-element.111.code_ref, bf16[1,2,224,512]{3,2,1,0:T(8,128)(2,1)} %get-tuple-element.120.refs_0_, ...), custom_call_target="tpu_custom_call" | custom-call | flops 8000000000 | bytes 1048576 | tf_op jit(solution)/shard_map/pallas_call | solution.py:564
  659.2 2.2 collective-permute-start.48
  661.4 27.0 %shard_map.142 = (f32[8,512,384]{2,1,0:T(8,128)}, f32[8,512,384]{2,1,0:T(8,128)}, f32[8,384,512]{2,1,0:T(8,128)}) custom-call(bf16[8,448,512]{2,1,0:T(8,128)(2,1)} %get-tuple-element.116.xa_ref, bf16[8,448,512]{2,1,0:T(8,128)(2,1)} %get-tuple-element.117.xb_ref, bf16[8,448,512]{2,1,0:T(8,128)(2,1)} %get-tuple-element.118.ca_ref, ...), custom_call_target="tpu_custom_call" | custom-call | flops 8000000000 | bytes 1048576 | tf_op jit(solution)/shard_map/pallas_call | solution.py:528
  691.1 15.5 %shard_map.140 = (bf16[8,448,512]{2,1,0:T(8,128)(2,1)}, bf16[8,448,512]{2,1,0:T(8,128)(2,1)}) custom-call(s32[3]{0:T(128)} %add_add_fusion.2.info_ref, s32[8,8,128]{2,1,0:T(8,128)} %get-tuple-element.112.start_ref, f32[8,64,256]{2,1,0:T(8,128)} %get-tuple-element.113.slot_ref, f32[8,8,256]{2,1,0:T(8,128)} %get-tuple-element.114.other_ref, ...), custom_call_target="tpu_custom_call" | custom-call | flops 8000000000 | bytes 1048576 | tf_op jit(solution)/shard_map/pallas_call | solution.py:513
  707.8 6.9 shard_map.138.refs_16_
  716.3 7.1 shard_map.139
  725.4 15.6 %shard_map.141 = (bf16[8,448,512]{2,1,0:T(8,128)(2,1)}, bf16[8,448,512]{2,1,0:T(8,128)(2,1)}) custom-call(s32[3]{0:T(128)} %add_add_fusion.3.info_ref, s32[8,8,128]{2,1,0:T(8,128)} %get-tuple-element.112.start_ref, f32[8,64,256]{2,1,0:T(8,128)} %get-tuple-element.113.slot_ref, f32[8,8,256]{2,1,0:T(8,128)} %get-tuple-element.114.other_ref, ...), custom_call_target="tpu_custom_call" | custom-call | flops 8000000000 | bytes 1048576 | tf_op jit(solution)/shard_map/pallas_call | solution.py:513
  741.0 15.6 %shard_map.143 = (f32[8,512,384]{2,1,0:T(8,128)}, f32[8,512,384]{2,1,0:T(8,128)}, f32[8,384,512]{2,1,0:T(8,128)}) custom-call(bf16[8,448,512]{2,1,0:T(8,128)(2,1)} %get-tuple-element.160.xa_ref, bf16[8,448,512]{2,1,0:T(8,128)(2,1)} %get-tuple-element.161.xb_ref, ...), custom_call_target="tpu_custom_call", output_to_operand_aliasing={{0}: (6, {}), {1}: (7, {}), {2}: (8, {})} | custom-call | flops 8000000000 | bytes 1048576 | tf_op jit(solution)/shard_map/pallas_call | solution.py:528
  756.6 15.8 %shard_map.144 = (f32[8,512,384]{2,1,0:T(8,128)}, f32[8,512,384]{2,1,0:T(8,128)}, f32[8,384,512]{2,1,0:T(8,128)}) custom-call(bf16[8,448,512]{2,1,0:T(8,128)(2,1)} %get-tuple-element.160.xa_ref, bf16[8,448,512]{2,1,0:T(8,128)(2,1)} %get-tuple-element.161.xb_ref, ...), custom_call_target="tpu_custom_call", output_to_operand_aliasing={{0}: (6, {}), {1}: (7, {}), {2}: (8, {})} | custom-call | flops 8000000000 | bytes 1048576 | tf_op jit(solution)/shard_map/pallas_call | solution.py:528
  (197 shorter events, 57.9 us)
Async XLA Ops:
  2.1 28.6 %collective-permute-start.6 = (s32[16,256]{1,0:T(8,128)}, s32[16,256]{1,0:T(8,128)}, u32[]{:S(2)}, u32[]{:S(2)}) collective-permute-start(s32[16,256]{1,0:T(8,128)} %reshape.92), channel_id=1, source_target_pairs={{0,7},{1,6},{2,5},{3,4},{4,3},{5,2},{6,1},{7,0}} | collective-permute-start | bytes 49160 | tf_op jit(solution)/shard_map/ppermute | solution.py:444
  5.8 26.1 %collective-permute-start.2 = (s32[16,256]{1,0:T(8,128)}, s32[16,256]{1,0:T(8,128)}, u32[]{:S(2)}, u32[]{:S(2)}) collective-permute-start(s32[16,256]{1,0:T(8,128)} %reshape.92), channel_id=1, source_target_pairs={{0,5},{1,4},{2,7},{3,6},{4,1},{5,0},{6,3},{7,2}} | collective-permute-start | bytes 49160 | tf_op jit(solution)/shard_map/ppermute | solution.py:444
  6.6 22.8 %collective-permute-start = (s32[16,256]{1,0:T(8,128)}, s32[16,256]{1,0:T(8,128)}, u32[]{:S(2)}, u32[]{:S(2)}) collective-permute-start(s32[16,256]{1,0:T(8,128)} %reshape.92), channel_id=1, source_target_pairs={{0,4},{1,5},{2,6},{3,7},{4,0},{5,1},{6,2},{7,3}} | collective-permute-start | bytes 49160 | tf_op jit(solution)/shard_map/ppermute | solution.py:444
  8.1 97.4 %collective-permute-start.9 = (bf16[2048,512]{1,0:T(8,128)(2,1)}, bf16[2048,512]{1,0:T(8,128)(2,1)}, u32[]{:S(2)}, u32[]{:S(2)}) collective-permute-start(bf16[2048,512]{1,0:T(8,128)(2,1)} %refs_14_.1), channel_id=1, source_target_pairs={{0,2},{1,3},{2,0},{3,1},{4,6},{5,7},{6,4},{7,5}} | collective-permute-start | bytes 6291464 | tf_op jit(solution)/shard_map/ppermute | solution.py:444
  8.7 97.6 %collective-permute-start.11 = (bf16[2048,512]{1,0:T(8,128)(2,1)}, bf16[2048,512]{1,0:T(8,128)(2,1)}, u32[]{:S(2)}, u32[]{:S(2)}) collective-permute-start(bf16[2048,512]{1,0:T(8,128)(2,1)} %refs_13_.3), channel_id=1, source_target_pairs={{0,2},{1,3},{2,0},{3,1},{4,6},{5,7},{6,4},{7,5}} | collective-permute-start | bytes 6291464 | tf_op jit(solution)/shard_map/ppermute | solution.py:444
  30.7 107.8 %collective-permute-start.7 = (bf16[2048,512]{1,0:T(8,128)(2,1)}, bf16[2048,512]{1,0:T(8,128)(2,1)}, u32[]{:S(2)}, u32[]{:S(2)}) collective-permute-start(bf16[2048,512]{1,0:T(8,128)(2,1)} %refs_14_.1), channel_id=1, source_target_pairs={{0,1},{1,0},{2,3},{3,2},{4,5},{5,4},{6,7},{7,6}} | collective-permute-start | bytes 6291464 | tf_op jit(solution)/shard_map/ppermute | solution.py:444
  31.3 107.9 %collective-permute-start.8 = (bf16[2048,512]{1,0:T(8,128)(2,1)}, bf16[2048,512]{1,0:T(8,128)(2,1)}, u32[]{:S(2)}, u32[]{:S(2)}) collective-permute-start(bf16[2048,512]{1,0:T(8,128)(2,1)} %refs_13_.3), channel_id=1, source_target_pairs={{0,1},{1,0},{2,3},{3,2},{4,5},{5,4},{6,7},{7,6}} | collective-permute-start | bytes 6291464 | tf_op jit(solution)/shard_map/ppermute | solution.py:444
  31.9 68.8 %collective-permute-start.3 = (s32[16,256]{1,0:T(8,128)}, s32[16,256]{1,0:T(8,128)S(1)}, u32[]{:S(2)}, u32[]{:S(2)}) collective-permute-start(s32[16,256]{1,0:T(8,128)} %reshape.92), channel_id=1, source_target_pairs={{0,2},{1,3},{2,0},{3,1},{4,6},{5,7},{6,4},{7,5}} | collective-permute-start | bytes 49160 | tf_op jit(solution)/shard_map/ppermute | solution.py:444
  105.6 53.5 %collective-permute-start.10 = (bf16[2048,512]{1,0:T(8,128)(2,1)}, bf16[2048,512]{1,0:T(8,128)(2,1)}, u32[]{:S(2)}, u32[]{:S(2)}) collective-permute-start(bf16[2048,512]{1,0:T(8,128)(2,1)} %collective-permute-done.9.ha_ref), channel_id=1, source_target_pairs={{0,1},{1,0},{2,3},{3,2},{4,5},{5,4},{6,7},{7,6}} | collective-permute-start | bytes 6291464 | tf_op jit(solution)/shard_map/ppermute | solution.py:444
  106.2 53.4 %collective-permute-start.12 = (bf16[2048,512]{1,0:T(8,128)(2,1)}, bf16[2048,512]{1,0:T(8,128)(2,1)}, u32[]{:S(2)}, u32[]{:S(2)}) collective-permute-start(bf16[2048,512]{1,0:T(8,128)(2,1)} %collective-permute-done.11.da_ref), channel_id=1, source_target_pairs={{0,1},{1,0},{2,3},{3,2},{4,5},{5,4},{6,7},{7,6}} | collective-permute-start | bytes 6291464 | tf_op jit(solution)/shard_map/ppermute | solution.py:444
  137.1 19.1 %collective-permute-start.19 = (bf16[1,384,512]{2,1,0:T(8,128)(2,1)S(1)}, bf16[1,384,512]{2,1,0:T(8,128)(2,1)}, u32[]{:S(2)}, u32[]{:S(2)}) collective-permute-start(bf16[1,384,512]{2,1,0:T(8,128)(2,1)S(1)} %copy-done.3), channel_id=1, source_target_pairs={{0,4},{1,5},{2,6},{3,7},{4,0},{5,1},{6,2},{7,3}} | collective-permute-start | bytes 1179656 | tf_op jit(solution)/shard_map/ppermute | solution.py:444
  138.6 19.1 %collective-permute-start.14 = (bf16[1,384,512]{2,1,0:T(8,128)(2,1)S(1)}, bf16[1,384,512]{2,1,0:T(8,128)(2,1)}, u32[]{:S(2)}, u32[]{:S(2)}) collective-permute-start(bf16[1,384,512]{2,1,0:T(8,128)(2,1)S(1)} %get-tuple-element.182), channel_id=1, source_target_pairs={{0,4},{1,5},{2,6},{3,7},{4,0},{5,1},{6,2},{7,3}} | collective-permute-start | bytes 1179656 | tf_op jit(solution)/shard_map/ppermute | solution.py:444
  139.2 37.6 %collective-permute-start.38 = (bf16[1,512,768]{2,1,0:T(8,128)(2,1)}, bf16[1,512,768]{2,1,0:T(8,128)(2,1)}, u32[]{:S(2)}, u32[]{:S(2)}) collective-permute-start(bf16[1,512,768]{2,1,0:T(8,128)(2,1)} %get-tuple-element.173), channel_id=1, source_target_pairs={{0,4},{1,5},{2,6},{3,7},{4,0},{5,1},{6,2},{7,3}} | collective-permute-start | bytes 2359304 | tf_op jit(solution)/shard_map/ppermute | solution.py:444
  156.2 35.2 %collective-permute-start.34 = (bf16[2,384,512]{2,1,0:T(8,128)(2,1)}, bf16[2,384,512]{2,1,0:T(8,128)(2,1)}, u32[]{:S(2)}, u32[]{:S(2)}) collective-permute-start(bf16[2,384,512]{2,1,0:T(8,128)(2,1)} %get-tuple-element.183), channel_id=1, source_target_pairs={{0,4},{1,5},{2,6},{3,7},{4,0},{5,1},{6,2},{7,3}} | collective-permute-start | bytes 2359304 | tf_op jit(solution)/shard_map/ppermute | solution.py:444
  157.6 50.6 %collective-permute-start.29 = (bf16[2,384,512]{2,1,0:T(8,128)(2,1)}, bf16[2,384,512]{2,1,0:T(8,128)(2,1)}, u32[]{:S(2)}, u32[]{:S(2)}) collective-permute-start(bf16[2,384,512]{2,1,0:T(8,128)(2,1)} %get-tuple-element.184), channel_id=1, source_target_pairs={{0,4},{1,5},{2,6},{3,7},{4,0},{5,1},{6,2},{7,3}} | collective-permute-start | bytes 2359304 | tf_op jit(solution)/shard_map/ppermute | solution.py:444
  159.1 66.0 %collective-permute-start.23 = (bf16[1,512,768]{2,1,0:T(8,128)(2,1)}, bf16[1,512,768]{2,1,0:T(8,128)(2,1)}, u32[]{:S(2)}, u32[]{:S(2)}) collective-permute-start(bf16[1,512,768]{2,1,0:T(8,128)(2,1)} %get-tuple-element.174), channel_id=1, source_target_pairs={{0,4},{1,5},{2,6},{3,7},{4,0},{5,1},{6,2},{7,3}} | collective-permute-start | bytes 2359304 | tf_op jit(solution)/shard_map/ppermute | solution.py:444
  159.7 82.2 %collective-permute-start.18 = (bf16[1,512,768]{2,1,0:T(8,128)(2,1)}, bf16[1,512,768]{2,1,0:T(8,128)(2,1)}, u32[]{:S(2)}, u32[]{:S(2)}) collective-permute-start(bf16[1,512,768]{2,1,0:T(8,128)(2,1)} %get-tuple-element.175), channel_id=1, source_target_pairs={{0,4},{1,5},{2,6},{3,7},{4,0},{5,1},{6,2},{7,3}} | collective-permute-start | bytes 2359304 | tf_op jit(solution)/shard_map/ppermute | solution.py:444
  176.8 205.5 %collective-permute-start.33 = (bf16[2,512,768]{2,1,0:T(8,128)(2,1)S(1)}, bf16[2,512,768]{2,1,0:T(8,128)(2,1)}, u32[]{:S(2)}, u32[]{:S(2)}) collective-permute-start(bf16[2,512,768]{2,1,0:T(8,128)(2,1)S(1)} %get-tuple-element.177), channel_id=1, source_target_pairs={{0,4},{1,5},{2,6},{3,7},{4,0},{5,1},{6,2},{7,3}} | collective-permute-start | bytes 4718600 | tf_op jit(solution)/shard_map/ppermute | solution.py:444
  191.3 221.5 %collective-permute-start.52 = (bf16[2048,512]{1,0:T(8,128)(2,1)}, bf16[2048,512]{1,0:T(8,128)(2,1)}, u32[]{:S(2)}, u32[]{:S(2)}) collective-permute-start(bf16[2048,512]{1,0:T(8,128)(2,1)} %refs_14_.1), channel_id=1, source_target_pairs={{0,4},{1,5},{2,6},{3,7},{4,0},{5,1},{6,2},{7,3}} | collective-permute-start | bytes 6291464 | tf_op jit(solution)/shard_map/ppermute | solution.py:444
  208.2 207.9 %collective-permute-start.54 = (bf16[2048,512]{1,0:T(8,128)(2,1)}, bf16[2048,512]{1,0:T(8,128)(2,1)}, u32[]{:S(2)}, u32[]{:S(2)}) collective-permute-start(bf16[2048,512]{1,0:T(8,128)(2,1)} %refs_13_.3), channel_id=1, source_target_pairs={{0,4},{1,5},{2,6},{3,7},{4,0},{5,1},{6,2},{7,3}} | collective-permute-start | bytes 6291464 | tf_op jit(solution)/shard_map/ppermute | solution.py:444
  225.1 157.3 %collective-permute-start.13 = (bf16[1,512,768]{2,1,0:T(8,128)(2,1)}, bf16[1,512,768]{2,1,0:T(8,128)(2,1)}, u32[]{:S(2)}, u32[]{:S(2)}) collective-permute-start(bf16[1,512,768]{2,1,0:T(8,128)(2,1)} %get-tuple-element.176), channel_id=1, source_target_pairs={{0,4},{1,5},{2,6},{3,7},{4,0},{5,1},{6,2},{7,3}} | collective-permute-start | bytes 2359304 | tf_op jit(solution)/shard_map/ppermute | solution.py:444
  241.9 171.0 %collective-permute-start.28 = (bf16[2,512,768]{2,1,0:T(8,128)(2,1)S(1)}, bf16[2,512,768]{2,1,0:T(8,128)(2,1)}, u32[]{:S(2)}, u32[]{:S(2)}) collective-permute-start(bf16[2,512,768]{2,1,0:T(8,128)(2,1)S(1)} %get-tuple-element.178), channel_id=1, source_target_pairs={{0,4},{1,5},{2,6},{3,7},{4,0},{5,1},{6,2},{7,3}} | collective-permute-start | bytes 4718600 | tf_op jit(solution)/shard_map/ppermute | solution.py:444
  382.4 33.8 %collective-permute-start.25 = (bf16[1,224,512]{2,1,0:T(8,128)(2,1)}, bf16[1,224,512]{2,1,0:T(8,128)(2,1)S(1)}, u32[]{:S(2)}, u32[]{:S(2)}) collective-permute-start(bf16[1,224,512]{2,1,0:T(8,128)(2,1)} %get-tuple-element.129), channel_id=1, source_target_pairs={{0,1},{1,0},{2,3},{3,2},{4,5},{5,4},{6,7},{7,6}} | collective-permute-start | bytes 688136 | tf_op jit(solution)/shard_map/ppermute | solution.py:444
  382.6 34.0 %collective-permute-start.26 = (bf16[1,224,512]{2,1,0:T(8,128)(2,1)}, bf16[1,224,512]{2,1,0:T(8,128)(2,1)S(1)}, u32[]{:S(2)}, u32[]{:S(2)}) collective-permute-start(bf16[1,224,512]{2,1,0:T(8,128)(2,1)} %get-tuple-element.130), channel_id=1, source_target_pairs={{0,2},{1,3},{2,0},{3,1},{4,6},{5,7},{6,4},{7,5}} | collective-permute-start | bytes 688136 | tf_op jit(solution)/shard_map/ppermute | solution.py:444
  412.9 22.5 %collective-permute-start.40 = (bf16[1,2,224,512]{3,2,1,0:T(8,128)(2,1)}, bf16[1,2,224,512]{3,2,1,0:T(8,128)(2,1)S(1)}, u32[]{:S(2)}, u32[]{:S(2)}) collective-permute-start(bf16[1,2,224,512]{3,2,1,0:T(8,128)(2,1)} %get-tuple-element.141), channel_id=1, source_target_pairs={{0,1},{1,0},{2,3},{3,2},{4,5},{5,4},{6,7},{7,6}} | collective-permute-start | bytes 1376264 | tf_op jit(solution)/shard_map/ppermute | solution.py:444
  412.9 19.6 %collective-permute-start.27 = (bf16[1,224,512]{2,1,0:T(8,128)(2,1)S(1)}, bf16[1,224,512]{2,1,0:T(8,128)(2,1)S(1)}, u32[]{:S(2)}, u32[]{:S(2)}) collective-permute-start(bf16[1,224,512]{2,1,0:T(8,128)(2,1)S(1)} %copy-done.30), channel_id=1, source_target_pairs={{0,3},{1,2},{2,1},{3,0},{4,7},{5,6},{6,5},{7,4}} | collective-permute-start | bytes 688136 | tf_op jit(solution)/shard_map/ppermute | solution.py:444
  433.5 32.6 %collective-permute-start.35 = (bf16[2,2,224,512]{3,2,1,0:T(8,128)(2,1)}, bf16[2,2,224,512]{3,2,1,0:T(8,128)(2,1)S(1)}, u32[]{:S(2)}, u32[]{:S(2)}) collective-permute-start(bf16[2,2,224,512]{3,2,1,0:T(8,128)(2,1)} %get-tuple-element.137), channel_id=1, source_target_pairs={{0,1},{1,0},{2,3},{3,2},{4,5},{5,4},{6,7},{7,6}} | collective-permute-start | bytes 2752520 | tf_op jit(solution)/shard_map/ppermute | solution.py:444
  433.6 21.1 %collective-permute-start.42 = (bf16[1,2,224,512]{3,2,1,0:T(8,128)(2,1)S(1)}, bf16[1,2,224,512]{3,2,1,0:T(8,128)(2,1)}, u32[]{:S(2)}, u32[]{:S(2)}) collective-permute-start(bf16[1,2,224,512]{3,2,1,0:T(8,128)(2,1)S(1)} %copy-done.14), channel_id=1, source_target_pairs={{0,3},{1,2},{2,1},{3,0},{4,7},{5,6},{6,5},{7,4}} | collective-permute-start | bytes 1376264 | tf_op jit(solution)/shard_map/ppermute | solution.py:444
  435.4 20.5 %collective-permute-start.15 = (bf16[1,2,224,512]{3,2,1,0:T(8,128)(2,1)}, bf16[1,2,224,512]{3,2,1,0:T(8,128)(2,1)}, u32[]{:S(2)}, u32[]{:S(2)}) collective-permute-start(bf16[1,2,224,512]{3,2,1,0:T(8,128)(2,1)} %get-tuple-element.121), channel_id=1, source_target_pairs={{0,1},{1,0},{2,3},{3,2},{4,5},{5,4},{6,7},{7,6}} | collective-permute-start | bytes 1376264 | tf_op jit(solution)/shard_map/ppermute | solution.py:444
  436.1 29.7 %collective-permute-start.16 = (bf16[1,2,224,512]{3,2,1,0:T(8,128)(2,1)}, bf16[1,2,224,512]{3,2,1,0:T(8,128)(2,1)S(1)}, u32[]{:S(2)}, u32[]{:S(2)}) collective-permute-start(bf16[1,2,224,512]{3,2,1,0:T(8,128)(2,1)} %get-tuple-element.122), channel_id=1, source_target_pairs={{0,2},{1,3},{2,0},{3,1},{4,6},{5,7},{6,4},{7,5}} | collective-permute-start | bytes 1376264 | tf_op jit(solution)/shard_map/ppermute | solution.py:444
  450.6 34.9 %collective-permute-start.36 = (bf16[2,2,224,512]{3,2,1,0:T(8,128)(2,1)S(1)}, bf16[2,2,224,512]{3,2,1,0:T(8,128)(2,1)}, u32[]{:S(2)}, u32[]{:S(2)}) collective-permute-start(bf16[2,2,224,512]{3,2,1,0:T(8,128)(2,1)S(1)} %copy-done.11), channel_id=1, source_target_pairs={{0,2},{1,3},{2,0},{3,1},{4,6},{5,7},{6,4},{7,5}} | collective-permute-start | bytes 2752520 | tf_op jit(solution)/shard_map/ppermute | solution.py:444
  454.8 49.2 %collective-permute-start.37 = (bf16[2,2,224,512]{3,2,1,0:T(8,128)(2,1)}, bf16[2,2,224,512]{3,2,1,0:T(8,128)(2,1)}, u32[]{:S(2)}, u32[]{:S(2)}) collective-permute-start(bf16[2,2,224,512]{3,2,1,0:T(8,128)(2,1)} %get-tuple-element.139), channel_id=1, source_target_pairs={{0,3},{1,2},{2,1},{3,0},{4,7},{5,6},{6,5},{7,4}} | collective-permute-start | bytes 2752520 | tf_op jit(solution)/shard_map/ppermute | solution.py:444
  455.8 49.2 %collective-permute-start.30 = (bf16[2,2,224,512]{3,2,1,0:T(8,128)(2,1)}, bf16[2,2,224,512]{3,2,1,0:T(8,128)(2,1)}, u32[]{:S(2)}, u32[]{:S(2)}) collective-permute-start(bf16[2,2,224,512]{3,2,1,0:T(8,128)(2,1)} %get-tuple-element.133), channel_id=1, source_target_pairs={{0,1},{1,0},{2,3},{3,2},{4,5},{5,4},{6,7},{7,6}} | collective-permute-start | bytes 2752520 | tf_op jit(solution)/shard_map/ppermute | solution.py:444
  465.8 59.1 %collective-permute-start.31 = (bf16[2,2,224,512]{3,2,1,0:T(8,128)(2,1)}, bf16[2,2,224,512]{3,2,1,0:T(8,128)(2,1)}, u32[]{:S(2)}, u32[]{:S(2)}) collective-permute-start(bf16[2,2,224,512]{3,2,1,0:T(8,128)(2,1)} %get-tuple-element.134), channel_id=1, source_target_pairs={{0,2},{1,3},{2,0},{3,1},{4,6},{5,7},{6,4},{7,5}} | collective-permute-start | bytes 2752520 | tf_op jit(solution)/shard_map/ppermute | solution.py:444
  466.2 77.1 %collective-permute-start.32 = (bf16[2,2,224,512]{3,2,1,0:T(8,128)(2,1)}, bf16[2,2,224,512]{3,2,1,0:T(8,128)(2,1)}, u32[]{:S(2)}, u32[]{:S(2)}) collective-permute-start(bf16[2,2,224,512]{3,2,1,0:T(8,128)(2,1)} %get-tuple-element.135), channel_id=1, source_target_pairs={{0,3},{1,2},{2,1},{3,0},{4,7},{5,6},{6,5},{7,4}} | collective-permute-start | bytes 2752520 | tf_op jit(solution)/shard_map/ppermute | solution.py:444
  485.6 173.1 %collective-permute-start.56 = (bf16[2048,512]{1,0:T(8,128)(2,1)}, bf16[2048,512]{1,0:T(8,128)(2,1)S(1)}, u32[]{:S(2)}, u32[]{:S(2)}) collective-permute-start(bf16[2048,512]{1,0:T(8,128)(2,1)} %collective-permute-done.52.ha_ref), channel_id=1, source_target_pairs={{0,2},{1,3},{2,0},{3,1},{4,6},{5,7},{6,4},{7,5}} | collective-permute-start | bytes 6291464 | tf_op jit(solution)/shard_map/ppermute | solution.py:444
  503.9 155.2 %collective-permute-start.53 = (bf16[2048,512]{1,0:T(8,128)(2,1)}, bf16[2048,512]{1,0:T(8,128)(2,1)}, u32[]{:S(2)}, u32[]{:S(2)}) collective-permute-start(bf16[2048,512]{1,0:T(8,128)(2,1)} %collective-permute-done.52.ha_ref), channel_id=1, source_target_pairs={{0,1},{1,0},{2,3},{3,2},{4,5},{5,4},{6,7},{7,6}} | collective-permute-start | bytes 6291464 | tf_op jit(solution)/shard_map/ppermute | solution.py:444
  505.0 156.3 %collective-permute-start.58 = (bf16[2048,512]{1,0:T(8,128)(2,1)}, bf16[2048,512]{1,0:T(8,128)(2,1)}, u32[]{:S(2)}, u32[]{:S(2)}) collective-permute-start(bf16[2048,512]{1,0:T(8,128)(2,1)} %collective-permute-done.54.da_ref), channel_id=1, source_target_pairs={{0,2},{1,3},{2,0},{3,1},{4,6},{5,7},{6,4},{7,5}} | collective-permute-start | bytes 6291464 | tf_op jit(solution)/shard_map/ppermute | solution.py:444
  524.9 163.5 %collective-permute-start.55 = (bf16[2048,512]{1,0:T(8,128)(2,1)}, bf16[2048,512]{1,0:T(8,128)(2,1)}, u32[]{:S(2)}, u32[]{:S(2)}) collective-permute-start(bf16[2048,512]{1,0:T(8,128)(2,1)} %collective-permute-done.54.da_ref), channel_id=1, source_target_pairs={{0,1},{1,0},{2,3},{3,2},{4,5},{5,4},{6,7},{7,6}} | collective-permute-start | bytes 6291464 | tf_op jit(solution)/shard_map/ppermute | solution.py:444
  543.2 99.6 %collective-permute-start.17 = (bf16[1,2,224,512]{3,2,1,0:T(8,128)(2,1)}, bf16[1,2,224,512]{3,2,1,0:T(8,128)(2,1)S(1)}, u32[]{:S(2)}, u32[]{:S(2)}) collective-permute-start(bf16[1,2,224,512]{3,2,1,0:T(8,128)(2,1)} %get-tuple-element.123), channel_id=1, source_target_pairs={{0,3},{1,2},{2,1},{3,0},{4,7},{5,6},{6,5},{7,4}} | collective-permute-start | bytes 1376264 | tf_op jit(solution)/shard_map/ppermute | solution.py:444
  642.9 46.0 %collective-permute-start.46 = (bf16[1,224,512]{2,1,0:T(8,128)(2,1)S(1)}, bf16[1,224,512]{2,1,0:T(8,128)(2,1)}, u32[]{:S(2)}, u32[]{:S(2)}) collective-permute-start(bf16[1,224,512]{2,1,0:T(8,128)(2,1)S(1)} %copy-done.22), channel_id=1, source_target_pairs={{0,1},{1,0},{2,3},{3,2},{4,5},{5,4},{6,7},{7,6}} | collective-permute-start | bytes 688136 | tf_op jit(solution)/shard_map/ppermute | solution.py:444
  658.7 30.5 %collective-permute-start.47 = (bf16[1,224,512]{2,1,0:T(8,128)(2,1)S(1)}, bf16[1,224,512]{2,1,0:T(8,128)(2,1)S(1)}, u32[]{:S(2)}, u32[]{:S(2)}) collective-permute-start(bf16[1,224,512]{2,1,0:T(8,128)(2,1)S(1)} %copy-done.21), channel_id=1, source_target_pairs={{0,2},{1,3},{2,0},{3,1},{4,6},{5,7},{6,4},{7,5}} | collective-permute-start | bytes 688136 | tf_op jit(solution)/shard_map/ppermute | solution.py:444
  659.2 31.2 %collective-permute-start.48 = (bf16[1,224,512]{2,1,0:T(8,128)(2,1)S(1)}, bf16[1,224,512]{2,1,0:T(8,128)(2,1)}, u32[]{:S(2)}, u32[]{:S(2)}) collective-permute-start(bf16[1,224,512]{2,1,0:T(8,128)(2,1)S(1)} %copy-done.20), channel_id=1, source_target_pairs={{0,3},{1,2},{2,1},{3,0},{4,7},{5,6},{6,5},{7,4}} | collective-permute-start | bytes 688136 | tf_op jit(solution)/shard_map/ppermute | solution.py:444
  661.4 29.6 %collective-permute-start.49 = (f32[40,512]{1,0:T(8,128)}, f32[40,512]{1,0:T(8,128)S(1)}, u32[]{:S(2)}, u32[]{:S(2)}) collective-permute-start(f32[40,512]{1,0:T(8,128)} %get-tuple-element.159), channel_id=1, source_target_pairs={{0,1},{1,0},{2,3},{3,2},{4,5},{5,4},{6,7},{7,6}} | collective-permute-start | bytes 245768 | tf_op jit(solution)/shard_map/ppermute | solution.py:444
  688.4 18.2 %collective-permute-start.43 = (bf16[1,224,512]{2,1,0:T(8,128)(2,1)S(1)}, bf16[1,224,512]{2,1,0:T(8,128)(2,1)}, u32[]{:S(2)}, u32[]{:S(2)}) collective-permute-start(bf16[1,224,512]{2,1,0:T(8,128)(2,1)S(1)} %copy-done.19), channel_id=1, source_target_pairs={{0,1},{1,0},{2,3},{3,2},{4,5},{5,4},{6,7},{7,6}} | collective-permute-start | bytes 688136 | tf_op jit(solution)/shard_map/ppermute | solution.py:444
  688.8 18.2 %collective-permute-start.44 = (bf16[1,224,512]{2,1,0:T(8,128)(2,1)S(1)}, bf16[1,224,512]{2,1,0:T(8,128)(2,1)S(1)}, u32[]{:S(2)}, u32[]{:S(2)}) collective-permute-start(bf16[1,224,512]{2,1,0:T(8,128)(2,1)S(1)} %copy-done.18), channel_id=1, source_target_pairs={{0,2},{1,3},{2,0},{3,1},{4,6},{5,7},{6,4},{7,5}} | collective-permute-start | bytes 688136 | tf_op jit(solution)/shard_map/ppermute | solution.py:444
  690.4 35.0 %collective-permute-start.57 = (bf16[2048,512]{1,0:T(8,128)(2,1)S(1)}, bf16[2048,512]{1,0:T(8,128)(2,1)}, u32[]{:S(2)}, u32[]{:S(2)}) collective-permute-start(bf16[2048,512]{1,0:T(8,128)(2,1)S(1)} %collective-permute-done.56.ha_ref), channel_id=1, source_target_pairs={{0,1},{1,0},{2,3},{3,2},{4,5},{5,4},{6,7},{7,6}} | collective-permute-start | bytes 6291464 | tf_op jit(solution)/shard_map/ppermute | solution.py:444
  691.0 34.4 %collective-permute-start.59 = (bf16[2048,512]{1,0:T(8,128)(2,1)}, bf16[2048,512]{1,0:T(8,128)(2,1)}, u32[]{:S(2)}, u32[]{:S(2)}) collective-permute-start(bf16[2048,512]{1,0:T(8,128)(2,1)} %collective-permute-done.58.da_ref), channel_id=1, source_target_pairs={{0,1},{1,0},{2,3},{3,2},{4,5},{5,4},{6,7},{7,6}} | collective-permute-start | bytes 6291464 | tf_op jit(solution)/shard_map/ppermute | solution.py:444
  (47 other events, 848.3 us)

commit v4 on v3

--- a/solution.py
+++ b/solution.py
@@ -61,7 +61,7 @@
 
 
 def params(**kw):
-    return pltpu.CompilerParams(vmem_limit_bytes=60 * 2**20, **kw)
+    return pltpu.CompilerParams(vmem_limit_bytes=63 * 2**20, **kw)
 
 
 def cost(flops):
@@ -113,11 +113,15 @@
     stat_ref[1:2, 0:n_experts] = stat_ref[1:2, 0:n_experts] + csum(p)
 
 
-def slot_kernel(capacity, slots, n_local, info_ref, ids_ref, wr_ref, slot_ref, other_ref, start_ref, wr3_ref, total_ref):
+def slot_kernel(capacity, slots, n_local, info_ref, wr_ref, *refs):
+    slot_ref, other_ref, start_ref, wr3_ref, total_ref, ids_ref = refs[-6:]
+
     @pl.when(pl.program_id(0) == 0)
     def _():
         total_ref[...] = jnp.zeros_like(total_ref)
         wr3_ref[...] = jnp.zeros_like(wr3_ref)
+        for k, ref in enumerate(refs[:-6]):
+            ids_ref[k] = ref[...]
         width = wr_ref.shape[1]
         for k, piece in enumerate(split3(wr_ref[...])):
             wr3_ref[:, k * width:(k + 1) * width] = piece
@@ -470,12 +474,14 @@
 
         tile_ids = expert_ids.reshape(steps, TILE, 2).transpose(0, 2, 1).reshape(2 * steps, TILE)
         near_ids = [tile_ids] + [permute(tile_ids, r // etp_size, r % etp_size) for r in range(1, n_dev)]
-        near_ids = jnp.stack(near_ids)
         rank = ep * etp_size + etp
         rank_info = jnp.concatenate([jnp.arange(n_dev, dtype=jnp.int32) ^ rank, (ep * n_local)[None]]).astype(jnp.int32)
         w13 = jnp.concatenate([w_gate, w_up], axis=2)
 
-        hx, hy = permute(hidden, 2, 0), permute(hidden, 0, 1)
+        cut = tok_rows // 2
+        h_lo, h_hi = hidden[:cut], hidden[cut:]
+        hx = jnp.concatenate([permute(h_lo, 2, 0), permute(h_hi, 2, 0)])
+        hy = jnp.concatenate([permute(h_lo, 0, 1), permute(h_hi, 0, 1)])
         dx_, dy_ = permute(d_out, 2, 0), permute(d_out, 0, 1)
         hd, dd = permute(hy, 2, 0), permute(dy_, 2, 0)
         core = lambda v: permute(v, 1, 0)
@@ -488,12 +494,12 @@
         slot_rows, others, starts, wr3 = kernel(
             functools.partial(slot_kernel, capacity, slots, n_local),
             grid=(n_dev,),
-            in_specs=[smem, whole(near_ids.shape), whole((d_model, n_experts))],
+            in_specs=[smem, whole((d_model, n_experts))] + [whole(tile_ids.shape)] * n_dev,
             out_specs=[per_block(steps * n_local, TILE), per_block(n_local, TILE), per_block(n_local, 128), whole((d_model, 128))],
             out_shape=[sds((n_dev, steps * n_local, TILE), f32), sds((n_dev, n_local, TILE), f32),
                        sds((n_dev, n_local, 128), jnp.int32), sds((d_model, 128), bf16)],
-            scratch_shapes=[pltpu.VMEM((n_local, 128), f32)],
-        )(rank_info, near_ids, w_router)
+            scratch_shapes=[pltpu.VMEM((n_local, 128), f32), pltpu.VMEM((n_dev, *tile_ids.shape), jnp.int32)],
+        )(rank_info, w_router, *near_ids)
 
         probs, code, wins, stats = kernel(
             functools.partial(route_kernel, n_experts, n_local),
@@ -555,7 +561,7 @@
         last = len(CHUNKS) - 1
         split = last - 1
         returned = [back(i) for i in range(len(CHUNKS))]
-        total = jnp.sum((near_ids.reshape(-1)[:, None] == jnp.arange(n_experts)[None, :]).astype(f32), axis=0)[None, :]
+        total = jnp.sum((jnp.concatenate(near_ids).reshape(-1)[:, None] == jnp.arange(n_experts)[None, :]).astype(f32), axis=0)[None, :]
         coef = (AUX_COEF * n_experts / n_tokens / (2 * n_tokens)) * total
 
         def token_kernel(body, chunk_ids, arrays, extra, extra_specs, out_specs, out_shape, scratch,
@@ -584,9 +590,9 @@
             [wide, tokens(n_experts), whole((n_experts + 8, d_model))],
             [sds((tok_rows, d_model), bf16), sds((tok_rows, n_experts), f32), sds((n_experts + 8, d_model), f32)],
             [pltpu.VMEM((width(late), d_model), bf16), pltpu.VMEM((2 * TILE, d_model), f32)])
-        mid = steps // 2
+        third = -(-steps // 3)
         d_hidden = []
-        for start in (0, mid):
+        for start in range(0, steps, third):
             wide = tokens(d_model, start)
             kw = {"input_output_aliases": {3 + len(half(1)) + 4: 0}} if d_hidden else {}
             d_hidden = token_kernel(
@@ -594,7 +600,7 @@
                 [wide] * 2 + [tokens(n_experts, start), whole((d_model, n_experts))] + [wide] * len(d_hidden),
                 [wide], [sds((tok_rows, d_model), bf16)],
                 [pltpu.VMEM((width(late), d_model), bf16), pltpu.VMEM((TILE, d_model), f32), pltpu.VMEM((n_experts, d_model), f32)],
-                start, mid, **kw)
+                start, min(third, steps - start), **kw)
         (d_hidden,) = d_hidden
         for dep, detp in ((1, 0), (2, 0), (0, 1)):
             d_rt = d_rt + permute(d_rt, dep, detp)

time: 779 us -> 656 us (0.84)
  waiting for transfers between devices: 432 us -> 301 us
    ppermute x60 -> x62, waiting for transfers between devices: 432 us -> 301 us  [permute(): return lax.ppermute(v, ('etp', 'ep'), pairs)]
    pallas_call x4 -> x5, Pallas kernels: 43 us -> 46.4 us  [token_kernel(): kernel(functools.partial(body, groups, slots, n_local), grid=(count,), in...]
    ppermute x60 -> x62, starting transfers between devices: 48.7 us -> 46 us  [permute(): return lax.ppermute(v, ('etp', 'ep'), pairs)]
    unnamed x82 -> x67, local copies, waits for them, and re-layouts: 15.8 us -> 14.6 us
  transfers between devices with their start and end apart: 60 -> 62, of which waited for: 18 -> 21; matrix products, arithmetic and copies ran while one was open for 4% -> 6% of each run, Pallas kernels for 27% -> 32%
where the time goes in v4:
time: 656 us; the launch traced here: 648 us
  waiting for transfers between devices  301 us (46%)
  Pallas kernels  256 us (39%)
  starting transfers between devices  46 us (7%)
  local copies, waits for them, and re-layouts  37.1 us (6%)
    ppermute x62, waiting for transfers between devices, permute(): return lax.ppermute(v, ('etp', 'ep'), pairs)  301 us
    pallas_call x4, Pallas kernels, gather(): kernel(functools.partial(gather_kernel, slots, n_local, n_experts), grid=...  62.4 us
    pallas_call x6, Pallas kernels, back(): kernel(functools.partial(row_kernel, slots), grid=(hi - lo,), in_specs=[a...  61.5 us
    pallas_call x3, Pallas kernels, grads(): kernel(functools.partial(grad_kernel, bool(acc)), grid=(hi - lo,), in_spe...  58.1 us
    pallas_call x5, Pallas kernels, token_kernel(): kernel(functools.partial(body, groups, slots, n_local), grid=(count,), in...  46.4 us
    ppermute x62, starting transfers between devices, permute(): return lax.ppermute(v, ('etp', 'ep'), pairs)  46 us
    pallas_call x1, Pallas kernels, layer(): kernel(functools.partial(slot_kernel, capacity, slots, n_local), grid=(n_...  16.7 us
    unnamed x67, local copies, waits for them, and re-layouts  14.6 us
  transfers between devices with their start and end apart: 62, of which 21 were waited for; matrix products, arithmetic and copies ran while one was open for 6% of the time, Pallas kernels for 32%

profile of v4, /device:TPU:0, one launch (start us, length us, event | category | flops | bytes accessed | tf_op | source)
XLA Modules:
  0.0 647.7 jit_solution(3853834542123515511)
XLA Ops:
  2.0 3.7 collective-permute-start.6
  8.0 2.4 fusion.5
  16.3 1.7 copy.29.wr_ref.refs_15_
  18.0 3.1 fusion.7
  21.2 2.0 constant_dynamic-update-slice_fusion.3
  24.2 2.0 constant_dynamic-update-slice_fusion.2.wo_ref.w13_ref
  26.8 11.0 %shard_map.126 = (f32[2048,32]{1,0:T(8,128)}, f32[2048,128]{1,0:T(8,128)}, s32[8,128]{1,0:T(8,128)}, f32[8,128]{1,0:T(8,128)}) custom-call(s32[5]{0:T(128)} %stack.61.info_ref, bf16[2048,512]{1,0:T(8,128)(2,1)} %refs_14_.1, f32[512,32]{1,0:T(8,128)} %copy.29.wr_ref.refs_15_, s32[2048,2]{1,0:T(8,128)} %copy.30.ids_ref), custom_call_target="tpu_custom_call" | custom-call | flops 8000000000 | bytes 1048576 | tf_op jit(solution)/shard_map/pallas_call | solution.py:504
  39.1 2.0 collective-permute-start.3
  41.7 43.8 %collective-permute-done.3.refs_4_ = s32[16,256]{1,0:T(8,128)S(1)} collective-permute-done((s32[16,256]{1,0:T(8,128)}, s32[16,256]{1,0:T(8,128)S(1)}, u32[]{:S(2)}, u32[]{:S(2)}) %collective-permute-start.3) | collective-permute-done | bytes 16416 | tf_op jit(solution)/shard_map/ppermute | solution.py:448
  93.7 3.7 fusion.4
  97.4 2.2 collective-permute-done.20.w2p_ref
  101.2 3.3 fusion.3
  104.5 19.7 %collective-permute-done.15.w2p_ref = bf16[1,384,512]{2,1,0:T(8,128)(2,1)S(1)} collective-permute-done((bf16[1,384,512]{2,1,0:T(8,128)(2,1)}, bf16[1,384,512]{2,1,0:T(8,128)(2,1)S(1)}, u32[]{:S(2)}, u32[]{:S(2)}) %collective-permute-start.15) | collective-permute-done | bytes 393248 | tf_op jit(solution)/shard_map/ppermute | solution.py:448
  127.2 9.4 %collective-permute-done.9 = bf16[1024,512]{1,0:T(8,128)(2,1)S(1)} collective-permute-done((bf16[1024,512]{1,0:T(8,128)(2,1)}, bf16[1024,512]{1,0:T(8,128)(2,1)S(1)}, u32[]{:S(2)}, u32[]{:S(2)}) %collective-permute-start.9) | collective-permute-done | bytes 1048608 | tf_op jit(solution)/shard_map/ppermute | solution.py:448
  140.9 24.5 %collective-permute-done.30.w2p_ref = bf16[2,384,512]{2,1,0:T(8,128)(2,1)S(1)} collective-permute-done((bf16[2,384,512]{2,1,0:T(8,128)(2,1)S(1)}, bf16[2,384,512]{2,1,0:T(8,128)(2,1)S(1)}, u32[]{:S(2)}, u32[]{:S(2)}) %collective-permute-start.30) | collective-permute-done | bytes 786464 | tf_op jit(solution)/shard_map/ppermute | solution.py:448
  167.7 16.7 %shard_map.127 = (f32[8,64,256]{2,1,0:T(8,128)}, f32[8,8,256]{2,1,0:T(8,128)}, s32[8,8,128]{2,1,0:T(8,128)}, bf16[512,128]{1,0:T(8,128)(2,1)}) custom-call(s32[9]{0:T(128)} %pad_add_fusion.info_ref, f32[512,32]{1,0:T(8,128)} %copy.29.wr_ref.refs_15_, s32[16,256]{1,0:T(8,128)} %reshape.109.refs_0_, s32[16,256]{1,0:T(8,128)} %copy-done.11, ...), custom_call_target="tpu_custom_call" | custom-call | flops 8000000000 | bytes 1048576 | tf_op jit(solution)/shard_map/pallas_call | solution.py:494
  184.4 2.3 constant_dynamic-update-slice_fusion.13
  186.7 5.3 collective-permute-done.54
  192.6 2.3 constant_dynamic-update-slice_fusion.12.ha_ref
  196.9 15.6 %shard_map.128 = (bf16[8,448,512]{2,1,0:T(8,128)(2,1)}, bf16[8,448,512]{2,1,0:T(8,128)(2,1)}) custom-call(s32[3]{0:T(128)} %add_add_fusion.info_ref, s32[8,8,128]{2,1,0:T(8,128)} %get-tuple-element.124.start_ref, f32[8,64,256]{2,1,0:T(8,128)} %get-tuple-element.125.slot_ref, f32[8,8,256]{2,1,0:T(8,128)} %get-tuple-element.126.other_ref, ...), custom_call_target="tpu_custom_call" | custom-call | flops 8000000000 | bytes 1048576 | tf_op jit(solution)/shard_map/pallas_call | solution.py:519
  215.9 15.6 %shard_map.129 = (bf16[8,448,512]{2,1,0:T(8,128)(2,1)}, bf16[8,448,512]{2,1,0:T(8,128)(2,1)}) custom-call(s32[3]{0:T(128)} %add_add_fusion.1.info_ref, s32[8,8,128]{2,1,0:T(8,128)} %get-tuple-element.124.start_ref, f32[8,64,256]{2,1,0:T(8,128)} %get-tuple-element.125.slot_ref, f32[8,8,256]{2,1,0:T(8,128)} %get-tuple-element.126.other_ref, ...), custom_call_target="tpu_custom_call" | custom-call | flops 8000000000 | bytes 1048576 | tf_op jit(solution)/shard_map/pallas_call | solution.py:519
  231.5 26.9 %shard_map.143 = (f32[8,512,384]{2,1,0:T(8,128)}, f32[8,512,384]{2,1,0:T(8,128)}, f32[8,384,512]{2,1,0:T(8,128)}) custom-call(bf16[8,448,512]{2,1,0:T(8,128)(2,1)} %get-tuple-element.128.xa_ref, bf16[8,448,512]{2,1,0:T(8,128)(2,1)} %get-tuple-element.129.xb_ref, bf16[8,448,512]{2,1,0:T(8,128)(2,1)} %get-tuple-element.130.ca_ref, ...), custom_call_target="tpu_custom_call" | custom-call | flops 8000000000 | bytes 1048576 | tf_op jit(solution)/shard_map/pallas_call | solution.py:534
  258.4 49.8 %collective-permute-done.24.wp_ref = bf16[1,512,768]{2,1,0:T(8,128)(2,1)} collective-permute-done((bf16[1,512,768]{2,1,0:T(8,128)(2,1)}, bf16[1,512,768]{2,1,0:T(8,128)(2,1)}, u32[]{:S(2)}, u32[]{:S(2)}) %collective-permute-start.24) | collective-permute-done | bytes 786464 | tf_op jit(solution)/shard_map/ppermute | solution.py:448
  308.8 16.2 %collective-permute-done.19.wp_ref = bf16[1,512,768]{2,1,0:T(8,128)(2,1)} collective-permute-done((bf16[1,512,768]{2,1,0:T(8,128)(2,1)}, bf16[1,512,768]{2,1,0:T(8,128)(2,1)}, u32[]{:S(2)}, u32[]{:S(2)}) %collective-permute-start.19) | collective-permute-done | bytes 786464 | tf_op jit(solution)/shard_map/ppermute | solution.py:448
  325.6 16.3 %collective-permute-done.14.wp_ref = bf16[1,512,768]{2,1,0:T(8,128)(2,1)} collective-permute-done((bf16[1,512,768]{2,1,0:T(8,128)(2,1)S(1)}, bf16[1,512,768]{2,1,0:T(8,128)(2,1)}, u32[]{:S(2)}, u32[]{:S(2)}) %collective-permute-start.14) | collective-permute-done | bytes 786464 | tf_op jit(solution)/shard_map/ppermute | solution.py:448
  342.7 8.4 %shard_map.135 = (bf16[1,2,224,512]{3,2,1,0:T(8,128)(2,1)}, bf16[1,2,224,512]{3,2,1,0:T(8,128)(2,1)}, bf16[1,2,224,512]{3,2,1,0:T(8,128)(2,1)}, bf16[1,2,224,512]{3,2,1,0:T(8,128)(2,1)}) custom-call(bf16[8,448,512]{2,1,0:T(8,128)(2,1)} %get-tuple-element.128.xa_ref, bf16[8,448,512]{2,1,0:T(8,128)(2,1)} %get-tuple-element.129.xb_ref, ...), custom_call_target="tpu_custom_call" | custom-call | flops 8000000000 | bytes 1048576 | tf_op jit(solution)/shard_map/pallas_call | solution.py:551
  351.0 8.2 %shard_map.132 = (bf16[1,224,512]{2,1,0:T(8,128)(2,1)}, bf16[1,224,512]{2,1,0:T(8,128)(2,1)}, bf16[1,224,512]{2,1,0:T(8,128)(2,1)}, bf16[1,224,512]{2,1,0:T(8,12...) custom-call(bf16[8,448,512]{2,1,0:T(8,128)(2,1)} %get-tuple-element., ...), custom_call_target="tpu_custom_call" | custom-call | flops 8000000000 | bytes 1048576 | tf_op jit(solution)/shard_map/pallas_call | solution.py:551
  359.2 14.2 %shard_map.134 = (bf16[2,2,224,512]{3,2,1,0:T(8,128)(2,1)}, bf16[2,2,224,512]{3,2,1,0:T(8,128)(2,1)}, bf16[2,2,224,512]{3,2,1,0:T(8,128)(2,1)}, bf16[2,2,224,512]{3,2,1,0:T(8,128)(2,1)}) custom-call(bf16[8,448,512]{2,1,0:T(8,128)(2,1)} %get-tuple-element.128.xa_ref, bf16[8,448,512]{2,1,0:T(8,128)(2,1)} %get-tuple-element.129.xb_ref, ...), custom_call_target="tpu_custom_call" | custom-call | flops 8000000000 | bytes 1048576 | tf_op jit(solution)/shard_map/pallas_call | solution.py:551
  375.6 43.1 %collective-permute-done.60.da_ref = bf16[2048,512]{1,0:T(8,128)(2,1)} collective-permute-done((bf16[2048,512]{1,0:T(8,128)(2,1)}, bf16[2048,512]{1,0:T(8,128)(2,1)}, u32[]{:S(2)}, u32[]{:S(2)}) %collective-permute-start.60) | collective-permute-done | bytes 2097184 | tf_op jit(solution)/shard_map/ppermute | solution.py:448
  419.3 8.2 %shard_map.131 = (bf16[1,224,512]{2,1,0:T(8,128)(2,1)}, bf16[1,224,512]{2,1,0:T(8,128)(2,1)}, bf16[1,224,512]{2,1,0:T(8,128)(2,1)}, bf16[1,224,512]{2,1,0:T(8,12...) custom-call(bf16[8,448,512]{2,1,0:T(8,128)(2,1)} %get-tuple-element., ...), custom_call_target="tpu_custom_call" | custom-call | flops 8000000000 | bytes 1048576 | tf_op jit(solution)/shard_map/pallas_call | solution.py:551
  430.4 14.2 %shard_map.133 = (bf16[2,2,224,512]{3,2,1,0:T(8,128)(2,1)}, bf16[2,2,224,512]{3,2,1,0:T(8,128)(2,1)}, bf16[2,2,224,512]{3,2,1,0:T(8,128)(2,1)}, bf16[2,2,224,512]{3,2,1,0:T(8,128)(2,1)}) custom-call(bf16[8,448,512]{2,1,0:T(8,128)(2,1)} %get-tuple-element.128.xa_ref, bf16[8,448,512]{2,1,0:T(8,128)(2,1)} %get-tuple-element.129.xb_ref, ...), custom_call_target="tpu_custom_call" | custom-call | flops 8000000000 | bytes 1048576 | tf_op jit(solution)/shard_map/pallas_call | solution.py:551
  446.7 4.1 collective-permute-done.43.refs_11_
  452.9 8.4 %shard_map.130 = (bf16[1,2,224,512]{3,2,1,0:T(8,128)(2,1)}, bf16[1,2,224,512]{3,2,1,0:T(8,128)(2,1)}, bf16[1,2,224,512]{3,2,1,0:T(8,128)(2,1)}, bf16[1,2,224,512]{3,2,1,0:T(8,128)(2,1)}) custom-call(bf16[8,448,512]{2,1,0:T(8,128)(2,1)} %get-tuple-element.128.xa_ref, bf16[8,448,512]{2,1,0:T(8,128)(2,1)} %get-tuple-element.129.xb_ref, ...), custom_call_target="tpu_custom_call" | custom-call | flops 8000000000 | bytes 1048576 | tf_op jit(solution)/shard_map/pallas_call | solution.py:551
  461.3 15.6 %shard_map.141 = (bf16[8,448,512]{2,1,0:T(8,128)(2,1)}, bf16[8,448,512]{2,1,0:T(8,128)(2,1)}) custom-call(s32[3]{0:T(128)} %add_add_fusion.2.info_ref, s32[8,8,128]{2,1,0:T(8,128)} %get-tuple-element.124.start_ref, f32[8,64,256]{2,1,0:T(8,128)} %get-tuple-element.125.slot_ref, f32[8,8,256]{2,1,0:T(8,128)} %get-tuple-element.126.other_ref, ...), custom_call_target="tpu_custom_call" | custom-call | flops 8000000000 | bytes 1048576 | tf_op jit(solution)/shard_map/pallas_call | solution.py:519
  477.5 12.7 %collective-permute-done.38.refs_7_ = bf16[2,2,224,512]{3,2,1,0:T(8,128)(2,1)} collective-permute-done((bf16[2,2,224,512]{3,2,1,0:T(8,128)(2,1)}, bf16[2,2,224,512]{3,2,1,0:T(8,128)(2,1)}, u32[]{:S(2)}, u32[]{:S(2)}) %collective-permute-start.38) | collective-permute-done | bytes 917536 | tf_op jit(solution)/shard_map/ppermute | solution.py:448
  491.1 19.7 %collective-permute-done.32.refs_2_ = bf16[2,2,224,512]{3,2,1,0:T(8,128)(2,1)} collective-permute-done((bf16[2,2,224,512]{3,2,1,0:T(8,128)(2,1)}, bf16[2,2,224,512]{3,2,1,0:T(8,128)(2,1)}, u32[]{:S(2)}, u32[]{:S(2)}) %collective-permute-start.32) | collective-permute-done | bytes 917536 | tf_op jit(solution)/shard_map/ppermute | solution.py:448
  511.3 18.2 %collective-permute-done.33.refs_3_ = bf16[2,2,224,512]{3,2,1,0:T(8,128)(2,1)} collective-permute-done((bf16[2,2,224,512]{3,2,1,0:T(8,128)(2,1)}, bf16[2,2,224,512]{3,2,1,0:T(8,128)(2,1)}, u32[]{:S(2)}, u32[]{:S(2)}) %collective-permute-start.33) | collective-permute-done | bytes 917536 | tf_op jit(solution)/shard_map/ppermute | solution.py:448
  530.4 13.9 %shard_map.136 = (bf16[2048,512]{1,0:T(8,128)(2,1)}, bf16[2048,512]{1,0:T(8,128)(2,1)}, f32[2048,512]{1,0:T(8,128)}) custom-call(s32[5]{0:T(128)} %copy-done.13, s32[8,128]{1,0:T(8,128)} %get-tuple-element.122.win_ref, f32[2048,128]{1,0:T(8,128)} %get-tuple-element.123.code_ref, bf16[2,2,224,512]{3,2,1,0:T(8,128)(2,1)} %get-tuple-element.144.refs_0_, ...), custom_call_target="tpu_custom_call" | custom-call | flops 8000000000 | bytes 1048576 | tf_op jit(solution)/shard_map/pallas_call | solution.py:570
  546.8 3.3 collective-permute-done.17.refs_2_
  550.6 8.3 %collective-permute-done.18.refs_3_ = bf16[1,2,224,512]{3,2,1,0:T(8,128)(2,1)} collective-permute-done((bf16[1,2,224,512]{3,2,1,0:T(8,128)(2,1)}, bf16[1,2,224,512]{3,2,1,0:T(8,128)(2,1)}, u32[]{:S(2)}, u32[]{:S(2)}) %collective-permute-start.18) | collective-permute-done | bytes 458784 | tf_op jit(solution)/shard_map/ppermute | solution.py:448
  559.9 15.0 %shard_map.137 = (bf16[2048,512]{1,0:T(8,128)(2,1)}, f32[2048,32]{1,0:T(8,128)}, f32[40,512]{1,0:T(8,128)}) custom-call(s32[5]{0:T(128)} %copy-done.13, s32[8,128]{1,0:T(8,128)} %get-tuple-element.122.win_ref, f32[2048,128]{1,0:T(8,128)} %get-tuple-element.123.code_ref, bf16[1,2,224,512]{3,2,1,0:T(8,128)(2,1)} %get-tuple-element.132.refs_0_, ...), custom_call_target="tpu_custom_call" | custom-call | flops 8000000000 | bytes 1048576 | tf_op jit(solution)/shard_map/pallas_call | solution.py:570
  576.1 2.5 collective-permute-done.46.refs_7_
  578.6 6.1 shard_map.138.refs_16_
  585.4 6.3 shard_map.139.refs_16_
  592.4 5.2 shard_map.140
  599.5 15.7 %shard_map.142 = (bf16[8,448,512]{2,1,0:T(8,128)(2,1)}, bf16[8,448,512]{2,1,0:T(8,128)(2,1)}) custom-call(s32[3]{0:T(128)} %add_add_fusion.3.info_ref, s32[8,8,128]{2,1,0:T(8,128)} %get-tuple-element.124.start_ref, f32[8,64,256]{2,1,0:T(8,128)} %get-tuple-element.125.slot_ref, f32[8,8,256]{2,1,0:T(8,128)} %get-tuple-element.126.other_ref, ...), custom_call_target="tpu_custom_call" | custom-call | flops 8000000000 | bytes 1048576 | tf_op jit(solution)/shard_map/pallas_call | solution.py:519
  615.2 15.6 %shard_map.144 = (f32[8,512,384]{2,1,0:T(8,128)}, f32[8,512,384]{2,1,0:T(8,128)}, f32[8,384,512]{2,1,0:T(8,128)}) custom-call(bf16[8,448,512]{2,1,0:T(8,128)(2,1)} %get-tuple-element.172.xa_ref, bf16[8,448,512]{2,1,0:T(8,128)(2,1)} %get-tuple-element.173.xb_ref, ...), custom_call_target="tpu_custom_call", output_to_operand_aliasing={{0}: (6, {}), {1}: (7, {}), {2}: (8, {})} | custom-call | flops 8000000000 | bytes 1048576 | tf_op jit(solution)/shard_map/pallas_call | solution.py:534
  630.8 15.6 %shard_map.145 = (f32[8,512,384]{2,1,0:T(8,128)}, f32[8,512,384]{2,1,0:T(8,128)}, f32[8,384,512]{2,1,0:T(8,128)}) custom-call(bf16[8,448,512]{2,1,0:T(8,128)(2,1)} %get-tuple-element.172.xa_ref, bf16[8,448,512]{2,1,0:T(8,128)(2,1)} %get-tuple-element.173.xb_ref, ...), custom_call_target="tpu_custom_call", output_to_operand_aliasing={{0}: (6, {}), {1}: (7, {}), {2}: (8, {})} | custom-call | flops 8000000000 | bytes 1048576 | tf_op jit(solution)/shard_map/pallas_call | solution.py:534
  (190 shorter events, 61.1 us)
Async XLA Ops:
  2.0 36.4 %collective-permute-start.6 = (s32[16,256]{1,0:T(8,128)}, s32[16,256]{1,0:T(8,128)}, u32[]{:S(2)}, u32[]{:S(2)}) collective-permute-start(s32[16,256]{1,0:T(8,128)} %reshape.109.refs_0_), channel_id=1, source_target_pairs={{0,7},{1,6},{2,5},{3,4},{4,3},{5,2},{6,1},{7,0}} | collective-permute-start | bytes 49160 | tf_op jit(solution)/shard_map/ppermute | solution.py:448
  5.7 33.3 %collective-permute-start.5 = (s32[16,256]{1,0:T(8,128)}, s32[16,256]{1,0:T(8,128)}, u32[]{:S(2)}, u32[]{:S(2)}) collective-permute-start(s32[16,256]{1,0:T(8,128)} %reshape.109.refs_0_), channel_id=1, source_target_pairs={{0,3},{1,2},{2,1},{3,0},{4,7},{5,6},{6,5},{7,4}} | collective-permute-start | bytes 49160 | tf_op jit(solution)/shard_map/ppermute | solution.py:448
  6.6 34.5 %collective-permute-start.4 = (s32[16,256]{1,0:T(8,128)}, s32[16,256]{1,0:T(8,128)}, u32[]{:S(2)}, u32[]{:S(2)}) collective-permute-start(s32[16,256]{1,0:T(8,128)} %reshape.109.refs_0_), channel_id=1, source_target_pairs={{0,6},{1,7},{2,4},{3,5},{4,2},{5,3},{6,0},{7,1}} | collective-permute-start | bytes 49160 | tf_op jit(solution)/shard_map/ppermute | solution.py:448
  10.4 79.8 %collective-permute-start.40 = (bf16[1,384,512]{2,1,0:T(8,128)(2,1)}, bf16[1,384,512]{2,1,0:T(8,128)(2,1)}, u32[]{:S(2)}, u32[]{:S(2)}) collective-permute-start(bf16[1,384,512]{2,1,0:T(8,128)(2,1)} %get-tuple-element.191), channel_id=1, source_target_pairs={{0,4},{1,5},{2,6},{3,7},{4,0},{5,1},{6,2},{7,3}} | collective-permute-start | bytes 1179656 | tf_op jit(solution)/shard_map/ppermute | solution.py:448
  11.9 80.3 %collective-permute-start.25 = (bf16[1,384,512]{2,1,0:T(8,128)(2,1)}, bf16[1,384,512]{2,1,0:T(8,128)(2,1)}, u32[]{:S(2)}, u32[]{:S(2)}) collective-permute-start(bf16[1,384,512]{2,1,0:T(8,128)(2,1)} %get-tuple-element.192), channel_id=1, source_target_pairs={{0,4},{1,5},{2,6},{3,7},{4,0},{5,1},{6,2},{7,3}} | collective-permute-start | bytes 1179656 | tf_op jit(solution)/shard_map/ppermute | solution.py:448
  38.4 127.0 %collective-permute-start.12 = (bf16[2048,512]{1,0:T(8,128)(2,1)}, bf16[2048,512]{1,0:T(8,128)(2,1)}, u32[]{:S(2)}, u32[]{:S(2)}) collective-permute-start(bf16[2048,512]{1,0:T(8,128)(2,1)} %refs_13_.5), channel_id=1, source_target_pairs={{0,2},{1,3},{2,0},{3,1},{4,6},{5,7},{6,4},{7,5}} | collective-permute-start | bytes 6291464 | tf_op jit(solution)/shard_map/ppermute | solution.py:448
  39.1 46.4 %collective-permute-start.3 = (s32[16,256]{1,0:T(8,128)}, s32[16,256]{1,0:T(8,128)S(1)}, u32[]{:S(2)}, u32[]{:S(2)}) collective-permute-start(s32[16,256]{1,0:T(8,128)} %reshape.109.refs_0_), channel_id=1, source_target_pairs={{0,2},{1,3},{2,0},{3,1},{4,6},{5,7},{6,4},{7,5}} | collective-permute-start | bytes 49160 | tf_op jit(solution)/shard_map/ppermute | solution.py:448
  41.1 44.5 %collective-permute-start.2 = (s32[16,256]{1,0:T(8,128)}, s32[16,256]{1,0:T(8,128)S(1)}, u32[]{:S(2)}, u32[]{:S(2)}) collective-permute-start(s32[16,256]{1,0:T(8,128)} %reshape.109.refs_0_), channel_id=1, source_target_pairs={{0,5},{1,4},{2,7},{3,6},{4,1},{5,0},{6,3},{7,2}} | collective-permute-start | bytes 49160 | tf_op jit(solution)/shard_map/ppermute | solution.py:448
  89.5 37.6 %collective-permute-start.10 = (bf16[1024,512]{1,0:T(8,128)(2,1)}, bf16[1024,512]{1,0:T(8,128)(2,1)S(1)}, u32[]{:S(2)}, u32[]{:S(2)}) collective-permute-start(bf16[1024,512]{1,0:T(8,128)(2,1)} %get-tuple-element.197), channel_id=1, source_target_pairs={{0,2},{1,3},{2,0},{3,1},{4,6},{5,7},{6,4},{7,5}} | collective-permute-start | bytes 3145736 | tf_op jit(solution)/shard_map/ppermute | solution.py:448
  90.1 46.5 %collective-permute-start.9 = (bf16[1024,512]{1,0:T(8,128)(2,1)}, bf16[1024,512]{1,0:T(8,128)(2,1)S(1)}, u32[]{:S(2)}, u32[]{:S(2)}) collective-permute-start(bf16[1024,512]{1,0:T(8,128)(2,1)} %get-tuple-element.198), channel_id=1, source_target_pairs={{0,2},{1,3},{2,0},{3,1},{4,6},{5,7},{6,4},{7,5}} | collective-permute-start | bytes 3145736 | tf_op jit(solution)/shard_map/ppermute | solution.py:448
  92.2 32.7 %collective-permute-start.35 = (bf16[2,384,512]{2,1,0:T(8,128)(2,1)}, bf16[2,384,512]{2,1,0:T(8,128)(2,1)S(1)}, u32[]{:S(2)}, u32[]{:S(2)}) collective-permute-start(bf16[2,384,512]{2,1,0:T(8,128)(2,1)} %get-tuple-element.195), channel_id=1, source_target_pairs={{0,4},{1,5},{2,6},{3,7},{4,0},{5,1},{6,2},{7,3}} | collective-permute-start | bytes 2359304 | tf_op jit(solution)/shard_map/ppermute | solution.py:448
  124.2 42.3 %collective-permute-start.53 = (bf16[1024,512]{1,0:T(8,128)(2,1)S(1)}, bf16[1024,512]{1,0:T(8,128)(2,1)}, u32[]{:S(2)}, u32[]{:S(2)}) collective-permute-start(bf16[1024,512]{1,0:T(8,128)(2,1)S(1)} %copy-done.3), channel_id=1, source_target_pairs={{0,4},{1,5},{2,6},{3,7},{4,0},{5,1},{6,2},{7,3}} | collective-permute-start | bytes 3145736 | tf_op jit(solution)/shard_map/ppermute | solution.py:448
  125.8 39.7 %collective-permute-start.30 = (bf16[2,384,512]{2,1,0:T(8,128)(2,1)S(1)}, bf16[2,384,512]{2,1,0:T(8,128)(2,1)S(1)}, u32[]{:S(2)}, u32[]{:S(2)}) collective-permute-start(bf16[2,384,512]{2,1,0:T(8,128)(2,1)S(1)} %copy-done.4), channel_id=1, source_target_pairs={{0,4},{1,5},{2,6},{3,7},{4,0},{5,1},{6,2},{7,3}} | collective-permute-start | bytes 2359304 | tf_op jit(solution)/shard_map/ppermute | solution.py:448
  127.1 67.8 %collective-permute-start.7 = (bf16[2048,512]{1,0:T(8,128)(2,1)}, bf16[2048,512]{1,0:T(8,128)(2,1)}, u32[]{:S(2)}, u32[]{:S(2)}) collective-permute-start(bf16[2048,512]{1,0:T(8,128)(2,1)} %refs_14_.1), channel_id=1, source_target_pairs={{0,1},{1,0},{2,3},{3,2},{4,5},{5,4},{6,7},{7,6}} | collective-permute-start | bytes 6291464 | tf_op jit(solution)/shard_map/ppermute | solution.py:448
  136.6 59.6 %collective-permute-start.8 = (bf16[2048,512]{1,0:T(8,128)(2,1)}, bf16[2048,512]{1,0:T(8,128)(2,1)}, u32[]{:S(2)}, u32[]{:S(2)}) collective-permute-start(bf16[2048,512]{1,0:T(8,128)(2,1)} %refs_13_.5), channel_id=1, source_target_pairs={{0,1},{1,0},{2,3},{3,2},{4,5},{5,4},{6,7},{7,6}} | collective-permute-start | bytes 6291464 | tf_op jit(solution)/shard_map/ppermute | solution.py:448
  165.5 48.4 %collective-permute-start.11 = (bf16[2048,512]{1,0:T(8,128)(2,1)}, bf16[2048,512]{1,0:T(8,128)(2,1)}, u32[]{:S(2)}, u32[]{:S(2)}) collective-permute-start(bf16[2048,512]{1,0:T(8,128)(2,1)} %constant_dynamic-update-slice_fusion.ha_ref), channel_id=1, source_target_pairs={{0,1},{1,0},{2,3},{3,2},{4,5},{5,4},{6,7},{7,6}} | collective-permute-start | bytes 6291464 | tf_op jit(solution)/shard_map/ppermute | solution.py:448
  165.5 49.2 %collective-permute-start.13 = (bf16[2048,512]{1,0:T(8,128)(2,1)}, bf16[2048,512]{1,0:T(8,128)(2,1)}, u32[]{:S(2)}, u32[]{:S(2)}) collective-permute-start(bf16[2048,512]{1,0:T(8,128)(2,1)} %collective-permute-done.12.da_ref), channel_id=1, source_target_pairs={{0,1},{1,0},{2,3},{3,2},{4,5},{5,4},{6,7},{7,6}} | collective-permute-start | bytes 6291464 | tf_op jit(solution)/shard_map/ppermute | solution.py:448
  166.5 25.4 %collective-permute-start.54 = (bf16[1024,512]{1,0:T(8,128)(2,1)}, bf16[1024,512]{1,0:T(8,128)(2,1)}, u32[]{:S(2)}, u32[]{:S(2)}) collective-permute-start(bf16[1024,512]{1,0:T(8,128)(2,1)} %get-tuple-element.197), channel_id=1, source_target_pairs={{0,4},{1,5},{2,6},{3,7},{4,0},{5,1},{6,2},{7,3}} | collective-permute-start | bytes 3145736 | tf_op jit(solution)/shard_map/ppermute | solution.py:448
  194.9 147.0 %collective-permute-start.56 = (bf16[2048,512]{1,0:T(8,128)(2,1)}, bf16[2048,512]{1,0:T(8,128)(2,1)}, u32[]{:S(2)}, u32[]{:S(2)}) collective-permute-start(bf16[2048,512]{1,0:T(8,128)(2,1)} %refs_13_.5), channel_id=1, source_target_pairs={{0,4},{1,5},{2,6},{3,7},{4,0},{5,1},{6,2},{7,3}} | collective-permute-start | bytes 6291464 | tf_op jit(solution)/shard_map/ppermute | solution.py:448
  196.2 146.2 %collective-permute-start.34 = (bf16[2,512,768]{2,1,0:T(8,128)(2,1)}, bf16[2,512,768]{2,1,0:T(8,128)(2,1)}, u32[]{:S(2)}, u32[]{:S(2)}) collective-permute-start(bf16[2,512,768]{2,1,0:T(8,128)(2,1)} %get-tuple-element.189), channel_id=1, source_target_pairs={{0,4},{1,5},{2,6},{3,7},{4,0},{5,1},{6,2},{7,3}} | collective-permute-start | bytes 4718600 | tf_op jit(solution)/shard_map/ppermute | solution.py:448
  212.7 95.5 %collective-permute-start.24 = (bf16[1,512,768]{2,1,0:T(8,128)(2,1)}, bf16[1,512,768]{2,1,0:T(8,128)(2,1)}, u32[]{:S(2)}, u32[]{:S(2)}) collective-permute-start(bf16[1,512,768]{2,1,0:T(8,128)(2,1)} %get-tuple-element.186), channel_id=1, source_target_pairs={{0,4},{1,5},{2,6},{3,7},{4,0},{5,1},{6,2},{7,3}} | collective-permute-start | bytes 2359304 | tf_op jit(solution)/shard_map/ppermute | solution.py:448
  213.9 111.1 %collective-permute-start.19 = (bf16[1,512,768]{2,1,0:T(8,128)(2,1)}, bf16[1,512,768]{2,1,0:T(8,128)(2,1)}, u32[]{:S(2)}, u32[]{:S(2)}) collective-permute-start(bf16[1,512,768]{2,1,0:T(8,128)(2,1)} %get-tuple-element.187), channel_id=1, source_target_pairs={{0,4},{1,5},{2,6},{3,7},{4,0},{5,1},{6,2},{7,3}} | collective-permute-start | bytes 2359304 | tf_op jit(solution)/shard_map/ppermute | solution.py:448
  214.7 127.2 %collective-permute-start.14 = (bf16[1,512,768]{2,1,0:T(8,128)(2,1)S(1)}, bf16[1,512,768]{2,1,0:T(8,128)(2,1)}, u32[]{:S(2)}, u32[]{:S(2)}) collective-permute-start(bf16[1,512,768]{2,1,0:T(8,128)(2,1)S(1)} %get-tuple-element.188), channel_id=1, source_target_pairs={{0,4},{1,5},{2,6},{3,7},{4,0},{5,1},{6,2},{7,3}} | collective-permute-start | bytes 2359304 | tf_op jit(solution)/shard_map/ppermute | solution.py:448
  308.2 65.6 %collective-permute-start.29 = (bf16[2,512,768]{2,1,0:T(8,128)(2,1)}, bf16[2,512,768]{2,1,0:T(8,128)(2,1)}, u32[]{:S(2)}, u32[]{:S(2)}) collective-permute-start(bf16[2,512,768]{2,1,0:T(8,128)(2,1)} %get-tuple-element.190), channel_id=1, source_target_pairs={{0,4},{1,5},{2,6},{3,7},{4,0},{5,1},{6,2},{7,3}} | collective-permute-start | bytes 4718600 | tf_op jit(solution)/shard_map/ppermute | solution.py:448
  325.0 48.8 %collective-permute-start.58 = (bf16[2048,512]{1,0:T(8,128)(2,1)}, bf16[2048,512]{1,0:T(8,128)(2,1)}, u32[]{:S(2)}, u32[]{:S(2)}) collective-permute-start(bf16[2048,512]{1,0:T(8,128)(2,1)} %constant_dynamic-update-slice_fusion.12.ha_ref), channel_id=1, source_target_pairs={{0,2},{1,3},{2,0},{3,1},{4,6},{5,7},{6,4},{7,5}} | collective-permute-start | bytes 6291464 | tf_op jit(solution)/shard_map/ppermute | solution.py:448
  341.9 33.4 %collective-permute-start.55 = (bf16[2048,512]{1,0:T(8,128)(2,1)}, bf16[2048,512]{1,0:T(8,128)(2,1)}, u32[]{:S(2)}, u32[]{:S(2)}) collective-permute-start(bf16[2048,512]{1,0:T(8,128)(2,1)} %constant_dynamic-update-slice_fusion.12.ha_ref), channel_id=1, source_target_pairs={{0,1},{1,0},{2,3},{3,2},{4,5},{5,4},{6,7},{7,6}} | collective-permute-start | bytes 6291464 | tf_op jit(solution)/shard_map/ppermute | solution.py:448
  341.9 76.9 %collective-permute-start.60 = (bf16[2048,512]{1,0:T(8,128)(2,1)}, bf16[2048,512]{1,0:T(8,128)(2,1)}, u32[]{:S(2)}, u32[]{:S(2)}) collective-permute-start(bf16[2048,512]{1,0:T(8,128)(2,1)} %collective-permute-done.56.da_ref), channel_id=1, source_target_pairs={{0,2},{1,3},{2,0},{3,1},{4,6},{5,7},{6,4},{7,5}} | collective-permute-start | bytes 6291464 | tf_op jit(solution)/shard_map/ppermute | solution.py:448
  342.4 76.3 %collective-permute-start.57 = (bf16[2048,512]{1,0:T(8,128)(2,1)}, bf16[2048,512]{1,0:T(8,128)(2,1)}, u32[]{:S(2)}, u32[]{:S(2)}) collective-permute-start(bf16[2048,512]{1,0:T(8,128)(2,1)} %collective-permute-done.56.da_ref), channel_id=1, source_target_pairs={{0,1},{1,0},{2,3},{3,2},{4,5},{5,4},{6,7},{7,6}} | collective-permute-start | bytes 6291464 | tf_op jit(solution)/shard_map/ppermute | solution.py:448
  373.8 53.7 %collective-permute-start.26 = (bf16[1,224,512]{2,1,0:T(8,128)(2,1)S(1)}, bf16[1,224,512]{2,1,0:T(8,128)(2,1)S(1)}, u32[]{:S(2)}, u32[]{:S(2)}) collective-permute-start(bf16[1,224,512]{2,1,0:T(8,128)(2,1)S(1)} %copy-done.23), channel_id=1, source_target_pairs={{0,1},{1,0},{2,3},{3,2},{4,5},{5,4},{6,7},{7,6}} | collective-permute-start | bytes 688136 | tf_op jit(solution)/shard_map/ppermute | solution.py:448
  373.8 54.4 %collective-permute-start.27 = (bf16[1,224,512]{2,1,0:T(8,128)(2,1)}, bf16[1,224,512]{2,1,0:T(8,128)(2,1)}, u32[]{:S(2)}, u32[]{:S(2)}) collective-permute-start(bf16[1,224,512]{2,1,0:T(8,128)(2,1)} %get-tuple-element.142), channel_id=1, source_target_pairs={{0,2},{1,3},{2,0},{3,1},{4,6},{5,7},{6,4},{7,5}} | collective-permute-start | bytes 688136 | tf_op jit(solution)/shard_map/ppermute | solution.py:448
  375.2 53.6 %collective-permute-start.28 = (bf16[1,224,512]{2,1,0:T(8,128)(2,1)}, bf16[1,224,512]{2,1,0:T(8,128)(2,1)}, u32[]{:S(2)}, u32[]{:S(2)}) collective-permute-start(bf16[1,224,512]{2,1,0:T(8,128)(2,1)} %get-tuple-element.143), channel_id=1, source_target_pairs={{0,3},{1,2},{2,1},{3,0},{4,7},{5,6},{6,5},{7,4}} | collective-permute-start | bytes 688136 | tf_op jit(solution)/shard_map/ppermute | solution.py:448
  418.8 32.6 %collective-permute-start.36 = (bf16[2,2,224,512]{3,2,1,0:T(8,128)(2,1)}, bf16[2,2,224,512]{3,2,1,0:T(8,128)(2,1)}, u32[]{:S(2)}, u32[]{:S(2)}) collective-permute-start(bf16[2,2,224,512]{3,2,1,0:T(8,128)(2,1)} %get-tuple-element.149), channel_id=1, source_target_pairs={{0,1},{1,0},{2,3},{3,2},{4,5},{5,4},{6,7},{7,6}} | collective-permute-start | bytes 2752520 | tf_op jit(solution)/shard_map/ppermute | solution.py:448
  444.6 32.3 %collective-permute-start.37 = (bf16[2,2,224,512]{3,2,1,0:T(8,128)(2,1)}, bf16[2,2,224,512]{3,2,1,0:T(8,128)(2,1)}, u32[]{:S(2)}, u32[]{:S(2)}) collective-permute-start(bf16[2,2,224,512]{3,2,1,0:T(8,128)(2,1)} %get-tuple-element.150), channel_id=1, source_target_pairs={{0,2},{1,3},{2,0},{3,1},{4,6},{5,7},{6,4},{7,5}} | collective-permute-start | bytes 2752520 | tf_op jit(solution)/shard_map/ppermute | solution.py:448
  445.2 45.0 %collective-permute-start.38 = (bf16[2,2,224,512]{3,2,1,0:T(8,128)(2,1)}, bf16[2,2,224,512]{3,2,1,0:T(8,128)(2,1)}, u32[]{:S(2)}, u32[]{:S(2)}) collective-permute-start(bf16[2,2,224,512]{3,2,1,0:T(8,128)(2,1)} %get-tuple-element.151), channel_id=1, source_target_pairs={{0,3},{1,2},{2,1},{3,0},{4,7},{5,6},{6,5},{7,4}} | collective-permute-start | bytes 2752520 | tf_op jit(solution)/shard_map/ppermute | solution.py:448
  446.2 44.9 %collective-permute-start.31 = (bf16[2,2,224,512]{3,2,1,0:T(8,128)(2,1)}, bf16[2,2,224,512]{3,2,1,0:T(8,128)(2,1)}, u32[]{:S(2)}, u32[]{:S(2)}) collective-permute-start(bf16[2,2,224,512]{3,2,1,0:T(8,128)(2,1)} %get-tuple-element.145), channel_id=1, source_target_pairs={{0,1},{1,0},{2,3},{3,2},{4,5},{5,4},{6,7},{7,6}} | collective-permute-start | bytes 2752520 | tf_op jit(solution)/shard_map/ppermute | solution.py:448
  450.8 59.9 %collective-permute-start.32 = (bf16[2,2,224,512]{3,2,1,0:T(8,128)(2,1)}, bf16[2,2,224,512]{3,2,1,0:T(8,128)(2,1)}, u32[]{:S(2)}, u32[]{:S(2)}) collective-permute-start(bf16[2,2,224,512]{3,2,1,0:T(8,128)(2,1)} %get-tuple-element.146), channel_id=1, source_target_pairs={{0,2},{1,3},{2,0},{3,1},{4,6},{5,7},{6,4},{7,5}} | collective-permute-start | bytes 2752520 | tf_op jit(solution)/shard_map/ppermute | solution.py:448
  451.4 78.1 %collective-permute-start.33 = (bf16[2,2,224,512]{3,2,1,0:T(8,128)(2,1)}, bf16[2,2,224,512]{3,2,1,0:T(8,128)(2,1)}, u32[]{:S(2)}, u32[]{:S(2)}) collective-permute-start(bf16[2,2,224,512]{3,2,1,0:T(8,128)(2,1)} %get-tuple-element.147), channel_id=1, source_target_pairs={{0,3},{1,2},{2,1},{3,0},{4,7},{5,6},{6,5},{7,4}} | collective-permute-start | bytes 2752520 | tf_op jit(solution)/shard_map/ppermute | solution.py:448
  476.9 67.4 %collective-permute-start.22 = (bf16[1,224,512]{2,1,0:T(8,128)(2,1)}, bf16[1,224,512]{2,1,0:T(8,128)(2,1)}, u32[]{:S(2)}, u32[]{:S(2)}) collective-permute-start(bf16[1,224,512]{2,1,0:T(8,128)(2,1)} %get-tuple-element.138), channel_id=1, source_target_pairs={{0,2},{1,3},{2,0},{3,1},{4,6},{5,7},{6,4},{7,5}} | collective-permute-start | bytes 688136 | tf_op jit(solution)/shard_map/ppermute | solution.py:448
  490.1 55.6 %collective-permute-start.23 = (bf16[1,224,512]{2,1,0:T(8,128)(2,1)}, bf16[1,224,512]{2,1,0:T(8,128)(2,1)}, u32[]{:S(2)}, u32[]{:S(2)}) collective-permute-start(bf16[1,224,512]{2,1,0:T(8,128)(2,1)} %get-tuple-element.139), channel_id=1, source_target_pairs={{0,3},{1,2},{2,1},{3,0},{4,7},{5,6},{6,5},{7,4}} | collective-permute-start | bytes 688136 | tf_op jit(solution)/shard_map/ppermute | solution.py:448
  491.1 55.7 %collective-permute-start.16 = (bf16[1,2,224,512]{3,2,1,0:T(8,128)(2,1)}, bf16[1,2,224,512]{3,2,1,0:T(8,128)(2,1)S(1)}, u32[]{:S(2)}, u32[]{:S(2)}) collective-permute-start(bf16[1,2,224,512]{3,2,1,0:T(8,128)(2,1)} %get-tuple-element.133), channel_id=1, source_target_pairs={{0,1},{1,0},{2,3},{3,2},{4,5},{5,4},{6,7},{7,6}} | collective-permute-start | bytes 1376264 | tf_op jit(solution)/shard_map/ppermute | solution.py:448
  510.7 39.3 %collective-permute-start.17 = (bf16[1,2,224,512]{3,2,1,0:T(8,128)(2,1)}, bf16[1,2,224,512]{3,2,1,0:T(8,128)(2,1)}, u32[]{:S(2)}, u32[]{:S(2)}) collective-permute-start(bf16[1,2,224,512]{3,2,1,0:T(8,128)(2,1)} %get-tuple-element.134), channel_id=1, source_target_pairs={{0,2},{1,3},{2,0},{3,1},{4,6},{5,7},{6,4},{7,5}} | collective-permute-start | bytes 1376264 | tf_op jit(solution)/shard_map/ppermute | solution.py:448
  529.5 29.5 %collective-permute-start.18 = (bf16[1,2,224,512]{3,2,1,0:T(8,128)(2,1)}, bf16[1,2,224,512]{3,2,1,0:T(8,128)(2,1)}, u32[]{:S(2)}, u32[]{:S(2)}) collective-permute-start(bf16[1,2,224,512]{3,2,1,0:T(8,128)(2,1)} %get-tuple-element.135), channel_id=1, source_target_pairs={{0,3},{1,2},{2,1},{3,0},{4,7},{5,6},{6,5},{7,4}} | collective-permute-start | bytes 1376264 | tf_op jit(solution)/shard_map/ppermute | solution.py:448
  544.3 30.6 %collective-permute-start.48 = (bf16[1,224,512]{2,1,0:T(8,128)(2,1)}, bf16[1,224,512]{2,1,0:T(8,128)(2,1)}, u32[]{:S(2)}, u32[]{:S(2)}) collective-permute-start(bf16[1,224,512]{2,1,0:T(8,128)(2,1)} %get-tuple-element.167), channel_id=1, source_target_pairs={{0,2},{1,3},{2,0},{3,1},{4,6},{5,7},{6,4},{7,5}} | collective-permute-start | bytes 688136 | tf_op jit(solution)/shard_map/ppermute | solution.py:448
  545.8 29.8 %collective-permute-start.49 = (bf16[1,224,512]{2,1,0:T(8,128)(2,1)S(1)}, bf16[1,224,512]{2,1,0:T(8,128)(2,1)}, u32[]{:S(2)}, u32[]{:S(2)}) collective-permute-start(bf16[1,224,512]{2,1,0:T(8,128)(2,1)S(1)} %copy-done.21), channel_id=1, source_target_pairs={{0,3},{1,2},{2,1},{3,0},{4,7},{5,6},{6,5},{7,4}} | collective-permute-start | bytes 688136 | tf_op jit(solution)/shard_map/ppermute | solution.py:448
  546.8 28.8 %collective-permute-start.44 = (bf16[1,224,512]{2,1,0:T(8,128)(2,1)}, bf16[1,224,512]{2,1,0:T(8,128)(2,1)}, u32[]{:S(2)}, u32[]{:S(2)}) collective-permute-start(bf16[1,224,512]{2,1,0:T(8,128)(2,1)} %get-tuple-element.162), channel_id=1, source_target_pairs={{0,1},{1,0},{2,3},{3,2},{4,5},{5,4},{6,7},{7,6}} | collective-permute-start | bytes 688136 | tf_op jit(solution)/shard_map/ppermute | solution.py:448
  550.1 26.0 %collective-permute-start.45 = (bf16[1,224,512]{2,1,0:T(8,128)(2,1)}, bf16[1,224,512]{2,1,0:T(8,128)(2,1)}, u32[]{:S(2)}, u32[]{:S(2)}) collective-permute-start(bf16[1,224,512]{2,1,0:T(8,128)(2,1)} %get-tuple-element.163), channel_id=1, source_target_pairs={{0,2},{1,3},{2,0},{3,1},{4,6},{5,7},{6,4},{7,5}} | collective-permute-start | bytes 688136 | tf_op jit(solution)/shard_map/ppermute | solution.py:448
  574.9 24.6 %collective-permute-start.59 = (bf16[2048,512]{1,0:T(8,128)(2,1)}, bf16[2048,512]{1,0:T(8,128)(2,1)}, u32[]{:S(2)}, u32[]{:S(2)}) collective-permute-start(bf16[2048,512]{1,0:T(8,128)(2,1)} %collective-permute-done.58.ha_ref), channel_id=1, source_target_pairs={{0,1},{1,0},{2,3},{3,2},{4,5},{5,4},{6,7},{7,6}} | collective-permute-start | bytes 6291464 | tf_op jit(solution)/shard_map/ppermute | solution.py:448
  575.6 23.9 %collective-permute-start.61 = (bf16[2048,512]{1,0:T(8,128)(2,1)}, bf16[2048,512]{1,0:T(8,128)(2,1)}, u32[]{:S(2)}, u32[]{:S(2)}) collective-permute-start(bf16[2048,512]{1,0:T(8,128)(2,1)} %collective-permute-done.60.da_ref), channel_id=1, source_target_pairs={{0,1},{1,0},{2,3},{3,2},{4,5},{5,4},{6,7},{7,6}} | collective-permute-start | bytes 6291464 | tf_op jit(solution)/shard_map/ppermute | solution.py:448
  (40 other events, 624.4 us)
